TPU v7x, 128 devices: a whole 4x4x4 slice. The times are simulated.
128 devices in a mesh: seq: 64 (over y, z, x), head: 2 (over core).
Axes of the slice: x: 4, y: 4, z: 4, core: 2. Of those that a mesh axis runs over, the one named last changes fastest.
Arguments:
- query: bfloat16 [8192, 8, 256], P('seq', 'head'), may hold values from -0.6 to 0.6
- key: bfloat16 [8192, 8, 256], P('seq', 'head'), may hold values from -0.59765625 to 0.59765625
- value: bfloat16 [8192, 8, 512], P('seq', 'head'), may hold values from -0.59765625 to 0.59765625
- out_grad: bfloat16 [8192, 8, 512], P(('seq', 'head')), may hold values from -0.6 to 0.6
- log_decay: bfloat16 [8192, 8, 256], P('seq', 'head'), may hold values from -0.1 to 0, as said below
- checkpoints: bfloat16 [64, 8, 256, 512], P('seq', 'head'), may hold values from -12 to 12
Outputs:
- grad_query: bfloat16 [8192, 8, 256], P('seq', 'head')
- grad_key: bfloat16 [8192, 8, 256], P('seq', 'head')
- grad_value: bfloat16 [8192, 8, 512], P('seq', 'head')
- grad_decay: bfloat16 [8192, 8, 256], P('seq', 'head')
Inputs may be any that keep to these rules, and one draw needn't show every extreme that they name: `log_decay`: every entry is negative.
All inputs are finite; a program needn't handle non-finite values.
Results may differ from a plain program's by a relative error of at most 0.001.
Values may be sent and summed in bfloat16 or wider, within the bound.
No kernel may reach another device: no remote copies, remote signals or barrier semaphores. Data moves between devices by JAX's collectives and lax.ppermute only.
A program may use at most 384 MiB of HBM per device.

v0:
```python
import jax
import jax.numpy as jnp
from jax import lax
from jax.experimental import pallas as pl
from jax.experimental.pallas import tpu as pltpu
from jax.sharding import Mesh
from jax.sharding import PartitionSpec as P


Y, Z, X, H = "seq_0", "seq_1", "seq_2", "head"
SEQ = (Y, Z, X)
F32 = jnp.float32
B16 = jnp.bfloat16
NN = ((1,), (0,))
NT = ((1,), (1,))
TN = ((0,), (0,))
TOK, NH, DK, DV = 128, 4, 256, 512
SCALE = DK ** (-0.5)


def split(x):
    high = x.astype(B16)
    return high, (x - high.astype(F32)).astype(B16)


def dot(a, b, dims):
    return lax.dot_general(a, b, (dims, ((), ())), preferred_element_type=F32)


def dot2(a, b, dims):
    high, low = split(a)
    return dot(high, b, dims) + dot(low, b, dims)


def dot3(a, b, dims):
    a_high, a_low = split(a)
    b_high, b_low = split(b)
    return dot(a_high, b_high, dims) + (dot(a_low, b_high, dims) + dot(a_high, b_low, dims))


def triangle(upper):
    row = lax.broadcasted_iota(jnp.int32, (TOK, TOK), 0)
    col = lax.broadcasted_iota(jnp.int32, (TOK, TOK), 1)
    return (col >= row) if upper else (col <= row)


def sds(shape, dtype=B16):
    return jax.ShapeDtypeStruct(shape, dtype)


def call(body, outs, n_in, scratch=(), after=()):
    specs = [pl.BlockSpec(memory_space=pltpu.SMEM)]
    specs += [pl.BlockSpec(memory_space=pltpu.VMEM)] * n_in
    specs += [pl.BlockSpec(memory_space=pl.ANY)] * len(after)

    def ordered(*refs):
        return body(*refs[: 1 + n_in], *refs[1 + n_in + len(after) :])

    run = pl.pallas_call(
        ordered,
        out_shape=outs,
        in_specs=specs,
        scratch_shapes=list(scratch),
        compiler_params=pltpu.CompilerParams(vmem_limit_bytes=16 * 1024 * 1024),
    )
    return lambda *operands: run(*operands, *after)


def pack_grad(idx, g, send, keep, scr):
    for h in range(2 * NH):
        scr[h] = g[:, h, :]
    c = idx[3]
    for i in range(NH):
        send[i] = scr[NH * (1 - c) + i]
        keep[i] = scr[NH * c + i]


def pack_rows(idx, a, b, out):
    width = a.shape[-1]
    for h in range(NH):
        out[h, :, :width] = a[:, h, :]
        out[h, :, width:] = b[:, h, :]


def pack_pair(idx, a, b, *rest):
    outs, scr = rest[:4], rest[4]
    pack_rows(idx, a, b, scr)
    for s in range(4):
        outs[s][...] = scr[(idx[0] + s) % 4]


def join_all(idx, qa, keep, recv, *outs):
    c = idx[3]
    half = TOK // 2
    mine = pl.ds(pl.multiple_of(half * c, half), half)
    theirs = pl.ds(pl.multiple_of(half * (1 - c), half), half)
    for s in range(4):
        h = (idx[0] + s) % 4
        outs[s][:, : 2 * DK] = qa[h]
        outs[s][mine, 2 * DK :] = keep[h]
        outs[s][theirs, 2 * DK :] = recv[h]


def query_part(idx, *refs):
    qag, kv = refs[0:4], refs[4:8]
    check = refs[8]
    dq_out, qdq_out = refs[9:11]
    kv_out = refs[11:15]
    scr = refs[15]
    low = triangle(False)
    tri = low.astype(B16)
    for s in range(4):
        h = (idx[0] + s) % 4
        q = qag[s][:, :DK].astype(F32)
        cum = dot(tri, qag[s][:, DK : 2 * DK], NN)
        k = kv[s][:, :DK].astype(F32)
        g = qag[s][:, 2 * DK :]
        scores = jnp.where(low, dot(g, kv[s][:, DK:], NT), 0.0)
        reached = dot(g, check[0, h], NT) + dot3(scores, k * jnp.exp(-cum), NN)
        dq = SCALE * jnp.exp(cum) * reached
        scr[h] = dq
        qdq = q * dq
        qdq_out[h] = qdq
        total = jnp.sum(qdq, axis=0, keepdims=True)
        t0 = total.astype(B16)
        rest = total - t0.astype(F32)
        t1 = rest.astype(B16)
        t2 = (rest - t1.astype(F32)).astype(B16)
        kv_out[s][:TOK, :] = kv[s][...]
        kv_out[s][TOK:, :DK] = jnp.broadcast_to(t0, (16, DK))
        kv_out[s][TOK:, DK : 2 * DK] = jnp.broadcast_to(t1, (16, DK))
        kv_out[s][TOK:, 2 * DK :] = jnp.broadcast_to(t2, (16, DK))
    for h in range(NH):
        dq_out[:, h, :] = scr[h].astype(B16)


def line_cum(qa, cum_scr):
    tri = triangle(False).astype(B16)
    base = jnp.zeros((1, DK), F32)
    for j in range(4):
        rows = slice(TOK * j, TOK * (j + 1))
        cum = dot(tri, qa[rows, DK:], NN) + base
        base = cum[TOK - 1 :, :]
        cum_scr[rows, :] = cum
    return base


def line_state(idx, *refs):
    qag = refs[0:4]
    chunks = refs[4:8]
    qa_out, g_out = refs[8:10]
    acc, cum_scr = refs[10:12]
    x, z = idx[0], idx[1]
    for s in range(4):
        j = (x - s + 4) % 4
        rows = pl.ds(pl.multiple_of(TOK * j, TOK), TOK)
        qa_out[rows, :] = qag[s][:, : 2 * DK]
        g_out[rows, :] = qag[s][:, 2 * DK :]
    base = line_cum(qa_out, cum_scr)
    rise = qa_out[:, :DK].astype(F32) * jnp.exp(cum_scr[...])
    high, lo = split(SCALE * rise)
    g = g_out[...]
    acc[...] = dot(g, high, TN) + dot(g, lo, TN)
    for s in range(4):
        at = pl.multiple_of(TOK * ((z + s) % 4), TOK)
        chunks[s][:TOK, :] = acc[pl.ds(at, TOK), :]
        chunks[s][TOK:, :] = jnp.broadcast_to(base, (8, DK))


def scan_z(idx, *refs):
    parts = refs[0:4]
    total, suffix = refs[4:6]
    scr = refs[6]
    z = idx[1]
    for s in range(4):
        scr[(z - s + 4) % 4] = parts[s][...]
    state = jnp.zeros((TOK, DK), F32)
    logs = jnp.zeros((1, DK), F32)
    for j in reversed(range(4)):
        suffix[j, :TOK, :] = state
        suffix[j, TOK:, :] = jnp.broadcast_to(logs, (8, DK))
        own = scr[j, TOK : TOK + 1, :]
        state = jnp.exp(own) * state + scr[j, :TOK, :]
        logs = logs + own
    total[:TOK, :] = state
    total[TOK:, :] = jnp.broadcast_to(logs, (8, DK))


def scan_y(idx, *refs):
    parts, suffix = refs[0:4], refs[4]
    outs, token = refs[5:9], refs[9]
    scr = refs[10]
    y, z = idx[2], idx[1]
    token[...] = jnp.zeros((8, 128), F32)
    for s in range(4):
        scr[(y - s + 4) % 4] = parts[s][...]
    state = jnp.zeros((TOK, DK), F32)
    for j in (3, 2, 1):
        joined = jnp.exp(scr[j, TOK : TOK + 1, :]) * state + scr[j, :TOK, :]
        state = jnp.where(j > y, joined, state)
    for s in range(4):
        j = (z + s) % 4
        outs[s][...] = suffix[j, :TOK, :] + jnp.exp(suffix[j, TOK : TOK + 1, :]) * state


def near_part(idx, *refs):
    qa, g = refs[0:2]
    kv = refs[2:6]
    dk_near, dv_near, k_end, ends, v_out, k_out = refs[6:12]
    rise, cum = refs[12:14]
    last = line_cum(qa, cum)
    x = idx[0]
    for s in range(4):
        j = (x - s + 4) % 4
        rows = pl.ds(pl.multiple_of(TOK * j, TOK), TOK)
        k_out[rows, :] = kv[s][:TOK, :DK]
        v_out[rows, :] = kv[s][:TOK, DK:]
    rise[...] = SCALE * qa[:, :DK].astype(F32) * jnp.exp(cum[...])
    end = jnp.exp(last - cum[...])
    ends[...] = end
    k_end[...] = k_out[...].astype(F32) * end
    upper = triangle(True)
    for j in range(4):
        rows = slice(TOK * j, TOK * (j + 1))
        width = 4 * TOK - TOK * j
        later = slice(TOK * j, 4 * TOK)
        fall = jnp.exp(-cum[rows, :])
        keep = lax.broadcasted_iota(jnp.int32, (TOK, width), 1) >= lax.broadcasted_iota(
            jnp.int32, (TOK, width), 0
        )
        scores = jnp.where(keep, dot(v_out[rows, :], g[later, :], NT), 0.0)
        dk_near[rows, :] = fall * dot3(scores, rise[later, :], NN)
        k_fall = k_out[rows, :].astype(F32) * fall
        affinity = jnp.where(keep, dot3(k_fall, rise[later, :], NT), 0.0)
        dv_near[rows, :] = dot2(affinity, g[later, :], NN)


def far_part(idx, *refs):
    parts = refs[0:4]
    kv = refs[4:8]
    dk_near, dv_near, k_end, ends, v, k = refs[8:14]
    outs = refs[14:18]
    sums = refs[18]
    state, scr = refs[19:21]
    x, z = idx[0], idx[1]
    for s in range(4):
        j = (z - s + 4) % 4
        state[pl.ds(pl.multiple_of(TOK * j, TOK), TOK), :] = parts[s][...]
    high, lo = split(state[...])
    reached = dot(v[...], high, NN) + dot(v[...], lo, NN)
    dk = dk_near[...] + ends[...] * reached
    dk_high, dk_low = split(dk)
    e_high, e_low = split(k_end[...])
    dv = dv_near[...] + (
        dot(e_high, high, NT) + (dot(e_low, high, NT) + dot(e_high, lo, NT))
    )
    kdk = k[...].astype(F32) * dk
    for j in range(4):
        rows = slice(TOK * j, TOK * (j + 1))
        scr[j, :, :DK] = dk_high[rows, :]
        scr[j, :, DK : 2 * DK] = dk_low[rows, :]
        scr[j, :, 2 * DK :] = dv[rows, :].astype(B16)
        sums[j : j + 1, :] = -jnp.sum(kdk[rows, :], axis=0, keepdims=True)
    for s in range(4):
        j = (x - s + 4) % 4
        tot = (
            kv[s][TOK : TOK + 1, :DK].astype(F32)
            + kv[s][TOK : TOK + 1, DK : 2 * DK].astype(F32)
            + kv[s][TOK : TOK + 1, 2 * DK :].astype(F32)
        )
        sums[pl.ds(j, 1), :] = sums[pl.ds(j, 1), :] + tot
    sums[4:5, :] = jnp.sum(sums[0:4, :], axis=0, keepdims=True)
    sums[5:8, :] = jnp.zeros((3, DK), F32)
    for s in range(4):
        outs[s][...] = scr[(x + s) % 4]


def final_part(idx, *refs):
    parts, later = refs[0:4], refs[4:8]
    qdq = refs[8]
    key = refs[9]
    dk_out, dv_out, da_out = refs[10:13]
    s_dk, s_dv, s_da, s_k = refs[13:17]
    x = idx[0]
    for h in range(NH):
        s_k[h] = key[:, h, :]
    upper = triangle(True).astype(B16)
    for s in range(4):
        h = (x - s + 4) % 4
        dk_high = parts[s][:, :DK]
        dk = dk_high.astype(F32) + parts[s][:, DK : 2 * DK].astype(F32)
        s_dk[h] = dk_high
        s_dv[h] = parts[s][:, 2 * DK :]
        weight = qdq[h] - s_k[h].astype(F32) * dk
        w_high, w_low = split(weight)
        da = dot(upper, w_high, NN) + dot(upper, w_low, NN) + later[s][pl.ds(x, 1), :]
        s_da[h] = da.astype(B16)
    for h in range(NH):
        dk_out[:, h, :] = s_dk[h]
        dv_out[:, h, :] = s_dv[h]
        da_out[:, h, :] = s_da[h]


def shifted(value, axis, s):
    return lax.ppermute(value, axis, [(i, (i + s) % 4) for i in range(4)])


def spread(parts, axis):
    moved = [parts[0]]
    for s in (1, 2, 3):
        moved.append(shifted(parts[s], axis, s))
    return moved


def whole(query, key, value, out_grad, log_decay, checkpoints):
    x, z, y, c = (lax.axis_index(axis) for axis in (X, Z, Y, H))
    idx = jnp.stack([x, z, y, c]).astype(jnp.int32)
    vm = pltpu.VMEM

    half = TOK // 2
    send, keep = call(
        pack_grad, [sds((NH, half, DV))] * 2, 1, [vm((2 * NH, half, DV), B16)]
    )(idx, out_grad)
    recv = lax.ppermute(send, H, [(0, 1), (1, 0)])
    qa = call(pack_rows, sds((NH, TOK, 2 * DK)), 2, ())(idx, query, log_decay)
    qag = call(join_all, [sds((TOK, 2 * DK + DV))] * 4, 3, ())(idx, qa, keep, recv)
    qag_line = spread(qag, X)
    kv = call(
        pack_pair, [sds((TOK, DK + DV))] * 4, 2, [vm((NH, TOK, DK + DV), B16)]
    )(idx, key, value)
    res = call(
        query_part,
        [sds((TOK, NH, DK)), sds((NH, TOK, DK), F32)] + [sds((TOK + 16, DK + DV))] * 4,
        9,
        [vm((NH, TOK, DK), F32)],
    )(idx, *qag, *kv, checkpoints)
    dq, qdq, kv = res[0], res[1], res[2:]
    res = call(
        line_state,
        [sds((TOK + 8, DK), F32)] * 4
        + [sds((4 * TOK, 2 * DK)), sds((4 * TOK, DV))],
        4,
        [vm((DV, DK), F32), vm((4 * TOK, DK), F32)],
        (qdq,),
    )(idx, *qag_line)
    chunks, qa_rows, g_rows = res[:4], res[4], res[5]
    z_in = spread(chunks, Z)
    kv_line = spread(kv, X)
    total, suffix = call(
        scan_z,
        [sds((TOK + 8, DK), F32), sds((4, TOK + 8, DK), F32)],
        4,
        [vm((4, TOK + 8, DK), F32)],
    )(idx, *z_in)
    y_in = spread([total] * 4, Y)
    *carry, token = call(
        scan_y, [sds((TOK, DK), F32)] * 4 + [sds((8, 128), F32)], 5, [vm((4, TOK + 8, DK), F32)]
    )(idx, *y_in, suffix)
    carry_in = spread(carry, Z)
    near = call(
        near_part,
        [
            sds((4 * TOK, DK), F32),
            sds((4 * TOK, DV), F32),
            sds((4 * TOK, DK), F32),
            sds((4 * TOK, DK), F32),
            sds((4 * TOK, DV)),
            sds((4 * TOK, DK)),
        ],
        6,
        [vm((4 * TOK, DK), F32)] * 2,
        (token,),
    )(idx, qa_rows, g_rows, *kv_line)
    res = call(
        far_part,
        [sds((TOK, 2 * DK + DV))] * 4 + [sds((8, DK), F32)],
        14,
        [vm((DV, DK), F32), vm((4, TOK, 2 * DK + DV), B16)],
    )(idx, *carry_in, *kv_line, *near)
    back, sums = res[:4], res[4]
    back_in = spread(back, X)

    def beyond(total, axis, index):
        parts = spread([total] * 4, axis)
        later = jnp.zeros_like(total)
        everything = total
        for s in (1, 2, 3):
            later = later + jnp.where((index - s) % 4 > index, parts[s], 0.0)
            everything = everything + parts[s]
        return later, everything

    line_total = sums[4:5]
    z_later, z_all = beyond(jnp.broadcast_to(line_total, (8, DK)), Z, z)
    y_later, _ = beyond(z_all, Y, y)
    outside = z_later + y_later
    inside = jnp.stack([jnp.sum(sums[j + 1 : 4], axis=0) for j in range(4)])
    later = outside + jnp.concatenate([inside, jnp.zeros((4, DK), F32)])
    later_in = spread([later] * 4, X)
    dk, dv, da = call(
        final_part,
        [sds((TOK, NH, DK)), sds((TOK, NH, DV)), sds((TOK, NH, DK))],
        10,
        [
            vm((NH, TOK, DK), B16),
            vm((NH, TOK, DV), B16),
            vm((NH, TOK, DK), B16),
            vm((NH, TOK, DK), B16),
        ],
    )(idx, *back_in, *later_in, qdq, key)
    return dq, dk, dv, da


def solution(mesh):
    torus = Mesh(mesh.devices.reshape(4, 4, 4, 2), (Y, Z, X, H))
    by_token = P(SEQ, H, None)
    placed = (
        by_token,
        by_token,
        by_token,
        P(SEQ + (H,), None, None),
        by_token,
        P(SEQ, H, None, None),
    )
    return jax.shard_map(
        whole, mesh=torus, in_specs=placed, out_specs=(by_token,) * 4, check_vma=False
    )
```

profile of v0, /device:TPU:0, one launch (start us, length us, event | category | flops | bytes accessed | tf_op | source)
XLA Modules:
  0.0 92.9 jit_solution(9191753273241127815)
XLA Ops:
  1.8 1.5 %shard_map.94 = (bf16[4,64,512]{2,1,0:T(8,128)(2,1)S(1)}, bf16[4,64,512]{2,1,0:T(8,128)(2,1)S(1)}) custom-call(s32[4]{0:T(128)S(1)} %pad_add_fusion.refs_0_, bf16[64,8,512]{2,1,0:T(8,128)(2,1)S(1)} %copy-done.2), custom_call_target="tpu_custom_call" | custom-call | tf_op jit(solution)/shard_map/pallas_call | solution.py:66
  5.6 1.7 %collective-permute-start.1 = (bf16[128,1024]{1,0:T(8,128)(2,1)S(1)}, bf16[128,1024]{1,0:T(8,128)(2,1)S(1)}, u32[]{:S(2)}, u32[]{:S(2)}) collective-permute-start(bf16[128,1024]{1,0:T(8,128)(2,1)S(1)} %get-tuple-element.50.refs_2_), channel_id=1, source_target_pairs={{0,2},{2,4},{4,6},{6,0},{1,3},{3,5},{5,7},{7,1},{8,10},{10,12},{12... | collective-permute-start | bytes 786440 | tf_op jit(solution)/shard_map/ppermute | solution.py:305
  7.2 2.7 %collective-permute-start.2 = (bf16[128,1024]{1,0:T(8,128)(2,1)S(1)}, bf16[128,1024]{1,0:T(8,128)(2,1)S(1)}, u32[]{:S(2)}, u32[]{:S(2)}) collective-permute-start(bf16[128,1024]{1,0:T(8,128)(2,1)S(1)} %get-tuple-element.51.refs_3_), channel_id=1, source_target_pairs={{0,4},{2,6},{4,0},{6,2},{1,5},{3,7},{5,1},{7,3},{8,12},{10,14},{12... | collective-permute-start | bytes 786440 | tf_op jit(solution)/shard_map/ppermute | solution.py:305
  11.4 2.3 %shard_map.96 = (bf16[128,768]{1,0:T(8,128)(2,1)S(1)}, bf16[128,768]{1,0:T(8,128)(2,1)S(1)}, bf16[128,768]{1,0:T(8,128)(2,1)S(1)}, bf16[128,768]{1,0:T(8,128)(2,1)S(1)}) custom-call(s32[4]{0:T(128)S(1)} %pad_add_fusion.refs_0_, bf16[128,4,256]{2,1,0:T(4,128)(2,1)S(1)} %copy-done.1, bf16[128,4,512]{2,1,0:T(4,128)(2,1)S(1)} %copy-done.3), custom_call_target="tpu_custom_call" | custom-call | tf_op jit(solution)/shard_map/pallas_call | solution.py:66
  13.7 3.2 %shard_map.97 = (bf16[128,4,256]{2,1,0:T(4,128)(2,1)}, f32[4,128,256]{2,1,0:T(8,128)S(1)}, bf16[144,768]{1,0:T(8,128)(2,1)S(1)}, bf16[144,768]{1,0:T(8,128)(2,1)...) custom-call(s32[4]{0:T(128)S(1)} %pad_add_fusion.refs_0_, ...), custom_call_target="tpu_custom_call" | custom-call | tf_op jit(solution)/shard_map/pallas_call | solution.py:66
  16.9 5.3 %collective-permute-done.2.refs_3_ = bf16[128,1024]{1,0:T(8,128)(2,1)S(1)} collective-permute-done((bf16[128,1024]{1,0:T(8,128)(2,1)S(1)}, bf16[128,1024]{1,0:T(8,128)(2,1)S(1)}, u32[]{:S(2)}, u32[]{:S(2)}) %collective-permute-start.2) | collective-permute-done | bytes 262176 | tf_op jit(solution)/shard_map/ppermute | solution.py:305
  23.4 2.0 %collective-permute-start.4 = (f32[136,256]{1,0:T(8,128)S(1)}, f32[136,256]{1,0:T(8,128)S(1)}, u32[]{:S(2)}, u32[]{:S(2)}) collective-permute-start(f32[136,256]{1,0:T(8,128)S(1)} %get-tuple-element.60), channel_id=1, source_target_pairs={{0,8},{8,16},{16,24},{24,0},{1,9},{9,17},{17,25},{25,1},{2,10},{10... | collective-permute-start | bytes 417800 | tf_op jit(solution)/shard_map/ppermute | solution.py:305
  25.4 3.6 %collective-permute-start.5 = (f32[136,256]{1,0:T(8,128)S(1)}, f32[136,256]{1,0:T(8,128)S(1)}, u32[]{:S(2)}, u32[]{:S(2)}) collective-permute-start(f32[136,256]{1,0:T(8,128)S(1)} %get-tuple-element.61), channel_id=1, source_target_pairs={{0,16},{8,24},{16,0},{24,8},{1,17},{9,25},{17,1},{25,9},{2,18},{10... | collective-permute-start | bytes 417800 | tf_op jit(solution)/shard_map/ppermute | solution.py:305
  31.2 3.9 %collective-permute-done.5.refs_3_ = f32[136,256]{1,0:T(8,128)S(1)} collective-permute-done((f32[136,256]{1,0:T(8,128)S(1)}, f32[136,256]{1,0:T(8,128)S(1)}, u32[]{:S(2)}, u32[]{:S(2)}) %collective-permute-start.5) | collective-permute-done | bytes 139296 | tf_op jit(solution)/shard_map/ppermute | solution.py:305
  35.7 1.6 %collective-permute-start.7 = (f32[136,256]{1,0:T(8,128)S(1)}, f32[136,256]{1,0:T(8,128)S(1)}, u32[]{:S(2)}, u32[]{:S(2)}) collective-permute-start(f32[136,256]{1,0:T(8,128)S(1)} %get-tuple-element.63.refs_1_), channel_id=1, source_target_pairs={{0,32},{32,64},{64,96},{96,0},{1,33},{33,65},{65,97},{97,1},{2,34}... | collective-permute-start | bytes 417800 | tf_op jit(solution)/shard_map/ppermute | solution.py:305
  38.5 2.9 %collective-permute-start.8 = (f32[136,256]{1,0:T(8,128)S(1)}, f32[136,256]{1,0:T(8,128)S(1)}, u32[]{:S(2)}, u32[]{:S(2)}) collective-permute-start(f32[136,256]{1,0:T(8,128)S(1)} %get-tuple-element.63.refs_1_), channel_id=1, source_target_pairs={{0,64},{32,96},{64,0},{96,32},{1,65},{33,97},{65,1},{97,33},{2,66}... | collective-permute-start | bytes 417800 | tf_op jit(solution)/shard_map/ppermute | solution.py:305
  42.8 3.1 %collective-permute-start.14 = (bf16[144,768]{1,0:T(8,128)(2,1)S(1)}, bf16[144,768]{1,0:T(8,128)(2,1)S(1)}, u32[]{:S(2)}, u32[]{:S(2)}) collective-permute-start(bf16[144,768]{1,0:T(8,128)(2,1)S(1)} %get-tuple-element.71), channel_id=1, source_target_pairs={{0,4},{2,6},{4,0},{6,2},{1,5},{3,7},{5,1},{7,3},{8,12},{10,14},{12... | collective-permute-start | bytes 663560 | tf_op jit(solution)/shard_map/ppermute | solution.py:305
  47.4 1.7 %collective-permute-start.10 = (f32[128,256]{1,0:T(8,128)S(1)}, f32[128,256]{1,0:T(8,128)S(1)}, u32[]{:S(2)}, u32[]{:S(2)}) collective-permute-start(f32[128,256]{1,0:T(8,128)S(1)} %get-tuple-element.66), channel_id=1, source_target_pairs={{0,8},{8,16},{16,24},{24,0},{1,9},{9,17},{17,25},{25,1},{2,10},{10... | collective-permute-start | bytes 393224 | tf_op jit(solution)/shard_map/ppermute | solution.py:305
  49.1 2.2 %collective-permute-start.11 = (f32[128,256]{1,0:T(8,128)S(1)}, f32[128,256]{1,0:T(8,128)S(1)}, u32[]{:S(2)}, u32[]{:S(2)}) collective-permute-start(f32[128,256]{1,0:T(8,128)S(1)} %get-tuple-element.67), channel_id=1, source_target_pairs={{0,16},{8,24},{16,0},{24,8},{1,17},{9,25},{17,1},{25,9},{2,18},{10... | collective-permute-start | bytes 393224 | tf_op jit(solution)/shard_map/ppermute | solution.py:305
  53.6 3.1 %shard_map.101 = (f32[512,256]{1,0:T(8,128)S(1)}, f32[512,512]{1,0:T(8,128)S(1)}, f32[512,256]{1,0:T(8,128)S(1)}, f32[512,256]{1,0:T(8,128)S(1)}, bf16[512,512]{...) custom-call(s32[4]{0:T(128)S(1)} %pad_add_fusion.refs_0_, bf16[512,512]{1,0:T(8,128)(2,1)S(1)} %get-tuple-element.73.refs_1_, ...), custom_call_target="tpu_custom_call" | custom-call | tf_op jit(solution)/shard_map/pallas_call | solution.py:66
  56.8 1.6 %shard_map.102 = (bf16[128,1024]{1,0:T(8,128)(2,1)S(1)}, bf16[128,1024]{1,0:T(8,128)(2,1)S(1)}, bf16[128,1024]{1,0:T(8,128)(2,1)S(1)}, bf16[128,1024]{1,0:T(8,128)(2,1)S(1)}, f32[8,256]{1,0:T(8,128)S(1)}) custom-call(s32[4]{0:T(128)S(1)} %pad_add_fusion.refs_0_, f32[128,256]{1,0:T(8,128)S(1)} %get-tuple-element.65.refs_1_, ...), custom_call_target="tpu_custom_call" | custom-call | tf_op jit(solution)/shard_map/pallas_call | solution.py:66
  58.4 2.7 %collective-permute-start.21 = (f32[8,256]{1,0:T(8,128)S(1)}, f32[8,256]{1,0:T(8,128)S(1)}, u32[]{:S(2)}, u32[]{:S(2)}) collective-permute-start(f32[8,256]{1,0:T(8,128)S(1)} %broadcast_in_dim.20), channel_id=1, source_target_pairs={{0,24},{8,0},{16,8},{24,16},{1,25},{9,1},{17,9},{25,17},{2,26},{10... | collective-permute-start | bytes 24584 | tf_op jit(solution)/shard_map/ppermute | solution.py:305
  62.5 3.8 %collective-permute-done.20 = f32[8,256]{1,0:T(8,128)S(1)} collective-permute-done((f32[8,256]{1,0:T(8,128)S(1)}, f32[8,256]{1,0:T(8,128)S(1)}, u32[]{:S(2)}, u32[]{:S(2)}) %collective-permute-start.20) | collective-permute-done | bytes 8224 | tf_op jit(solution)/shard_map/ppermute | solution.py:305
  70.1 2.5 %collective-permute-start.17 = (bf16[128,1024]{1,0:T(8,128)(2,1)S(1)}, bf16[128,1024]{1,0:T(8,128)(2,1)S(1)}, u32[]{:S(2)}, u32[]{:S(2)}) collective-permute-start(bf16[128,1024]{1,0:T(8,128)(2,1)S(1)} %get-tuple-element.84), channel_id=1, source_target_pairs={{0,4},{2,6},{4,0},{6,2},{1,5},{3,7},{5,1},{7,3},{8,12},{10,14},{12... | collective-permute-start | bytes 786440 | tf_op jit(solution)/shard_map/ppermute | solution.py:305
  72.5 2.5 %collective-permute-start.18 = (bf16[128,1024]{1,0:T(8,128)(2,1)S(1)}, bf16[128,1024]{1,0:T(8,128)(2,1)S(1)}, u32[]{:S(2)}, u32[]{:S(2)}) collective-permute-start(bf16[128,1024]{1,0:T(8,128)(2,1)S(1)} %get-tuple-element.85), channel_id=1, source_target_pairs={{0,6},{2,0},{4,2},{6,4},{1,7},{3,1},{5,3},{7,5},{8,14},{10,8},{12,... | collective-permute-start | bytes 786440 | tf_op jit(solution)/shard_map/ppermute | solution.py:305
  75.9 4.2 %collective-permute-done.23 = f32[8,256]{1,0:T(8,128)S(1)} collective-permute-done((f32[8,256]{1,0:T(8,128)S(1)}, f32[8,256]{1,0:T(8,128)S(1)}, u32[]{:S(2)}, u32[]{:S(2)}) %collective-permute-start.23) | collective-permute-done | bytes 8224 | tf_op jit(solution)/shard_map/ppermute | solution.py:305
  82.4 3.1 %collective-permute-done.25.refs_6_ = f32[8,256]{1,0:T(8,128)S(1)} collective-permute-done((f32[8,256]{1,0:T(8,128)S(1)}, f32[8,256]{1,0:T(8,128)S(1)}, u32[]{:S(2)}, u32[]{:S(2)}) %collective-permute-start.25) | collective-permute-done | bytes 8224 | tf_op jit(solution)/shard_map/ppermute | solution.py:305
  86.4 2.7 %collective-permute-done.27.refs_8_ = f32[8,256]{1,0:T(8,128)S(1)} collective-permute-done((f32[8,256]{1,0:T(8,128)S(1)}, f32[8,256]{1,0:T(8,128)S(1)}, u32[]{:S(2)}, u32[]{:S(2)}) %collective-permute-start.27) | collective-permute-done | bytes 8224 | tf_op jit(solution)/shard_map/ppermute | solution.py:305
  89.1 3.8 %shard_map.103 = (bf16[128,4,256]{2,1,0:T(4,128)(2,1)}, bf16[128,4,512]{2,1,0:T(4,128)(2,1)}, bf16[128,4,256]{2,1,0:T(4,128)(2,1)}) custom-call(s32[4]{0:T(128)S(1)} %pad_add_fusion.refs_0_, bf16[128,1024]{1,0:T(8,128)(2,1)S(1)} %get-tuple-element.82.refs_1_, bf16[128,1024]{1,0:T(8,128)(2,1)S(1)} %collective-permute-done.16.refs_2_, ...), custom_call_target="tpu_custom_call" | custom-call | tf_op jit(solution)/shard_map/pallas_call | solution.py:66
  (65 shorter events, 24.6 us)
Async XLA Ops:
  5.6 11.3 %collective-permute-start.1 = (bf16[128,1024]{1,0:T(8,128)(2,1)S(1)}, bf16[128,1024]{1,0:T(8,128)(2,1)S(1)}, u32[]{:S(2)}, u32[]{:S(2)}) collective-permute-start(bf16[128,1024]{1,0:T(8,128)(2,1)S(1)} %get-tuple-element.50.refs_2_), channel_id=1, source_target_pairs={{0,2},{2,4},{4,6},{6,0},{1,3},{3,5},{5,7},{7,1},{8,10},{10,12},{12... | collective-permute-start | bytes 786440 | tf_op jit(solution)/shard_map/ppermute | solution.py:305
  7.2 14.9 %collective-permute-start.2 = (bf16[128,1024]{1,0:T(8,128)(2,1)S(1)}, bf16[128,1024]{1,0:T(8,128)(2,1)S(1)}, u32[]{:S(2)}, u32[]{:S(2)}) collective-permute-start(bf16[128,1024]{1,0:T(8,128)(2,1)S(1)} %get-tuple-element.51.refs_3_), channel_id=1, source_target_pairs={{0,4},{2,6},{4,0},{6,2},{1,5},{3,7},{5,1},{7,3},{8,12},{10,14},{12... | collective-permute-start | bytes 786440 | tf_op jit(solution)/shard_map/ppermute | solution.py:305
  10.0 12.2 %collective-permute-start.3 = (bf16[128,1024]{1,0:T(8,128)(2,1)S(1)}, bf16[128,1024]{1,0:T(8,128)(2,1)S(1)}, u32[]{:S(2)}, u32[]{:S(2)}) collective-permute-start(bf16[128,1024]{1,0:T(8,128)(2,1)S(1)} %get-tuple-element.52.refs_4_), channel_id=1, source_target_pairs={{0,6},{2,0},{4,2},{6,4},{1,7},{3,1},{5,3},{7,5},{8,14},{10,8},{12,... | collective-permute-start | bytes 786440 | tf_op jit(solution)/shard_map/ppermute | solution.py:305
  23.4 7.7 %collective-permute-start.4 = (f32[136,256]{1,0:T(8,128)S(1)}, f32[136,256]{1,0:T(8,128)S(1)}, u32[]{:S(2)}, u32[]{:S(2)}) collective-permute-start(f32[136,256]{1,0:T(8,128)S(1)} %get-tuple-element.60), channel_id=1, source_target_pairs={{0,8},{8,16},{16,24},{24,0},{1,9},{9,17},{17,25},{25,1},{2,10},{10... | collective-permute-start | bytes 417800 | tf_op jit(solution)/shard_map/ppermute | solution.py:305
  25.4 9.6 %collective-permute-start.5 = (f32[136,256]{1,0:T(8,128)S(1)}, f32[136,256]{1,0:T(8,128)S(1)}, u32[]{:S(2)}, u32[]{:S(2)}) collective-permute-start(f32[136,256]{1,0:T(8,128)S(1)} %get-tuple-element.61), channel_id=1, source_target_pairs={{0,16},{8,24},{16,0},{24,8},{1,17},{9,25},{17,1},{25,9},{2,18},{10... | collective-permute-start | bytes 417800 | tf_op jit(solution)/shard_map/ppermute | solution.py:305
  29.0 6.1 %collective-permute-start.6 = (f32[136,256]{1,0:T(8,128)S(1)}, f32[136,256]{1,0:T(8,128)S(1)}, u32[]{:S(2)}, u32[]{:S(2)}) collective-permute-start(f32[136,256]{1,0:T(8,128)S(1)} %get-tuple-element.62), channel_id=1, source_target_pairs={{0,24},{8,0},{16,8},{24,16},{1,25},{9,1},{17,9},{25,17},{2,26},{10... | collective-permute-start | bytes 417800 | tf_op jit(solution)/shard_map/ppermute | solution.py:305
  35.7 10.1 %collective-permute-start.7 = (f32[136,256]{1,0:T(8,128)S(1)}, f32[136,256]{1,0:T(8,128)S(1)}, u32[]{:S(2)}, u32[]{:S(2)}) collective-permute-start(f32[136,256]{1,0:T(8,128)S(1)} %get-tuple-element.63.refs_1_), channel_id=1, source_target_pairs={{0,32},{32,64},{64,96},{96,0},{1,33},{33,65},{65,97},{97,1},{2,34}... | collective-permute-start | bytes 417800 | tf_op jit(solution)/shard_map/ppermute | solution.py:305
  37.4 13.9 %collective-permute-start.13 = (bf16[144,768]{1,0:T(8,128)(2,1)S(1)}, bf16[144,768]{1,0:T(8,128)(2,1)S(1)}, u32[]{:S(2)}, u32[]{:S(2)}) collective-permute-start(bf16[144,768]{1,0:T(8,128)(2,1)S(1)} %get-tuple-element.70), channel_id=1, source_target_pairs={{0,2},{2,4},{4,6},{6,0},{1,3},{3,5},{5,7},{7,1},{8,10},{10,12},{12... | collective-permute-start | bytes 663560 | tf_op jit(solution)/shard_map/ppermute | solution.py:305
  38.5 8.1 %collective-permute-start.8 = (f32[136,256]{1,0:T(8,128)S(1)}, f32[136,256]{1,0:T(8,128)S(1)}, u32[]{:S(2)}, u32[]{:S(2)}) collective-permute-start(f32[136,256]{1,0:T(8,128)S(1)} %get-tuple-element.63.refs_1_), channel_id=1, source_target_pairs={{0,64},{32,96},{64,0},{96,32},{1,65},{33,97},{65,1},{97,33},{2,66}... | collective-permute-start | bytes 417800 | tf_op jit(solution)/shard_map/ppermute | solution.py:305
  41.4 5.2 %collective-permute-start.9 = (f32[136,256]{1,0:T(8,128)S(1)}, f32[136,256]{1,0:T(8,128)S(1)}, u32[]{:S(2)}, u32[]{:S(2)}) collective-permute-start(f32[136,256]{1,0:T(8,128)S(1)} %get-tuple-element.63.refs_1_), channel_id=1, source_target_pairs={{0,96},{32,0},{64,32},{96,64},{1,97},{33,1},{65,33},{97,65},{2,98}... | collective-permute-start | bytes 417800 | tf_op jit(solution)/shard_map/ppermute | solution.py:305
  42.8 9.5 %collective-permute-start.14 = (bf16[144,768]{1,0:T(8,128)(2,1)S(1)}, bf16[144,768]{1,0:T(8,128)(2,1)S(1)}, u32[]{:S(2)}, u32[]{:S(2)}) collective-permute-start(bf16[144,768]{1,0:T(8,128)(2,1)S(1)} %get-tuple-element.71), channel_id=1, source_target_pairs={{0,4},{2,6},{4,0},{6,2},{1,5},{3,7},{5,1},{7,3},{8,12},{10,14},{12... | collective-permute-start | bytes 663560 | tf_op jit(solution)/shard_map/ppermute | solution.py:305
  45.8 7.8 %collective-permute-start.15 = (bf16[144,768]{1,0:T(8,128)(2,1)S(1)}, bf16[144,768]{1,0:T(8,128)(2,1)S(1)}, u32[]{:S(2)}, u32[]{:S(2)}) collective-permute-start(bf16[144,768]{1,0:T(8,128)(2,1)S(1)} %get-tuple-element.72), channel_id=1, source_target_pairs={{0,6},{2,0},{4,2},{6,4},{1,7},{3,1},{5,3},{7,5},{8,14},{10,8},{12,... | collective-permute-start | bytes 663560 | tf_op jit(solution)/shard_map/ppermute | solution.py:305
  47.4 9.4 %collective-permute-start.10 = (f32[128,256]{1,0:T(8,128)S(1)}, f32[128,256]{1,0:T(8,128)S(1)}, u32[]{:S(2)}, u32[]{:S(2)}) collective-permute-start(f32[128,256]{1,0:T(8,128)S(1)} %get-tuple-element.66), channel_id=1, source_target_pairs={{0,8},{8,16},{16,24},{24,0},{1,9},{9,17},{17,25},{25,1},{2,10},{10... | collective-permute-start | bytes 393224 | tf_op jit(solution)/shard_map/ppermute | solution.py:305
  49.1 7.7 %collective-permute-start.11 = (f32[128,256]{1,0:T(8,128)S(1)}, f32[128,256]{1,0:T(8,128)S(1)}, u32[]{:S(2)}, u32[]{:S(2)}) collective-permute-start(f32[128,256]{1,0:T(8,128)S(1)} %get-tuple-element.67), channel_id=1, source_target_pairs={{0,16},{8,24},{16,0},{24,8},{1,17},{9,25},{17,1},{25,9},{2,18},{10... | collective-permute-start | bytes 393224 | tf_op jit(solution)/shard_map/ppermute | solution.py:305
  51.2 5.5 %collective-permute-start.12 = (f32[128,256]{1,0:T(8,128)S(1)}, f32[128,256]{1,0:T(8,128)S(1)}, u32[]{:S(2)}, u32[]{:S(2)}) collective-permute-start(f32[128,256]{1,0:T(8,128)S(1)} %get-tuple-element.68), channel_id=1, source_target_pairs={{0,24},{8,0},{16,8},{24,16},{1,25},{9,1},{17,9},{25,17},{2,26},{10... | collective-permute-start | bytes 393224 | tf_op jit(solution)/shard_map/ppermute | solution.py:305
  61.1 5.2 %collective-permute-start.20 = (f32[8,256]{1,0:T(8,128)S(1)}, f32[8,256]{1,0:T(8,128)S(1)}, u32[]{:S(2)}, u32[]{:S(2)}) collective-permute-start(f32[8,256]{1,0:T(8,128)S(1)} %broadcast_in_dim.20), channel_id=1, source_target_pairs={{0,16},{8,24},{16,0},{24,8},{1,17},{9,25},{17,1},{25,9},{2,18},{10... | collective-permute-start | bytes 24584 | tf_op jit(solution)/shard_map/ppermute | solution.py:305
  67.3 8.3 %collective-permute-start.24 = (f32[8,256]{1,0:T(8,128)S(1)}, f32[8,256]{1,0:T(8,128)S(1)}, u32[]{:S(2)}, u32[]{:S(2)}) collective-permute-start(f32[8,256]{1,0:T(8,128)S(1)} %add_add_fusion.1), channel_id=1, source_target_pairs={{0,96},{32,0},{64,32},{96,64},{1,97},{33,1},{65,33},{97,65},{2,98}... | collective-permute-start | bytes 24584 | tf_op jit(solution)/shard_map/ppermute | solution.py:305
  68.9 20.2 %collective-permute-start.16 = (bf16[128,1024]{1,0:T(8,128)(2,1)S(1)}, bf16[128,1024]{1,0:T(8,128)(2,1)S(1)}, u32[]{:S(2)}, u32[]{:S(2)}) collective-permute-start(bf16[128,1024]{1,0:T(8,128)(2,1)S(1)} %get-tuple-element.83), channel_id=1, source_target_pairs={{0,2},{2,4},{4,6},{6,0},{1,3},{3,5},{5,7},{7,1},{8,10},{10,12},{12... | collective-permute-start | bytes 786440 | tf_op jit(solution)/shard_map/ppermute | solution.py:305
  70.1 19.0 %collective-permute-start.17 = (bf16[128,1024]{1,0:T(8,128)(2,1)S(1)}, bf16[128,1024]{1,0:T(8,128)(2,1)S(1)}, u32[]{:S(2)}, u32[]{:S(2)}) collective-permute-start(bf16[128,1024]{1,0:T(8,128)(2,1)S(1)} %get-tuple-element.84), channel_id=1, source_target_pairs={{0,4},{2,6},{4,0},{6,2},{1,5},{3,7},{5,1},{7,3},{8,12},{10,14},{12... | collective-permute-start | bytes 786440 | tf_op jit(solution)/shard_map/ppermute | solution.py:305
  72.5 16.6 %collective-permute-start.18 = (bf16[128,1024]{1,0:T(8,128)(2,1)S(1)}, bf16[128,1024]{1,0:T(8,128)(2,1)S(1)}, u32[]{:S(2)}, u32[]{:S(2)}) collective-permute-start(bf16[128,1024]{1,0:T(8,128)(2,1)S(1)} %get-tuple-element.85), channel_id=1, source_target_pairs={{0,6},{2,0},{4,2},{6,4},{1,7},{3,1},{5,3},{7,5},{8,14},{10,8},{12,... | collective-permute-start | bytes 786440 | tf_op jit(solution)/shard_map/ppermute | solution.py:305
  75.0 5.2 %collective-permute-start.23 = (f32[8,256]{1,0:T(8,128)S(1)}, f32[8,256]{1,0:T(8,128)S(1)}, u32[]{:S(2)}, u32[]{:S(2)}) collective-permute-start(f32[8,256]{1,0:T(8,128)S(1)} %add_add_fusion.1), channel_id=1, source_target_pairs={{0,64},{32,96},{64,0},{96,32},{1,65},{33,97},{65,1},{97,33},{2,66}... | collective-permute-start | bytes 24584 | tf_op jit(solution)/shard_map/ppermute | solution.py:305
  75.6 4.9 %collective-permute-start.22 = (f32[8,256]{1,0:T(8,128)S(1)}, f32[8,256]{1,0:T(8,128)S(1)}, u32[]{:S(2)}, u32[]{:S(2)}) collective-permute-start(f32[8,256]{1,0:T(8,128)S(1)} %add_add_fusion.1), channel_id=1, source_target_pairs={{0,32},{32,64},{64,96},{96,0},{1,33},{33,65},{65,97},{97,1},{2,34}... | collective-permute-start | bytes 24584 | tf_op jit(solution)/shard_map/ppermute | solution.py:305
  80.5 4.9 %collective-permute-start.25 = (f32[8,256]{1,0:T(8,128)S(1)}, f32[8,256]{1,0:T(8,128)S(1)}, u32[]{:S(2)}, u32[]{:S(2)}) collective-permute-start(f32[8,256]{1,0:T(8,128)S(1)} %add_add_fusion.refs_5_), channel_id=1, source_target_pairs={{0,2},{2,4},{4,6},{6,0},{1,3},{3,5},{5,7},{7,1},{8,10},{10,12},{12... | collective-permute-start | bytes 24584 | tf_op jit(solution)/shard_map/ppermute | solution.py:305
  81.3 5.2 %collective-permute-start.26 = (f32[8,256]{1,0:T(8,128)S(1)}, f32[8,256]{1,0:T(8,128)S(1)}, u32[]{:S(2)}, u32[]{:S(2)}) collective-permute-start(f32[8,256]{1,0:T(8,128)S(1)} %add_add_fusion.refs_5_), channel_id=1, source_target_pairs={{0,4},{2,6},{4,0},{6,2},{1,5},{3,7},{5,1},{7,3},{8,12},{10,14},{12... | collective-permute-start | bytes 24584 | tf_op jit(solution)/shard_map/ppermute | solution.py:305
  (10 other events, 43.3 us)
where the time goes:
time: 93 us; the launch traced here: 92.9 us
  starting transfers between devices  42.8 us (46%)
  waiting for transfers between devices  27.9 us (30%)
  Pallas kernels  20.1 us (22%)
  local copies, waits for them, and re-layouts  1.11 us (1%)
    ppermute x27, starting transfers between devices, shifted(): return lax.ppermute(value, axis, [(i, (i + s) % 4) for i in range(4)])  42.7 us
    ppermute x27, waiting for transfers between devices, shifted(): return lax.ppermute(value, axis, [(i, (i + s) % 4) for i in range(4)])  27.8 us
    pallas_call x11, Pallas kernels, call(): return lambda *operands: run(*operands, *after)  20.1 us
  transfers between devices with their start and end apart: 28, of which 12 were waited for; matrix products, arithmetic and copies ran while one was open for 0% of the time, Pallas kernels for 11%

commit v1 on v0

--- a/solution.py
+++ b/solution.py
@@ -15,12 +15,20 @@
 NT = ((1,), (1,))
 TN = ((0,), (0,))
 TOK, NH, DK, DV = 128, 4, 256, 512
+GROUPS = 16
 SCALE = DK ** (-0.5)
 
 
 def split(x):
     high = x.astype(B16)
     return high, (x - high.astype(F32)).astype(B16)
+
+
+def three(x):
+    first = x.astype(B16)
+    rest = x - first.astype(F32)
+    second = rest.astype(B16)
+    return first, second, (rest - second.astype(F32)).astype(B16)
 
 
 def dot(a, b, dims):
@@ -122,14 +130,9 @@
         qdq = q * dq
         qdq_out[h] = qdq
         total = jnp.sum(qdq, axis=0, keepdims=True)
-        t0 = total.astype(B16)
-        rest = total - t0.astype(F32)
-        t1 = rest.astype(B16)
-        t2 = (rest - t1.astype(F32)).astype(B16)
         kv_out[s][:TOK, :] = kv[s][...]
-        kv_out[s][TOK:, :DK] = jnp.broadcast_to(t0, (16, DK))
-        kv_out[s][TOK:, DK : 2 * DK] = jnp.broadcast_to(t1, (16, DK))
-        kv_out[s][TOK:, 2 * DK :] = jnp.broadcast_to(t2, (16, DK))
+        for i, word in enumerate(three(total)):
+            kv_out[s][TOK:, DK * i : DK * (i + 1)] = jnp.broadcast_to(word, (16, DK))
     for h in range(NH):
         dq_out[:, h, :] = scr[h].astype(B16)
 
@@ -241,7 +244,7 @@
     dk_near, dv_near, k_end, ends, v, k = refs[8:14]
     outs = refs[14:18]
     sums = refs[18]
-    state, scr = refs[19:21]
+    state, scr, total = refs[19:22]
     x, z = idx[0], idx[1]
     for s in range(4):
         j = (z - s + 4) % 4
@@ -249,18 +252,23 @@
     high, lo = split(state[...])
     reached = dot(v[...], high, NN) + dot(v[...], lo, NN)
     dk = dk_near[...] + ends[...] * reached
-    dk_high, dk_low = split(dk)
     e_high, e_low = split(k_end[...])
     dv = dv_near[...] + (
         dot(e_high, high, NT) + (dot(e_low, high, NT) + dot(e_high, lo, NT))
     )
     kdk = k[...].astype(F32) * dk
+    group = lax.broadcasted_iota(jnp.int32, (GROUPS, TOK), 0)
+    token = lax.broadcasted_iota(jnp.int32, (GROUPS, TOK), 1)
+    after = (token >= (group + 1) * (TOK // GROUPS)).astype(B16)
     for j in range(4):
         rows = slice(TOK * j, TOK * (j + 1))
-        scr[j, :, :DK] = dk_high[rows, :]
-        scr[j, :, DK : 2 * DK] = dk_low[rows, :]
-        scr[j, :, 2 * DK :] = dv[rows, :].astype(B16)
-        sums[j : j + 1, :] = -jnp.sum(kdk[rows, :], axis=0, keepdims=True)
+        part_high, part_low = split(kdk[rows, :])
+        ahead = three(dot(after, part_high, NN) + dot(after, part_low, NN))
+        scr[j, :TOK, :DK] = dk[rows, :].astype(B16)
+        scr[j, :TOK, DK:] = dv[rows, :].astype(B16)
+        for i in range(3):
+            scr[j, TOK:, DK * i : DK * (i + 1)] = ahead[i]
+        total[j : j + 1, :] = -jnp.sum(kdk[rows, :], axis=0, keepdims=True)
     for s in range(4):
         j = (x - s + 4) % 4
         tot = (
@@ -268,37 +276,67 @@
             + kv[s][TOK : TOK + 1, DK : 2 * DK].astype(F32)
             + kv[s][TOK : TOK + 1, 2 * DK :].astype(F32)
         )
-        sums[pl.ds(j, 1), :] = sums[pl.ds(j, 1), :] + tot
-    sums[4:5, :] = jnp.sum(sums[0:4, :], axis=0, keepdims=True)
-    sums[5:8, :] = jnp.zeros((3, DK), F32)
+        total[pl.ds(j, 1), :] = total[pl.ds(j, 1), :] + tot
+    for j in range(4):
+        sums[0, 2 * j : 2 * j + 1, :] = total[j : j + 1, :128]
+        sums[0, 2 * j + 1 : 2 * j + 2, :] = total[j : j + 1, 128:]
+    block = sums[0]
+    for d in range(1, 64):
+        sums[d] = block
     for s in range(4):
         outs[s][...] = scr[(x + s) % 4]
 
 
 def final_part(idx, *refs):
-    parts, later = refs[0:4], refs[4:8]
-    qdq = refs[8]
-    key = refs[9]
-    dk_out, dv_out, da_out = refs[10:13]
-    s_dk, s_dv, s_da, s_k = refs[13:17]
+    parts = refs[0:4]
+    qdq, key = refs[4:6]
+    dk_out, dv_out, da_part = refs[6:9]
+    s_dk, s_dv, s_k = refs[9:12]
     x = idx[0]
     for h in range(NH):
         s_k[h] = key[:, h, :]
-    upper = triangle(True).astype(B16)
+    row = lax.broadcasted_iota(jnp.int32, (TOK, TOK), 0)
+    col = lax.broadcasted_iota(jnp.int32, (TOK, TOK), 1)
+    size = TOK // GROUPS
+    upper = (col >= row).astype(B16)
+    inner = ((col >= row) & (col // size == row // size)).astype(B16)
+    pick_row = lax.broadcasted_iota(jnp.int32, (TOK, GROUPS), 0)
+    pick_col = lax.broadcasted_iota(jnp.int32, (TOK, GROUPS), 1)
+    pick = (pick_row // size == pick_col).astype(B16)
     for s in range(4):
         h = (x - s + 4) % 4
-        dk_high = parts[s][:, :DK]
-        dk = dk_high.astype(F32) + parts[s][:, DK : 2 * DK].astype(F32)
-        s_dk[h] = dk_high
-        s_dv[h] = parts[s][:, 2 * DK :]
-        weight = qdq[h] - s_k[h].astype(F32) * dk
-        w_high, w_low = split(weight)
-        da = dot(upper, w_high, NN) + dot(upper, w_low, NN) + later[s][pl.ds(x, 1), :]
-        s_da[h] = da.astype(B16)
+        dk = parts[s][:TOK, :DK]
+        s_dk[h] = dk
+        s_dv[h] = parts[s][:TOK, DK:]
+        q_high, q_low = split(qdq[h])
+        k_high, k_low = split(s_k[h].astype(F32) * dk.astype(F32))
+        ahead = (
+            dot(pick, parts[s][TOK:, :DK], NN)
+            + dot(pick, parts[s][TOK:, DK : 2 * DK], NN)
+            + dot(pick, parts[s][TOK:, 2 * DK :], NN)
+        )
+        da_part[h] = (
+            (dot(upper, q_high, NN) + dot(upper, q_low, NN))
+            - (dot(inner, k_high, NN) + dot(inner, k_low, NN))
+            - ahead
+        )
     for h in range(NH):
         dk_out[:, h, :] = s_dk[h]
         dv_out[:, h, :] = s_dv[h]
-        da_out[:, h, :] = s_da[h]
+
+
+def decay_part(idx, da_part, sums, da_out):
+    x, line = idx[0], idx[2] * 4 + idx[1]
+    segment = lax.broadcasted_iota(jnp.int32, (8, 128), 0) // 2
+    for h in range(NH):
+        acc = jnp.zeros((8, 128), F32)
+        for l in range(16):
+            counted = (l > line) | ((l == line) & (segment > x))
+            acc = acc + jnp.where(counted, sums[4 * l + h], 0.0)
+        first = acc[0:1] + acc[2:3] + acc[4:5] + acc[6:7]
+        second = acc[1:2] + acc[3:4] + acc[5:6] + acc[7:8]
+        later = jnp.concatenate([first, second], axis=1)
+        da_out[:, h, :] = (da_part[h] + later).astype(B16)
 
 
 def shifted(value, axis, s):
@@ -373,40 +411,20 @@
     )(idx, qa_rows, g_rows, *kv_line)
     res = call(
         far_part,
-        [sds((TOK, 2 * DK + DV))] * 4 + [sds((8, DK), F32)],
+        [sds((TOK + GROUPS, DK + DV))] * 4 + [sds((64, 8, 128), F32)],
         14,
-        [vm((DV, DK), F32), vm((4, TOK, 2 * DK + DV), B16)],
+        [vm((DV, DK), F32), vm((4, TOK + GROUPS, DK + DV), B16), vm((4, DK), F32)],
     )(idx, *carry_in, *kv_line, *near)
     back, sums = res[:4], res[4]
     back_in = spread(back, X)
-
-    def beyond(total, axis, index):
-        parts = spread([total] * 4, axis)
-        later = jnp.zeros_like(total)
-        everything = total
-        for s in (1, 2, 3):
-            later = later + jnp.where((index - s) % 4 > index, parts[s], 0.0)
-            everything = everything + parts[s]
-        return later, everything
-
-    line_total = sums[4:5]
-    z_later, z_all = beyond(jnp.broadcast_to(line_total, (8, DK)), Z, z)
-    y_later, _ = beyond(z_all, Y, y)
-    outside = z_later + y_later
-    inside = jnp.stack([jnp.sum(sums[j + 1 : 4], axis=0) for j in range(4)])
-    later = outside + jnp.concatenate([inside, jnp.zeros((4, DK), F32)])
-    later_in = spread([later] * 4, X)
-    dk, dv, da = call(
+    sums = lax.all_to_all(sums, SEQ, split_axis=0, concat_axis=0, tiled=True)
+    dk, dv, da_part = call(
         final_part,
-        [sds((TOK, NH, DK)), sds((TOK, NH, DV)), sds((TOK, NH, DK))],
-        10,
-        [
-            vm((NH, TOK, DK), B16),
-            vm((NH, TOK, DV), B16),
-            vm((NH, TOK, DK), B16),
-            vm((NH, TOK, DK), B16),
-        ],
-    )(idx, *back_in, *later_in, qdq, key)
+        [sds((TOK, NH, DK)), sds((TOK, NH, DV)), sds((NH, TOK, DK), F32)],
+        6,
+        [vm((NH, TOK, DK), B16), vm((NH, TOK, DV), B16), vm((NH, TOK, DK), B16)],
+    )(idx, *back_in, qdq, key)
+    da = call(decay_part, sds((TOK, NH, DK)), 2, ())(idx, da_part, sums)
     return dq, dk, dv, da
 
 

time: 93 us -> 88.4 us (0.951)
  waiting for transfers between devices: 27.9 us -> 22.1 us
  Pallas kernels: 20.1 us -> 22.2 us
    ppermute x27 -> x18, starting transfers between devices: 42.7 us -> 34.4 us  [shifted(): return lax.ppermute(value, axis, [(i, (i + s) % 4) for i in range(4)])]
    all_to_all x0 -> x1, starting transfers between devices: none -> 7.39 us  [whole(): sums = lax.all_to_all(sums, SEQ, split_axis=0, concat_axis=0, tiled=True)]
    ppermute x27 -> x18, waiting for transfers between devices: 27.8 us -> 22 us  [shifted(): return lax.ppermute(value, axis, [(i, (i + s) % 4) for i in range(4)])]
    pallas_call x11 -> x12, Pallas kernels: 20.1 us -> 22.2 us  [call(): return lambda *operands: run(*operands, *after)]
  transfers between devices with their start and end apart: 28 -> 20, of which waited for: 12 -> 8; matrix products, arithmetic and copies ran while one was open for 0% -> 0% of each run, Pallas kernels for 11% -> 16%
where the time goes in v1:
time: 88.4 us; the launch traced here: 88.1 us
  starting transfers between devices  41.9 us (47%)
  Pallas kernels  22.2 us (25%)
  waiting for transfers between devices  22.1 us (25%)
  local copies, waits for them, and re-layouts  1.07 us (1%)
    ppermute x18, starting transfers between devices, shifted(): return lax.ppermute(value, axis, [(i, (i + s) % 4) for i in range(4)])  34.4 us
    pallas_call x12, Pallas kernels, call(): return lambda *operands: run(*operands, *after)  22.2 us
    ppermute x18, waiting for transfers between devices, shifted(): return lax.ppermute(value, axis, [(i, (i + s) % 4) for i in range(4)])  22 us
    all_to_all x1, starting transfers between devices, whole(): sums = lax.all_to_all(sums, SEQ, split_axis=0, concat_axis=0, tiled=True)  7.39 us
  transfers between devices with their start and end apart: 20, of which 8 were waited for; matrix products, arithmetic and copies ran while one was open for 0% of the time, Pallas kernels for 16%

profile of v1, /device:TPU:0, one launch (start us, length us, event | category | flops | bytes accessed | tf_op | source)
XLA Modules:
  0.0 88.1 jit_solution(13022211989606133174)
XLA Ops:
  1.8 1.5 %shard_map.94 = (bf16[4,64,512]{2,1,0:T(8,128)(2,1)S(1)}, bf16[4,64,512]{2,1,0:T(8,128)(2,1)S(1)}) custom-call(s32[4]{0:T(128)S(1)} %pad_add_fusion.refs_0_, bf16[64,8,512]{2,1,0:T(8,128)(2,1)S(1)} %copy-done.2), custom_call_target="tpu_custom_call" | custom-call | tf_op jit(solution)/shard_map/pallas_call | solution.py:74
  5.6 1.7 %collective-permute-start.1 = (bf16[128,1024]{1,0:T(8,128)(2,1)S(1)}, bf16[128,1024]{1,0:T(8,128)(2,1)S(1)}, u32[]{:S(2)}, u32[]{:S(2)}) collective-permute-start(bf16[128,1024]{1,0:T(8,128)(2,1)S(1)} %get-tuple-element.50.refs_2_), channel_id=1, source_target_pairs={{0,2},{2,4},{4,6},{6,0},{1,3},{3,5},{5,7},{7,1},{8,10},{10,12},{12... | collective-permute-start | bytes 786440 | tf_op jit(solution)/shard_map/ppermute | solution.py:343
  7.2 2.7 %collective-permute-start.2 = (bf16[128,1024]{1,0:T(8,128)(2,1)S(1)}, bf16[128,1024]{1,0:T(8,128)(2,1)S(1)}, u32[]{:S(2)}, u32[]{:S(2)}) collective-permute-start(bf16[128,1024]{1,0:T(8,128)(2,1)S(1)} %get-tuple-element.51.refs_3_), channel_id=1, source_target_pairs={{0,4},{2,6},{4,0},{6,2},{1,5},{3,7},{5,1},{7,3},{8,12},{10,14},{12... | collective-permute-start | bytes 786440 | tf_op jit(solution)/shard_map/ppermute | solution.py:343
  11.4 2.3 %shard_map.96 = (bf16[128,768]{1,0:T(8,128)(2,1)S(1)}, bf16[128,768]{1,0:T(8,128)(2,1)S(1)}, bf16[128,768]{1,0:T(8,128)(2,1)S(1)}, bf16[128,768]{1,0:T(8,128)(2,1)S(1)}) custom-call(s32[4]{0:T(128)S(1)} %pad_add_fusion.refs_0_, bf16[128,4,256]{2,1,0:T(4,128)(2,1)S(1)} %copy-done.1, bf16[128,4,512]{2,1,0:T(4,128)(2,1)S(1)} %copy-done.3), custom_call_target="tpu_custom_call" | custom-call | tf_op jit(solution)/shard_map/pallas_call | solution.py:74
  13.7 3.2 %shard_map.97 = (bf16[128,4,256]{2,1,0:T(4,128)(2,1)}, f32[4,128,256]{2,1,0:T(8,128)S(1)}, bf16[144,768]{1,0:T(8,128)(2,1)S(1)}, bf16[144,768]{1,0:T(8,128)(2,1)...) custom-call(s32[4]{0:T(128)S(1)} %pad_add_fusion.refs_0_, ...), custom_call_target="tpu_custom_call" | custom-call | tf_op jit(solution)/shard_map/pallas_call | solution.py:74
  16.9 5.3 %collective-permute-done.2.refs_3_ = bf16[128,1024]{1,0:T(8,128)(2,1)S(1)} collective-permute-done((bf16[128,1024]{1,0:T(8,128)(2,1)S(1)}, bf16[128,1024]{1,0:T(8,128)(2,1)S(1)}, u32[]{:S(2)}, u32[]{:S(2)}) %collective-permute-start.2) | collective-permute-done | bytes 262176 | tf_op jit(solution)/shard_map/ppermute | solution.py:343
  23.4 2.0 %collective-permute-start.4 = (f32[136,256]{1,0:T(8,128)S(1)}, f32[136,256]{1,0:T(8,128)S(1)}, u32[]{:S(2)}, u32[]{:S(2)}) collective-permute-start(f32[136,256]{1,0:T(8,128)S(1)} %get-tuple-element.60), channel_id=1, source_target_pairs={{0,8},{8,16},{16,24},{24,0},{1,9},{9,17},{17,25},{25,1},{2,10},{10... | collective-permute-start | bytes 417800 | tf_op jit(solution)/shard_map/ppermute | solution.py:343
  25.4 3.6 %collective-permute-start.5 = (f32[136,256]{1,0:T(8,128)S(1)}, f32[136,256]{1,0:T(8,128)S(1)}, u32[]{:S(2)}, u32[]{:S(2)}) collective-permute-start(f32[136,256]{1,0:T(8,128)S(1)} %get-tuple-element.61), channel_id=1, source_target_pairs={{0,16},{8,24},{16,0},{24,8},{1,17},{9,25},{17,1},{25,9},{2,18},{10... | collective-permute-start | bytes 417800 | tf_op jit(solution)/shard_map/ppermute | solution.py:343
  31.2 3.9 %collective-permute-done.5.refs_3_ = f32[136,256]{1,0:T(8,128)S(1)} collective-permute-done((f32[136,256]{1,0:T(8,128)S(1)}, f32[136,256]{1,0:T(8,128)S(1)}, u32[]{:S(2)}, u32[]{:S(2)}) %collective-permute-start.5) | collective-permute-done | bytes 139296 | tf_op jit(solution)/shard_map/ppermute | solution.py:343
  35.7 3.1 %collective-permute-start.9 = (f32[136,256]{1,0:T(8,128)S(1)}, f32[136,256]{1,0:T(8,128)S(1)}, u32[]{:S(2)}, u32[]{:S(2)}) collective-permute-start(f32[136,256]{1,0:T(8,128)S(1)} %get-tuple-element.63.refs_1_), channel_id=1, source_target_pairs={{0,96},{32,0},{64,32},{96,64},{1,97},{33,1},{65,33},{97,65},{2,98}... | collective-permute-start | bytes 417800 | tf_op jit(solution)/shard_map/ppermute | solution.py:343
  41.6 3.1 %collective-permute-start.14 = (bf16[144,768]{1,0:T(8,128)(2,1)S(1)}, bf16[144,768]{1,0:T(8,128)(2,1)S(1)}, u32[]{:S(2)}, u32[]{:S(2)}) collective-permute-start(bf16[144,768]{1,0:T(8,128)(2,1)S(1)} %get-tuple-element.71), channel_id=1, source_target_pairs={{0,4},{2,6},{4,0},{6,2},{1,5},{3,7},{5,1},{7,3},{8,12},{10,14},{12... | collective-permute-start | bytes 663560 | tf_op jit(solution)/shard_map/ppermute | solution.py:343
  44.6 2.2 %collective-permute-start.15 = (bf16[144,768]{1,0:T(8,128)(2,1)S(1)}, bf16[144,768]{1,0:T(8,128)(2,1)S(1)}, u32[]{:S(2)}, u32[]{:S(2)}) collective-permute-start(bf16[144,768]{1,0:T(8,128)(2,1)S(1)} %get-tuple-element.72), channel_id=1, source_target_pairs={{0,6},{2,0},{4,2},{6,4},{1,7},{3,1},{5,3},{7,5},{8,14},{10,8},{12,... | collective-permute-start | bytes 663560 | tf_op jit(solution)/shard_map/ppermute | solution.py:343
  48.8 2.4 %collective-permute-start.10 = (f32[128,256]{1,0:T(8,128)S(1)}, f32[128,256]{1,0:T(8,128)S(1)}, u32[]{:S(2)}, u32[]{:S(2)}) collective-permute-start(f32[128,256]{1,0:T(8,128)S(1)} %get-tuple-element.66), channel_id=1, source_target_pairs={{0,8},{8,16},{16,24},{24,0},{1,9},{9,17},{17,25},{25,1},{2,10},{10... | collective-permute-start | bytes 393224 | tf_op jit(solution)/shard_map/ppermute | solution.py:343
  51.1 1.9 %collective-permute-start.11 = (f32[128,256]{1,0:T(8,128)S(1)}, f32[128,256]{1,0:T(8,128)S(1)}, u32[]{:S(2)}, u32[]{:S(2)}) collective-permute-start(f32[128,256]{1,0:T(8,128)S(1)} %get-tuple-element.67), channel_id=1, source_target_pairs={{0,16},{8,24},{16,0},{24,8},{1,17},{9,25},{17,1},{25,9},{2,18},{10... | collective-permute-start | bytes 393224 | tf_op jit(solution)/shard_map/ppermute | solution.py:343
  53.9 3.1 %shard_map.101 = (f32[512,256]{1,0:T(8,128)S(1)}, f32[512,512]{1,0:T(8,128)S(1)}, f32[512,256]{1,0:T(8,128)S(1)}, f32[512,256]{1,0:T(8,128)S(1)}, bf16[512,512]{...) custom-call(s32[4]{0:T(128)S(1)} %pad_add_fusion.refs_0_, bf16[512,512]{1,0:T(8,128)(2,1)S(1)} %get-tuple-element.73.refs_1_, ...), custom_call_target="tpu_custom_call" | custom-call | tf_op jit(solution)/shard_map/pallas_call | solution.py:74
  57.1 1.6 %collective-permute-done.11.refs_3_ = f32[128,256]{1,0:T(8,128)S(1)} collective-permute-done((f32[128,256]{1,0:T(8,128)S(1)}, f32[128,256]{1,0:T(8,128)S(1)}, u32[]{:S(2)}, u32[]{:S(2)}) %collective-permute-start.11) | collective-permute-done | bytes 131104 | tf_op jit(solution)/shard_map/ppermute | solution.py:343
  58.7 2.1 %shard_map.102 = (bf16[144,768]{1,0:T(8,128)(2,1)S(1)}, bf16[144,768]{1,0:T(8,128)(2,1)S(1)}, bf16[144,768]{1,0:T(8,128)(2,1)S(1)}, bf16[144,768]{1,0:T(8,128)(2,1)S(1)}, f32[64,8,128]{2,1,0:T(8,128)}) custom-call(s32[4]{0:T(128)S(1)} %pad_add_fusion.refs_0_, f32[128,256]{1,0:T(8,128)S(1)} %get-tuple-element.65.refs_1_, ...), custom_call_target="tpu_custom_call" | custom-call | tf_op jit(solution)/shard_map/pallas_call | solution.py:74
  60.8 7.4 %all-to-all-start = ((f32[64,8,128]{2,1,0:T(8,128)}), f32[64,8,128]{2,1,0:T(8,128)S(1)}, u32[]{:S(2)}, u32[]{:S(2)}) async-start(f32[64,8,128]{2,1,0:T(8,128)} %get-tuple-element.89), calls=%async_computation | async-start | bytes 524288 | tf_op jit(solution)/shard_map/all_to_all | solution.py:420
  68.2 1.6 %collective-permute-start.16 = (bf16[144,768]{1,0:T(8,128)(2,1)S(1)}, bf16[144,768]{1,0:T(8,128)(2,1)S(1)}, u32[]{:S(2)}, u32[]{:S(2)}) collective-permute-start(bf16[144,768]{1,0:T(8,128)(2,1)S(1)} %get-tuple-element.83), channel_id=1, source_target_pairs={{0,2},{2,4},{4,6},{6,0},{1,3},{3,5},{5,7},{7,1},{8,10},{10,12},{12... | collective-permute-start | bytes 663560 | tf_op jit(solution)/shard_map/ppermute | solution.py:343
  69.9 2.7 %collective-permute-start.17 = (bf16[144,768]{1,0:T(8,128)(2,1)S(1)}, bf16[144,768]{1,0:T(8,128)(2,1)S(1)}, u32[]{:S(2)}, u32[]{:S(2)}) collective-permute-start(bf16[144,768]{1,0:T(8,128)(2,1)S(1)} %get-tuple-element.84), channel_id=1, source_target_pairs={{0,4},{2,6},{4,0},{6,2},{1,5},{3,7},{5,1},{7,3},{8,12},{10,14},{12... | collective-permute-start | bytes 663560 | tf_op jit(solution)/shard_map/ppermute | solution.py:343
  74.0 5.6 %collective-permute-done.16.refs_2_ = bf16[144,768]{1,0:T(8,128)(2,1)S(1)} collective-permute-done((bf16[144,768]{1,0:T(8,128)(2,1)S(1)}, bf16[144,768]{1,0:T(8,128)(2,1)S(1)}, u32[]{:S(2)}, u32[]{:S(2)}) %collective-permute-start.16) | collective-permute-done | bytes 221216 | tf_op jit(solution)/shard_map/ppermute | solution.py:343
  79.6 3.1 %collective-permute-done.17.refs_3_ = bf16[144,768]{1,0:T(8,128)(2,1)S(1)} collective-permute-done((bf16[144,768]{1,0:T(8,128)(2,1)S(1)}, bf16[144,768]{1,0:T(8,128)(2,1)S(1)}, u32[]{:S(2)}, u32[]{:S(2)}) %collective-permute-start.17) | collective-permute-done | bytes 221216 | tf_op jit(solution)/shard_map/ppermute | solution.py:343
  82.8 3.5 %shard_map.103 = (bf16[128,4,256]{2,1,0:T(4,128)(2,1)}, bf16[128,4,512]{2,1,0:T(4,128)(2,1)}, f32[4,128,256]{2,1,0:T(8,128)S(1)}) custom-call(s32[4]{0:T(128)S(1)} %pad_add_fusion.refs_0_, bf16[144,768]{1,0:T(8,128)(2,1)S(1)} %get-tuple-element.82.refs_1_, bf16[144,768]{1,0:T(8,128)(2,1)S(1)} %collective-permute-done.16.refs_2_, ...), custom_call_target="tpu_custom_call" | custom-call | tf_op jit(solution)/shard_map/pallas_call | solution.py:74
  86.3 1.9 %shard_map.104 = bf16[128,4,256]{2,1,0:T(4,128)(2,1)} custom-call(s32[4]{0:T(128)S(1)} %pad_add_fusion.refs_0_, f32[4,128,256]{2,1,0:T(8,128)S(1)} %get-tuple-element.88.refs_1_, f32[64,8,128]{2,1,0:T(8,128)S(1)} %all-to-all-done.refs_2_), custom_call_target="tpu_custom_call" | custom-call | tf_op jit(solution)/shard_map/pallas_call | solution.py:74
  (41 shorter events, 15.9 us)
Async XLA Ops:
  1.8 1.7 %copy-start.5 = (bf16[128,4,256]{2,1,0:T(4,128)(2,1)S(1)}, bf16[128,4,256]{2,1,0:T(4,128)(2,1)}, u32[]{:S(2)}) copy-start(bf16[128,4,256]{2,1,0:T(4,128)(2,1)} %refs_2_.2) | copy-start | bytes 786436
  3.3 1.6 %collective-permute-start = (bf16[4,64,512]{2,1,0:T(8,128)(2,1)S(1)}, bf16[4,64,512]{2,1,0:T(8,128)(2,1)S(1)}, u32[]{:S(2)}, u32[]{:S(2)}) collective-permute-start(bf16[4,64,512]{2,1,0:T(8,128)(2,1)S(1)} %get-tuple-element.48), channel_id=1, source_target_pairs={{0,1},{1,0},{2,3},{3,2},{4,5},{5,4},{6,7},{7,6},{8,9},{9,8},{10,11... | collective-permute-start | bytes 786440 | tf_op jit(solution)/shard_map/ppermute | solution.py:362
  3.4 8.0 %copy-start.1 = (bf16[128,4,256]{2,1,0:T(4,128)(2,1)S(1)}, bf16[128,4,256]{2,1,0:T(4,128)(2,1)}, u32[]{:S(2)}) copy-start(bf16[128,4,256]{2,1,0:T(4,128)(2,1)} %refs_6_.1) | copy-start | bytes 786436
  3.4 8.0 %copy-start.3 = (bf16[128,4,512]{2,1,0:T(4,128)(2,1)S(1)}, bf16[128,4,512]{2,1,0:T(4,128)(2,1)}, u32[]{:S(2)}) copy-start(bf16[128,4,512]{2,1,0:T(4,128)(2,1)} %refs_2_.3) | copy-start | bytes 1572868
  4.8 8.9 %copy-start = (bf16[1,4,256,512]{3,2,1,0:T(8,128)(2,1)S(1)}, bf16[1,4,256,512]{3,2,1,0:T(8,128)(2,1)}, u32[]{:S(2)}) copy-start(bf16[1,4,256,512]{3,2,1,0:T(8,128)(2,1)} %refs_9_.1) | copy-start | bytes 3145732
  5.6 11.3 %collective-permute-start.1 = (bf16[128,1024]{1,0:T(8,128)(2,1)S(1)}, bf16[128,1024]{1,0:T(8,128)(2,1)S(1)}, u32[]{:S(2)}, u32[]{:S(2)}) collective-permute-start(bf16[128,1024]{1,0:T(8,128)(2,1)S(1)} %get-tuple-element.50.refs_2_), channel_id=1, source_target_pairs={{0,2},{2,4},{4,6},{6,0},{1,3},{3,5},{5,7},{7,1},{8,10},{10,12},{12... | collective-permute-start | bytes 786440 | tf_op jit(solution)/shard_map/ppermute | solution.py:343
  7.2 14.9 %collective-permute-start.2 = (bf16[128,1024]{1,0:T(8,128)(2,1)S(1)}, bf16[128,1024]{1,0:T(8,128)(2,1)S(1)}, u32[]{:S(2)}, u32[]{:S(2)}) collective-permute-start(bf16[128,1024]{1,0:T(8,128)(2,1)S(1)} %get-tuple-element.51.refs_3_), channel_id=1, source_target_pairs={{0,4},{2,6},{4,0},{6,2},{1,5},{3,7},{5,1},{7,3},{8,12},{10,14},{12... | collective-permute-start | bytes 786440 | tf_op jit(solution)/shard_map/ppermute | solution.py:343
  10.0 12.2 %collective-permute-start.3 = (bf16[128,1024]{1,0:T(8,128)(2,1)S(1)}, bf16[128,1024]{1,0:T(8,128)(2,1)S(1)}, u32[]{:S(2)}, u32[]{:S(2)}) collective-permute-start(bf16[128,1024]{1,0:T(8,128)(2,1)S(1)} %get-tuple-element.52.refs_4_), channel_id=1, source_target_pairs={{0,6},{2,0},{4,2},{6,4},{1,7},{3,1},{5,3},{7,5},{8,14},{10,8},{12,... | collective-permute-start | bytes 786440 | tf_op jit(solution)/shard_map/ppermute | solution.py:343
  23.4 7.7 %collective-permute-start.4 = (f32[136,256]{1,0:T(8,128)S(1)}, f32[136,256]{1,0:T(8,128)S(1)}, u32[]{:S(2)}, u32[]{:S(2)}) collective-permute-start(f32[136,256]{1,0:T(8,128)S(1)} %get-tuple-element.60), channel_id=1, source_target_pairs={{0,8},{8,16},{16,24},{24,0},{1,9},{9,17},{17,25},{25,1},{2,10},{10... | collective-permute-start | bytes 417800 | tf_op jit(solution)/shard_map/ppermute | solution.py:343
  25.4 9.6 %collective-permute-start.5 = (f32[136,256]{1,0:T(8,128)S(1)}, f32[136,256]{1,0:T(8,128)S(1)}, u32[]{:S(2)}, u32[]{:S(2)}) collective-permute-start(f32[136,256]{1,0:T(8,128)S(1)} %get-tuple-element.61), channel_id=1, source_target_pairs={{0,16},{8,24},{16,0},{24,8},{1,17},{9,25},{17,1},{25,9},{2,18},{10... | collective-permute-start | bytes 417800 | tf_op jit(solution)/shard_map/ppermute | solution.py:343
  29.0 6.1 %collective-permute-start.6 = (f32[136,256]{1,0:T(8,128)S(1)}, f32[136,256]{1,0:T(8,128)S(1)}, u32[]{:S(2)}, u32[]{:S(2)}) collective-permute-start(f32[136,256]{1,0:T(8,128)S(1)} %get-tuple-element.62), channel_id=1, source_target_pairs={{0,24},{8,0},{16,8},{24,16},{1,25},{9,1},{17,9},{25,17},{2,26},{10... | collective-permute-start | bytes 417800 | tf_op jit(solution)/shard_map/ppermute | solution.py:343
  35.7 8.9 %collective-permute-start.9 = (f32[136,256]{1,0:T(8,128)S(1)}, f32[136,256]{1,0:T(8,128)S(1)}, u32[]{:S(2)}, u32[]{:S(2)}) collective-permute-start(f32[136,256]{1,0:T(8,128)S(1)} %get-tuple-element.63.refs_1_), channel_id=1, source_target_pairs={{0,96},{32,0},{64,32},{96,64},{1,97},{33,1},{65,33},{97,65},{2,98}... | collective-permute-start | bytes 417800 | tf_op jit(solution)/shard_map/ppermute | solution.py:343
  38.8 14.3 %collective-permute-start.13 = (bf16[144,768]{1,0:T(8,128)(2,1)S(1)}, bf16[144,768]{1,0:T(8,128)(2,1)S(1)}, u32[]{:S(2)}, u32[]{:S(2)}) collective-permute-start(bf16[144,768]{1,0:T(8,128)(2,1)S(1)} %get-tuple-element.70), channel_id=1, source_target_pairs={{0,2},{2,4},{4,6},{6,0},{1,3},{3,5},{5,7},{7,1},{8,10},{10,12},{12... | collective-permute-start | bytes 663560 | tf_op jit(solution)/shard_map/ppermute | solution.py:343
  40.0 6.9 %collective-permute-start.8 = (f32[136,256]{1,0:T(8,128)S(1)}, f32[136,256]{1,0:T(8,128)S(1)}, u32[]{:S(2)}, u32[]{:S(2)}) collective-permute-start(f32[136,256]{1,0:T(8,128)S(1)} %get-tuple-element.63.refs_1_), channel_id=1, source_target_pairs={{0,64},{32,96},{64,0},{96,32},{1,65},{33,97},{65,1},{97,33},{2,66}... | collective-permute-start | bytes 417800 | tf_op jit(solution)/shard_map/ppermute | solution.py:343
  40.6 7.5 %collective-permute-start.7 = (f32[136,256]{1,0:T(8,128)S(1)}, f32[136,256]{1,0:T(8,128)S(1)}, u32[]{:S(2)}, u32[]{:S(2)}) collective-permute-start(f32[136,256]{1,0:T(8,128)S(1)} %get-tuple-element.63.refs_1_), channel_id=1, source_target_pairs={{0,32},{32,64},{64,96},{96,0},{1,33},{33,65},{65,97},{97,1},{2,34}... | collective-permute-start | bytes 417800 | tf_op jit(solution)/shard_map/ppermute | solution.py:343
  41.6 12.4 %collective-permute-start.14 = (bf16[144,768]{1,0:T(8,128)(2,1)S(1)}, bf16[144,768]{1,0:T(8,128)(2,1)S(1)}, u32[]{:S(2)}, u32[]{:S(2)}) collective-permute-start(bf16[144,768]{1,0:T(8,128)(2,1)S(1)} %get-tuple-element.71), channel_id=1, source_target_pairs={{0,4},{2,6},{4,0},{6,2},{1,5},{3,7},{5,1},{7,3},{8,12},{10,14},{12... | collective-permute-start | bytes 663560 | tf_op jit(solution)/shard_map/ppermute | solution.py:343
  44.6 9.3 %collective-permute-start.15 = (bf16[144,768]{1,0:T(8,128)(2,1)S(1)}, bf16[144,768]{1,0:T(8,128)(2,1)S(1)}, u32[]{:S(2)}, u32[]{:S(2)}) collective-permute-start(bf16[144,768]{1,0:T(8,128)(2,1)S(1)} %get-tuple-element.72), channel_id=1, source_target_pairs={{0,6},{2,0},{4,2},{6,4},{1,7},{3,1},{5,3},{7,5},{8,14},{10,8},{12,... | collective-permute-start | bytes 663560 | tf_op jit(solution)/shard_map/ppermute | solution.py:343
  48.8 8.3 %collective-permute-start.10 = (f32[128,256]{1,0:T(8,128)S(1)}, f32[128,256]{1,0:T(8,128)S(1)}, u32[]{:S(2)}, u32[]{:S(2)}) collective-permute-start(f32[128,256]{1,0:T(8,128)S(1)} %get-tuple-element.66), channel_id=1, source_target_pairs={{0,8},{8,16},{16,24},{24,0},{1,9},{9,17},{17,25},{25,1},{2,10},{10... | collective-permute-start | bytes 393224 | tf_op jit(solution)/shard_map/ppermute | solution.py:343
  51.1 7.6 %collective-permute-start.11 = (f32[128,256]{1,0:T(8,128)S(1)}, f32[128,256]{1,0:T(8,128)S(1)}, u32[]{:S(2)}, u32[]{:S(2)}) collective-permute-start(f32[128,256]{1,0:T(8,128)S(1)} %get-tuple-element.67), channel_id=1, source_target_pairs={{0,16},{8,24},{16,0},{24,8},{1,17},{9,25},{17,1},{25,9},{2,18},{10... | collective-permute-start | bytes 393224 | tf_op jit(solution)/shard_map/ppermute | solution.py:343
  53.1 5.7 %collective-permute-start.12 = (f32[128,256]{1,0:T(8,128)S(1)}, f32[128,256]{1,0:T(8,128)S(1)}, u32[]{:S(2)}, u32[]{:S(2)}) collective-permute-start(f32[128,256]{1,0:T(8,128)S(1)} %get-tuple-element.68), channel_id=1, source_target_pairs={{0,24},{8,0},{16,8},{24,16},{1,25},{9,1},{17,9},{25,17},{2,26},{10... | collective-permute-start | bytes 393224 | tf_op jit(solution)/shard_map/ppermute | solution.py:343
  60.8 25.4 %all-to-all-start = ((f32[64,8,128]{2,1,0:T(8,128)}), f32[64,8,128]{2,1,0:T(8,128)S(1)}, u32[]{:S(2)}, u32[]{:S(2)}) async-start(f32[64,8,128]{2,1,0:T(8,128)} %get-tuple-element.89), calls=%async_computation | async-start | bytes 524288 | tf_op jit(solution)/shard_map/all_to_all | solution.py:420
  68.2 11.4 %collective-permute-start.16 = (bf16[144,768]{1,0:T(8,128)(2,1)S(1)}, bf16[144,768]{1,0:T(8,128)(2,1)S(1)}, u32[]{:S(2)}, u32[]{:S(2)}) collective-permute-start(bf16[144,768]{1,0:T(8,128)(2,1)S(1)} %get-tuple-element.83), channel_id=1, source_target_pairs={{0,2},{2,4},{4,6},{6,0},{1,3},{3,5},{5,7},{7,1},{8,10},{10,12},{12... | collective-permute-start | bytes 663560 | tf_op jit(solution)/shard_map/ppermute | solution.py:343
  69.9 12.9 %collective-permute-start.17 = (bf16[144,768]{1,0:T(8,128)(2,1)S(1)}, bf16[144,768]{1,0:T(8,128)(2,1)S(1)}, u32[]{:S(2)}, u32[]{:S(2)}) collective-permute-start(bf16[144,768]{1,0:T(8,128)(2,1)S(1)} %get-tuple-element.84), channel_id=1, source_target_pairs={{0,4},{2,6},{4,0},{6,2},{1,5},{3,7},{5,1},{7,3},{8,12},{10,14},{12... | collective-permute-start | bytes 663560 | tf_op jit(solution)/shard_map/ppermute | solution.py:343
  72.5 10.2 %collective-permute-start.18 = (bf16[144,768]{1,0:T(8,128)(2,1)S(1)}, bf16[144,768]{1,0:T(8,128)(2,1)S(1)}, u32[]{:S(2)}, u32[]{:S(2)}) collective-permute-start(bf16[144,768]{1,0:T(8,128)(2,1)S(1)} %get-tuple-element.85), channel_id=1, source_target_pairs={{0,6},{2,0},{4,2},{6,4},{1,7},{3,1},{5,3},{7,5},{8,14},{10,8},{12,... | collective-permute-start | bytes 663560 | tf_op jit(solution)/shard_map/ppermute | solution.py:343
  (2 other events, 2.7 us)

commit v2 on v1

--- a/solution.py
+++ b/solution.py
@@ -75,8 +75,7 @@
 
 
 def pack_grad(idx, g, send, keep, scr):
-    for h in range(2 * NH):
-        scr[h] = g[:, h, :]
+    scr[...] = jnp.swapaxes(g[...], 0, 1)
     c = idx[3]
     for i in range(NH):
         send[i] = scr[NH * (1 - c) + i]
@@ -85,9 +84,8 @@
 
 def pack_rows(idx, a, b, out):
     width = a.shape[-1]
-    for h in range(NH):
-        out[h, :, :width] = a[:, h, :]
-        out[h, :, width:] = b[:, h, :]
+    out[:, :, :width] = jnp.swapaxes(a[...], 0, 1)
+    out[:, :, width:] = jnp.swapaxes(b[...], 0, 1)
 
 
 def pack_pair(idx, a, b, *rest):
@@ -133,8 +131,7 @@
         kv_out[s][:TOK, :] = kv[s][...]
         for i, word in enumerate(three(total)):
             kv_out[s][TOK:, DK * i : DK * (i + 1)] = jnp.broadcast_to(word, (16, DK))
-    for h in range(NH):
-        dq_out[:, h, :] = scr[h].astype(B16)
+    dq_out[...] = jnp.swapaxes(scr[...].astype(B16), 0, 1)
 
 
 def line_cum(qa, cum_scr):
@@ -221,7 +218,7 @@
     rise[...] = SCALE * qa[:, :DK].astype(F32) * jnp.exp(cum[...])
     end = jnp.exp(last - cum[...])
     ends[...] = end
-    k_end[...] = k_out[...].astype(F32) * end
+    k_end[:, :DK], k_end[:, DK:] = split(k_out[...].astype(F32) * end)
     upper = triangle(True)
     for j in range(4):
         rows = slice(TOK * j, TOK * (j + 1))
@@ -252,7 +249,7 @@
     high, lo = split(state[...])
     reached = dot(v[...], high, NN) + dot(v[...], lo, NN)
     dk = dk_near[...] + ends[...] * reached
-    e_high, e_low = split(k_end[...])
+    e_high, e_low = k_end[:, :DK], k_end[:, DK:]
     dv = dv_near[...] + (
         dot(e_high, high, NT) + (dot(e_low, high, NT) + dot(e_high, lo, NT))
     )
@@ -261,14 +258,9 @@
     token = lax.broadcasted_iota(jnp.int32, (GROUPS, TOK), 1)
     after = (token >= (group + 1) * (TOK // GROUPS)).astype(B16)
     for j in range(4):
-        rows = slice(TOK * j, TOK * (j + 1))
-        part_high, part_low = split(kdk[rows, :])
-        ahead = three(dot(after, part_high, NN) + dot(after, part_low, NN))
-        scr[j, :TOK, :DK] = dk[rows, :].astype(B16)
-        scr[j, :TOK, DK:] = dv[rows, :].astype(B16)
-        for i in range(3):
-            scr[j, TOK:, DK * i : DK * (i + 1)] = ahead[i]
-        total[j : j + 1, :] = -jnp.sum(kdk[rows, :], axis=0, keepdims=True)
+        total[j : j + 1, :] = -jnp.sum(
+            kdk[TOK * j : TOK * (j + 1), :], axis=0, keepdims=True
+        )
     for s in range(4):
         j = (x - s + 4) % 4
         tot = (
@@ -277,11 +269,18 @@
             + kv[s][TOK : TOK + 1, 2 * DK :].astype(F32)
         )
         total[pl.ds(j, 1), :] = total[pl.ds(j, 1), :] + tot
-    for j in range(4):
-        sums[0, 2 * j : 2 * j + 1, :] = total[j : j + 1, :128]
-        sums[0, 2 * j + 1 : 2 * j + 2, :] = total[j : j + 1, 128:]
-    block = sums[0]
-    for d in range(1, 64):
+    running = jnp.zeros((1, DK), F32)
+    for j in reversed(range(4)):
+        rows = slice(TOK * j, TOK * (j + 1))
+        part_high, part_low = split(kdk[rows, :])
+        ahead = three(running - (dot(after, part_high, NN) + dot(after, part_low, NN)))
+        running = running + total[j : j + 1, :]
+        scr[j, :TOK, :DK] = dk[rows, :].astype(B16)
+        scr[j, :TOK, DK:] = dv[rows, :].astype(B16)
+        for i in range(3):
+            scr[j, TOK:, DK * i : DK * (i + 1)] = ahead[i]
+    block = jnp.concatenate([running[:, :128], running[:, 128:]], axis=0)
+    for d in range(64):
         sums[d] = block
     for s in range(4):
         outs[s][...] = scr[(x + s) % 4]
@@ -291,10 +290,9 @@
     parts = refs[0:4]
     qdq, key = refs[4:6]
     dk_out, dv_out, da_part = refs[6:9]
-    s_dk, s_dv, s_k = refs[9:12]
+    s_dk, s_dv, s_k, s_da = refs[9:13]
     x = idx[0]
-    for h in range(NH):
-        s_k[h] = key[:, h, :]
+    s_k[...] = jnp.swapaxes(key[...], 0, 1)
     row = lax.broadcasted_iota(jnp.int32, (TOK, TOK), 0)
     col = lax.broadcasted_iota(jnp.int32, (TOK, TOK), 1)
     size = TOK // GROUPS
@@ -315,28 +313,25 @@
             + dot(pick, parts[s][TOK:, DK : 2 * DK], NN)
             + dot(pick, parts[s][TOK:, 2 * DK :], NN)
         )
-        da_part[h] = (
+        s_da[h] = (
             (dot(upper, q_high, NN) + dot(upper, q_low, NN))
             - (dot(inner, k_high, NN) + dot(inner, k_low, NN))
-            - ahead
+            + ahead
         )
+    dk_out[...] = jnp.swapaxes(s_dk[...], 0, 1)
+    dv_out[...] = jnp.swapaxes(s_dv[...], 0, 1)
+    da_part[...] = jnp.swapaxes(s_da[...], 0, 1)
+
+
+def decay_part(idx, da_part, sums, da_out):
+    line = idx[2] * 4 + idx[1]
+    later = []
     for h in range(NH):
-        dk_out[:, h, :] = s_dk[h]
-        dv_out[:, h, :] = s_dv[h]
-
-
-def decay_part(idx, da_part, sums, da_out):
-    x, line = idx[0], idx[2] * 4 + idx[1]
-    segment = lax.broadcasted_iota(jnp.int32, (8, 128), 0) // 2
-    for h in range(NH):
-        acc = jnp.zeros((8, 128), F32)
-        for l in range(16):
-            counted = (l > line) | ((l == line) & (segment > x))
-            acc = acc + jnp.where(counted, sums[4 * l + h], 0.0)
-        first = acc[0:1] + acc[2:3] + acc[4:5] + acc[6:7]
-        second = acc[1:2] + acc[3:4] + acc[5:6] + acc[7:8]
-        later = jnp.concatenate([first, second], axis=1)
-        da_out[:, h, :] = (da_part[h] + later).astype(B16)
+        acc = jnp.zeros((2, 128), F32)
+        for l in range(1, 16):
+            acc = acc + jnp.where(l > line, sums[4 * l + h], 0.0)
+        later.append(jnp.concatenate([acc[0:1], acc[1:2]], axis=1))
+    da_out[...] = (da_part[...] + jnp.concatenate(later, axis=0)[None]).astype(B16)
 
 
 def shifted(value, axis, s):
@@ -400,7 +395,7 @@
         [
             sds((4 * TOK, DK), F32),
             sds((4 * TOK, DV), F32),
-            sds((4 * TOK, DK), F32),
+            sds((4 * TOK, 2 * DK)),
             sds((4 * TOK, DK), F32),
             sds((4 * TOK, DV)),
             sds((4 * TOK, DK)),
@@ -411,7 +406,7 @@
     )(idx, qa_rows, g_rows, *kv_line)
     res = call(
         far_part,
-        [sds((TOK + GROUPS, DK + DV))] * 4 + [sds((64, 8, 128), F32)],
+        [sds((TOK + GROUPS, DK + DV))] * 4 + [sds((64, 2, 128), F32)],
         14,
         [vm((DV, DK), F32), vm((4, TOK + GROUPS, DK + DV), B16), vm((4, DK), F32)],
     )(idx, *carry_in, *kv_line, *near)
@@ -420,9 +415,14 @@
     sums = lax.all_to_all(sums, SEQ, split_axis=0, concat_axis=0, tiled=True)
     dk, dv, da_part = call(
         final_part,
-        [sds((TOK, NH, DK)), sds((TOK, NH, DV)), sds((NH, TOK, DK), F32)],
+        [sds((TOK, NH, DK)), sds((TOK, NH, DV)), sds((TOK, NH, DK), F32)],
         6,
-        [vm((NH, TOK, DK), B16), vm((NH, TOK, DV), B16), vm((NH, TOK, DK), B16)],
+        [
+            vm((NH, TOK, DK), B16),
+            vm((NH, TOK, DV), B16),
+            vm((NH, TOK, DK), B16),
+            vm((NH, TOK, DK), F32),
+        ],
     )(idx, *back_in, qdq, key)
     da = call(decay_part, sds((TOK, NH, DK)), 2, ())(idx, da_part, sums)
     return dq, dk, dv, da

time: 88.4 us -> 82.6 us (0.934)
  Pallas kernels: 22.2 us -> 17.3 us
  starting transfers between devices: 41.9 us -> 40.5 us
    ppermute x18, waiting for transfers between devices: 22 us -> 15.9 us  [shifted(): return lax.ppermute(value, axis, [(i, (i + s) % 4) for i in range(4)])]
    all_to_all x1, waiting for transfers between devices: 0.01 us -> 5.84 us  [whole(): sums = lax.all_to_all(sums, SEQ, split_axis=0, concat_axis=0, tiled=True)]
    pallas_call x12, Pallas kernels: 22.2 us -> 17.3 us  [call(): return lambda *operands: run(*operands, *after)]
    all_to_all x1, starting transfers between devices: 7.39 us -> 5.32 us  [whole(): sums = lax.all_to_all(sums, SEQ, split_axis=0, concat_axis=0, tiled=True)]
  transfers between devices with their start and end apart: 20 -> 20, of which waited for: 8 -> 9; matrix products, arithmetic and copies ran while one was open for 0% -> 0% of each run, Pallas kernels for 16% -> 13%
where the time goes in v2:
time: 82.6 us; the launch traced here: 82.3 us
  starting transfers between devices  40.5 us (49%)
  waiting for transfers between devices  22.4 us (27%)
  Pallas kernels  17.3 us (21%)
  local copies, waits for them, and re-layouts  1.28 us (2%)
    ppermute x18, starting transfers between devices, shifted(): return lax.ppermute(value, axis, [(i, (i + s) % 4) for i in range(4)])  35.1 us
    pallas_call x12, Pallas kernels, call(): return lambda *operands: run(*operands, *after)  17.3 us
    ppermute x18, waiting for transfers between devices, shifted(): return lax.ppermute(value, axis, [(i, (i + s) % 4) for i in range(4)])  15.9 us
    all_to_all x1, waiting for transfers between devices, whole(): sums = lax.all_to_all(sums, SEQ, split_axis=0, concat_axis=0, tiled=True)  5.84 us
    all_to_all x1, starting transfers between devices, whole(): sums = lax.all_to_all(sums, SEQ, split_axis=0, concat_axis=0, tiled=True)  5.32 us
  transfers between devices with their start and end apart: 20, of which 9 were waited for; matrix products, arithmetic and copies ran while one was open for 0% of the time, Pallas kernels for 13%

profile of v2, /device:TPU:0, one launch (start us, length us, event | category | flops | bytes accessed | tf_op | source)
XLA Modules:
  0.0 82.3 jit_solution(6093877926916874534)
XLA Ops:
  4.7 1.7 %collective-permute-start.1 = (bf16[128,1024]{1,0:T(8,128)(2,1)S(1)}, bf16[128,1024]{1,0:T(8,128)(2,1)S(1)}, u32[]{:S(2)}, u32[]{:S(2)}) collective-permute-start(bf16[128,1024]{1,0:T(8,128)(2,1)S(1)} %get-tuple-element.50.refs_2_), channel_id=1, source_target_pairs={{0,2},{2,4},{4,6},{6,0},{1,3},{3,5},{5,7},{7,1},{8,10},{10,12},{12... | collective-permute-start | bytes 786440 | tf_op jit(solution)/shard_map/ppermute | solution.py:338
  6.4 2.7 %collective-permute-start.2 = (bf16[128,1024]{1,0:T(8,128)(2,1)S(1)}, bf16[128,1024]{1,0:T(8,128)(2,1)S(1)}, u32[]{:S(2)}, u32[]{:S(2)}) collective-permute-start(bf16[128,1024]{1,0:T(8,128)(2,1)S(1)} %get-tuple-element.51.refs_3_), channel_id=1, source_target_pairs={{0,4},{2,6},{4,0},{6,2},{1,5},{3,7},{5,1},{7,3},{8,12},{10,14},{12... | collective-permute-start | bytes 786440 | tf_op jit(solution)/shard_map/ppermute | solution.py:338
  9.1 1.4 %collective-permute-start.3 = (bf16[128,1024]{1,0:T(8,128)(2,1)S(1)}, bf16[128,1024]{1,0:T(8,128)(2,1)S(1)}, u32[]{:S(2)}, u32[]{:S(2)}) collective-permute-start(bf16[128,1024]{1,0:T(8,128)(2,1)S(1)} %get-tuple-element.52.refs_4_), channel_id=1, source_target_pairs={{0,6},{2,0},{4,2},{6,4},{1,7},{3,1},{5,3},{7,5},{8,14},{10,8},{12,... | collective-permute-start | bytes 786440 | tf_op jit(solution)/shard_map/ppermute | solution.py:338
  11.4 2.8 %shard_map.97 = (bf16[128,4,256]{2,1,0:T(4,128)(2,1)}, f32[4,128,256]{2,1,0:T(8,128)S(1)}, bf16[144,768]{1,0:T(8,128)(2,1)S(1)}, bf16[144,768]{1,0:T(8,128)(2,1)...) custom-call(s32[4]{0:T(128)S(1)} %pad_add_fusion.refs_0_, ...), custom_call_target="tpu_custom_call" | custom-call | tf_op jit(solution)/shard_map/pallas_call | solution.py:74
  14.4 6.7 %collective-permute-done.2.refs_3_ = bf16[128,1024]{1,0:T(8,128)(2,1)S(1)} collective-permute-done((bf16[128,1024]{1,0:T(8,128)(2,1)S(1)}, bf16[128,1024]{1,0:T(8,128)(2,1)S(1)}, u32[]{:S(2)}, u32[]{:S(2)}) %collective-permute-start.2) | collective-permute-done | bytes 262176 | tf_op jit(solution)/shard_map/ppermute | solution.py:338
  22.4 2.0 %collective-permute-start.4 = (f32[136,256]{1,0:T(8,128)S(1)}, f32[136,256]{1,0:T(8,128)S(1)}, u32[]{:S(2)}, u32[]{:S(2)}) collective-permute-start(f32[136,256]{1,0:T(8,128)S(1)} %get-tuple-element.60), channel_id=1, source_target_pairs={{0,8},{8,16},{16,24},{24,0},{1,9},{9,17},{17,25},{25,1},{2,10},{10... | collective-permute-start | bytes 417800 | tf_op jit(solution)/shard_map/ppermute | solution.py:338
  24.4 3.6 %collective-permute-start.5 = (f32[136,256]{1,0:T(8,128)S(1)}, f32[136,256]{1,0:T(8,128)S(1)}, u32[]{:S(2)}, u32[]{:S(2)}) collective-permute-start(f32[136,256]{1,0:T(8,128)S(1)} %get-tuple-element.61), channel_id=1, source_target_pairs={{0,16},{8,24},{16,0},{24,8},{1,17},{9,25},{17,1},{25,9},{2,18},{10... | collective-permute-start | bytes 417800 | tf_op jit(solution)/shard_map/ppermute | solution.py:338
  30.1 3.7 %collective-permute-done.5.refs_3_ = f32[136,256]{1,0:T(8,128)S(1)} collective-permute-done((f32[136,256]{1,0:T(8,128)S(1)}, f32[136,256]{1,0:T(8,128)S(1)}, u32[]{:S(2)}, u32[]{:S(2)}) %collective-permute-start.5) | collective-permute-done | bytes 139296 | tf_op jit(solution)/shard_map/ppermute | solution.py:338
  34.4 3.1 %collective-permute-start.9 = (f32[136,256]{1,0:T(8,128)S(1)}, f32[136,256]{1,0:T(8,128)S(1)}, u32[]{:S(2)}, u32[]{:S(2)}) collective-permute-start(f32[136,256]{1,0:T(8,128)S(1)} %get-tuple-element.63.refs_1_), channel_id=1, source_target_pairs={{0,96},{32,0},{64,32},{96,64},{1,97},{33,1},{65,33},{97,65},{2,98}... | collective-permute-start | bytes 417800 | tf_op jit(solution)/shard_map/ppermute | solution.py:338
  37.5 1.4 %collective-permute-start.13 = (bf16[144,768]{1,0:T(8,128)(2,1)S(1)}, bf16[144,768]{1,0:T(8,128)(2,1)S(1)}, u32[]{:S(2)}, u32[]{:S(2)}) collective-permute-start(bf16[144,768]{1,0:T(8,128)(2,1)S(1)} %get-tuple-element.70), channel_id=1, source_target_pairs={{0,2},{2,4},{4,6},{6,0},{1,3},{3,5},{5,7},{7,1},{8,10},{10,12},{12... | collective-permute-start | bytes 663560 | tf_op jit(solution)/shard_map/ppermute | solution.py:338
  40.5 3.1 %collective-permute-start.14 = (bf16[144,768]{1,0:T(8,128)(2,1)S(1)}, bf16[144,768]{1,0:T(8,128)(2,1)S(1)}, u32[]{:S(2)}, u32[]{:S(2)}) collective-permute-start(bf16[144,768]{1,0:T(8,128)(2,1)S(1)} %get-tuple-element.71), channel_id=1, source_target_pairs={{0,4},{2,6},{4,0},{6,2},{1,5},{3,7},{5,1},{7,3},{8,12},{10,14},{12... | collective-permute-start | bytes 663560 | tf_op jit(solution)/shard_map/ppermute | solution.py:338
  43.6 2.2 %collective-permute-start.15 = (bf16[144,768]{1,0:T(8,128)(2,1)S(1)}, bf16[144,768]{1,0:T(8,128)(2,1)S(1)}, u32[]{:S(2)}, u32[]{:S(2)}) collective-permute-start(bf16[144,768]{1,0:T(8,128)(2,1)S(1)} %get-tuple-element.72), channel_id=1, source_target_pairs={{0,6},{2,0},{4,2},{6,4},{1,7},{3,1},{5,3},{7,5},{8,14},{10,8},{12,... | collective-permute-start | bytes 663560 | tf_op jit(solution)/shard_map/ppermute | solution.py:338
  47.7 2.4 %collective-permute-start.10 = (f32[128,256]{1,0:T(8,128)S(1)}, f32[128,256]{1,0:T(8,128)S(1)}, u32[]{:S(2)}, u32[]{:S(2)}) collective-permute-start(f32[128,256]{1,0:T(8,128)S(1)} %get-tuple-element.66), channel_id=1, source_target_pairs={{0,8},{8,16},{16,24},{24,0},{1,9},{9,17},{17,25},{25,1},{2,10},{10... | collective-permute-start | bytes 393224 | tf_op jit(solution)/shard_map/ppermute | solution.py:338
  50.1 1.9 %collective-permute-start.11 = (f32[128,256]{1,0:T(8,128)S(1)}, f32[128,256]{1,0:T(8,128)S(1)}, u32[]{:S(2)}, u32[]{:S(2)}) collective-permute-start(f32[128,256]{1,0:T(8,128)S(1)} %get-tuple-element.67), channel_id=1, source_target_pairs={{0,16},{8,24},{16,0},{24,8},{1,17},{9,25},{17,1},{25,9},{2,18},{10... | collective-permute-start | bytes 393224 | tf_op jit(solution)/shard_map/ppermute | solution.py:338
  52.9 3.2 %shard_map.101 = (f32[512,256]{1,0:T(8,128)S(1)}, f32[512,512]{1,0:T(8,128)S(1)}, bf16[512,512]{1,0:T(8,128)(2,1)S(1)}, f32[512,256]{1,0:T(8,128)S(1)}, bf16[512...) custom-call(s32[4]{0:T(128)S(1)} %pad_add_fusion.refs_0_, bf16[512,512]{1,0:T(8,128)(2,1)S(1)} %get-tuple-element.73.refs_1_, ...), custom_call_target="tpu_custom_call" | custom-call | tf_op jit(solution)/shard_map/pallas_call | solution.py:74
  56.1 1.6 %collective-permute-done.11.refs_3_ = f32[128,256]{1,0:T(8,128)S(1)} collective-permute-done((f32[128,256]{1,0:T(8,128)S(1)}, f32[128,256]{1,0:T(8,128)S(1)}, u32[]{:S(2)}, u32[]{:S(2)}) %collective-permute-start.11) | collective-permute-done | bytes 131104 | tf_op jit(solution)/shard_map/ppermute | solution.py:338
  57.7 2.2 %shard_map.102 = (bf16[144,768]{1,0:T(8,128)(2,1)S(1)}, bf16[144,768]{1,0:T(8,128)(2,1)S(1)}, bf16[144,768]{1,0:T(8,128)(2,1)S(1)}, bf16[144,768]{1,0:T(8,128)(2,1)S(1)}, f32[64,2,128]{2,1,0:T(2,128)}) custom-call(s32[4]{0:T(128)S(1)} %pad_add_fusion.refs_0_, f32[128,256]{1,0:T(8,128)S(1)} %get-tuple-element.65.refs_1_, ...), custom_call_target="tpu_custom_call" | custom-call | tf_op jit(solution)/shard_map/pallas_call | solution.py:74
  60.3 3.4 %collective-permute-start.17 = (bf16[144,768]{1,0:T(8,128)(2,1)S(1)}, bf16[144,768]{1,0:T(8,128)(2,1)S(1)}, u32[]{:S(2)}, u32[]{:S(2)}) collective-permute-start(bf16[144,768]{1,0:T(8,128)(2,1)S(1)} %get-tuple-element.84), channel_id=1, source_target_pairs={{0,4},{2,6},{4,0},{6,2},{1,5},{3,7},{5,1},{7,3},{8,12},{10,14},{12... | collective-permute-start | bytes 663560 | tf_op jit(solution)/shard_map/ppermute | solution.py:338
  63.7 2.3 %collective-permute-start.18 = (bf16[144,768]{1,0:T(8,128)(2,1)S(1)}, bf16[144,768]{1,0:T(8,128)(2,1)S(1)}, u32[]{:S(2)}, u32[]{:S(2)}) collective-permute-start(bf16[144,768]{1,0:T(8,128)(2,1)S(1)} %get-tuple-element.85), channel_id=1, source_target_pairs={{0,6},{2,0},{4,2},{6,4},{1,7},{3,1},{5,3},{7,5},{8,14},{10,8},{12,... | collective-permute-start | bytes 663560 | tf_op jit(solution)/shard_map/ppermute | solution.py:338
  66.1 5.3 %all-to-all-start = ((f32[64,2,128]{2,1,0:T(2,128)}), f32[64,2,128]{2,1,0:T(2,128)S(1)}, u32[]{:S(2)}, u32[]{:S(2)}) async-start(f32[64,2,128]{2,1,0:T(2,128)} %get-tuple-element.89), calls=%async_computation | async-start | bytes 131072 | tf_op jit(solution)/shard_map/all_to_all | solution.py:415
  71.4 1.4 %collective-permute-done.17.refs_3_ = bf16[144,768]{1,0:T(8,128)(2,1)S(1)} collective-permute-done((bf16[144,768]{1,0:T(8,128)(2,1)S(1)}, bf16[144,768]{1,0:T(8,128)(2,1)S(1)}, u32[]{:S(2)}, u32[]{:S(2)}) %collective-permute-start.17) | collective-permute-done | bytes 221216 | tf_op jit(solution)/shard_map/ppermute | solution.py:338
  72.8 2.3 %shard_map.103 = (bf16[128,4,256]{2,1,0:T(4,128)(2,1)}, bf16[128,4,512]{2,1,0:T(4,128)(2,1)}, f32[128,4,256]{2,1,0:T(4,128)S(1)}) custom-call(s32[4]{0:T(128)S(1)} %pad_add_fusion.refs_0_, bf16[144,768]{1,0:T(8,128)(2,1)S(1)} %get-tuple-element.82.refs_1_, bf16[144,768]{1,0:T(8,128)(2,1)S(1)} %collective-permute-done.16.refs_2_, ...), custom_call_target="tpu_custom_call" | custom-call | tf_op jit(solution)/shard_map/pallas_call | solution.py:74
  75.1 5.8 %all-to-all-done.refs_2_ = f32[64,2,128]{2,1,0:T(2,128)S(1)} async-done(((f32[64,2,128]{2,1,0:T(2,128)}), f32[64,2,128]{2,1,0:T(2,128)S(1)}, u32[]{:S(2)}, u32[]{:S(2)}) %all-to-all-start) | async-done | bytes 65568 | tf_op jit(solution)/shard_map/all_to_all | solution.py:415
  81.0 1.3 %shard_map.104 = bf16[128,4,256]{2,1,0:T(4,128)(2,1)} custom-call(s32[4]{0:T(128)S(1)} %pad_add_fusion.refs_0_, f32[128,4,256]{2,1,0:T(4,128)S(1)} %get-tuple-element.88.refs_1_, f32[64,2,128]{2,1,0:T(2,128)S(1)} %all-to-all-done.refs_2_), custom_call_target="tpu_custom_call" | custom-call | tf_op jit(solution)/shard_map/pallas_call | solution.py:74
  (41 shorter events, 14.0 us)
Async XLA Ops:
  0.7 1.0 %copy-start.2 = (bf16[64,8,512]{2,1,0:T(8,128)(2,1)S(1)}, bf16[64,8,512]{2,1,0:T(8,128)(2,1)}, u32[]{:S(2)}) copy-start(bf16[64,8,512]{2,1,0:T(8,128)(2,1)} %refs_1_.4) | copy-start | bytes 1572868
  2.5 1.6 %collective-permute-start = (bf16[4,64,512]{2,1,0:T(8,128)(2,1)S(1)}, bf16[4,64,512]{2,1,0:T(8,128)(2,1)S(1)}, u32[]{:S(2)}, u32[]{:S(2)}) collective-permute-start(bf16[4,64,512]{2,1,0:T(8,128)(2,1)S(1)} %get-tuple-element.48), channel_id=1, source_target_pairs={{0,1},{1,0},{2,3},{3,2},{4,5},{5,4},{6,7},{7,6},{8,9},{9,8},{10,11... | collective-permute-start | bytes 786440 | tf_op jit(solution)/shard_map/ppermute | solution.py:357
  2.8 7.8 %copy-start.1 = (bf16[128,4,256]{2,1,0:T(4,128)(2,1)S(1)}, bf16[128,4,256]{2,1,0:T(4,128)(2,1)}, u32[]{:S(2)}) copy-start(bf16[128,4,256]{2,1,0:T(4,128)(2,1)} %refs_6_.1) | copy-start | bytes 786436
  2.8 7.8 %copy-start.3 = (bf16[128,4,512]{2,1,0:T(4,128)(2,1)S(1)}, bf16[128,4,512]{2,1,0:T(4,128)(2,1)}, u32[]{:S(2)}) copy-start(bf16[128,4,512]{2,1,0:T(4,128)(2,1)} %refs_2_.3) | copy-start | bytes 1572868
  3.5 7.9 %copy-start = (bf16[1,4,256,512]{3,2,1,0:T(8,128)(2,1)S(1)}, bf16[1,4,256,512]{3,2,1,0:T(8,128)(2,1)}, u32[]{:S(2)}) copy-start(bf16[1,4,256,512]{3,2,1,0:T(8,128)(2,1)} %refs_9_.1) | copy-start | bytes 3145732
  4.7 9.6 %collective-permute-start.1 = (bf16[128,1024]{1,0:T(8,128)(2,1)S(1)}, bf16[128,1024]{1,0:T(8,128)(2,1)S(1)}, u32[]{:S(2)}, u32[]{:S(2)}) collective-permute-start(bf16[128,1024]{1,0:T(8,128)(2,1)S(1)} %get-tuple-element.50.refs_2_), channel_id=1, source_target_pairs={{0,2},{2,4},{4,6},{6,0},{1,3},{3,5},{5,7},{7,1},{8,10},{10,12},{12... | collective-permute-start | bytes 786440 | tf_op jit(solution)/shard_map/ppermute | solution.py:338
  6.4 14.7 %collective-permute-start.2 = (bf16[128,1024]{1,0:T(8,128)(2,1)S(1)}, bf16[128,1024]{1,0:T(8,128)(2,1)S(1)}, u32[]{:S(2)}, u32[]{:S(2)}) collective-permute-start(bf16[128,1024]{1,0:T(8,128)(2,1)S(1)} %get-tuple-element.51.refs_3_), channel_id=1, source_target_pairs={{0,4},{2,6},{4,0},{6,2},{1,5},{3,7},{5,1},{7,3},{8,12},{10,14},{12... | collective-permute-start | bytes 786440 | tf_op jit(solution)/shard_map/ppermute | solution.py:338
  9.1 11.9 %collective-permute-start.3 = (bf16[128,1024]{1,0:T(8,128)(2,1)S(1)}, bf16[128,1024]{1,0:T(8,128)(2,1)S(1)}, u32[]{:S(2)}, u32[]{:S(2)}) collective-permute-start(bf16[128,1024]{1,0:T(8,128)(2,1)S(1)} %get-tuple-element.52.refs_4_), channel_id=1, source_target_pairs={{0,6},{2,0},{4,2},{6,4},{1,7},{3,1},{5,3},{7,5},{8,14},{10,8},{12,... | collective-permute-start | bytes 786440 | tf_op jit(solution)/shard_map/ppermute | solution.py:338
  22.4 7.7 %collective-permute-start.4 = (f32[136,256]{1,0:T(8,128)S(1)}, f32[136,256]{1,0:T(8,128)S(1)}, u32[]{:S(2)}, u32[]{:S(2)}) collective-permute-start(f32[136,256]{1,0:T(8,128)S(1)} %get-tuple-element.60), channel_id=1, source_target_pairs={{0,8},{8,16},{16,24},{24,0},{1,9},{9,17},{17,25},{25,1},{2,10},{10... | collective-permute-start | bytes 417800 | tf_op jit(solution)/shard_map/ppermute | solution.py:338
  24.4 9.4 %collective-permute-start.5 = (f32[136,256]{1,0:T(8,128)S(1)}, f32[136,256]{1,0:T(8,128)S(1)}, u32[]{:S(2)}, u32[]{:S(2)}) collective-permute-start(f32[136,256]{1,0:T(8,128)S(1)} %get-tuple-element.61), channel_id=1, source_target_pairs={{0,16},{8,24},{16,0},{24,8},{1,17},{9,25},{17,1},{25,9},{2,18},{10... | collective-permute-start | bytes 417800 | tf_op jit(solution)/shard_map/ppermute | solution.py:338
  27.9 5.8 %collective-permute-start.6 = (f32[136,256]{1,0:T(8,128)S(1)}, f32[136,256]{1,0:T(8,128)S(1)}, u32[]{:S(2)}, u32[]{:S(2)}) collective-permute-start(f32[136,256]{1,0:T(8,128)S(1)} %get-tuple-element.62), channel_id=1, source_target_pairs={{0,24},{8,0},{16,8},{24,16},{1,25},{9,1},{17,9},{25,17},{2,26},{10... | collective-permute-start | bytes 417800 | tf_op jit(solution)/shard_map/ppermute | solution.py:338
  34.4 9.1 %collective-permute-start.9 = (f32[136,256]{1,0:T(8,128)S(1)}, f32[136,256]{1,0:T(8,128)S(1)}, u32[]{:S(2)}, u32[]{:S(2)}) collective-permute-start(f32[136,256]{1,0:T(8,128)S(1)} %get-tuple-element.63.refs_1_), channel_id=1, source_target_pairs={{0,96},{32,0},{64,32},{96,64},{1,97},{33,1},{65,33},{97,65},{2,98}... | collective-permute-start | bytes 417800 | tf_op jit(solution)/shard_map/ppermute | solution.py:338
  37.5 14.5 %collective-permute-start.13 = (bf16[144,768]{1,0:T(8,128)(2,1)S(1)}, bf16[144,768]{1,0:T(8,128)(2,1)S(1)}, u32[]{:S(2)}, u32[]{:S(2)}) collective-permute-start(bf16[144,768]{1,0:T(8,128)(2,1)S(1)} %get-tuple-element.70), channel_id=1, source_target_pairs={{0,2},{2,4},{4,6},{6,0},{1,3},{3,5},{5,7},{7,1},{8,10},{10,12},{12... | collective-permute-start | bytes 663560 | tf_op jit(solution)/shard_map/ppermute | solution.py:338
  38.9 6.9 %collective-permute-start.8 = (f32[136,256]{1,0:T(8,128)S(1)}, f32[136,256]{1,0:T(8,128)S(1)}, u32[]{:S(2)}, u32[]{:S(2)}) collective-permute-start(f32[136,256]{1,0:T(8,128)S(1)} %get-tuple-element.63.refs_1_), channel_id=1, source_target_pairs={{0,64},{32,96},{64,0},{96,32},{1,65},{33,97},{65,1},{97,33},{2,66}... | collective-permute-start | bytes 417800 | tf_op jit(solution)/shard_map/ppermute | solution.py:338
  39.5 7.5 %collective-permute-start.7 = (f32[136,256]{1,0:T(8,128)S(1)}, f32[136,256]{1,0:T(8,128)S(1)}, u32[]{:S(2)}, u32[]{:S(2)}) collective-permute-start(f32[136,256]{1,0:T(8,128)S(1)} %get-tuple-element.63.refs_1_), channel_id=1, source_target_pairs={{0,32},{32,64},{64,96},{96,0},{1,33},{33,65},{65,97},{97,1},{2,34}... | collective-permute-start | bytes 417800 | tf_op jit(solution)/shard_map/ppermute | solution.py:338
  40.5 12.4 %collective-permute-start.14 = (bf16[144,768]{1,0:T(8,128)(2,1)S(1)}, bf16[144,768]{1,0:T(8,128)(2,1)S(1)}, u32[]{:S(2)}, u32[]{:S(2)}) collective-permute-start(bf16[144,768]{1,0:T(8,128)(2,1)S(1)} %get-tuple-element.71), channel_id=1, source_target_pairs={{0,4},{2,6},{4,0},{6,2},{1,5},{3,7},{5,1},{7,3},{8,12},{10,14},{12... | collective-permute-start | bytes 663560 | tf_op jit(solution)/shard_map/ppermute | solution.py:338
  43.6 9.3 %collective-permute-start.15 = (bf16[144,768]{1,0:T(8,128)(2,1)S(1)}, bf16[144,768]{1,0:T(8,128)(2,1)S(1)}, u32[]{:S(2)}, u32[]{:S(2)}) collective-permute-start(bf16[144,768]{1,0:T(8,128)(2,1)S(1)} %get-tuple-element.72), channel_id=1, source_target_pairs={{0,6},{2,0},{4,2},{6,4},{1,7},{3,1},{5,3},{7,5},{8,14},{10,8},{12,... | collective-permute-start | bytes 663560 | tf_op jit(solution)/shard_map/ppermute | solution.py:338
  47.7 8.4 %collective-permute-start.10 = (f32[128,256]{1,0:T(8,128)S(1)}, f32[128,256]{1,0:T(8,128)S(1)}, u32[]{:S(2)}, u32[]{:S(2)}) collective-permute-start(f32[128,256]{1,0:T(8,128)S(1)} %get-tuple-element.66), channel_id=1, source_target_pairs={{0,8},{8,16},{16,24},{24,0},{1,9},{9,17},{17,25},{25,1},{2,10},{10... | collective-permute-start | bytes 393224 | tf_op jit(solution)/shard_map/ppermute | solution.py:338
  50.1 7.6 %collective-permute-start.11 = (f32[128,256]{1,0:T(8,128)S(1)}, f32[128,256]{1,0:T(8,128)S(1)}, u32[]{:S(2)}, u32[]{:S(2)}) collective-permute-start(f32[128,256]{1,0:T(8,128)S(1)} %get-tuple-element.67), channel_id=1, source_target_pairs={{0,16},{8,24},{16,0},{24,8},{1,17},{9,25},{17,1},{25,9},{2,18},{10... | collective-permute-start | bytes 393224 | tf_op jit(solution)/shard_map/ppermute | solution.py:338
  52.0 5.7 %collective-permute-start.12 = (f32[128,256]{1,0:T(8,128)S(1)}, f32[128,256]{1,0:T(8,128)S(1)}, u32[]{:S(2)}, u32[]{:S(2)}) collective-permute-start(f32[128,256]{1,0:T(8,128)S(1)} %get-tuple-element.68), channel_id=1, source_target_pairs={{0,24},{8,0},{16,8},{24,16},{1,25},{9,1},{17,9},{25,17},{2,26},{10... | collective-permute-start | bytes 393224 | tf_op jit(solution)/shard_map/ppermute | solution.py:338
  59.9 11.5 %collective-permute-start.16 = (bf16[144,768]{1,0:T(8,128)(2,1)S(1)}, bf16[144,768]{1,0:T(8,128)(2,1)S(1)}, u32[]{:S(2)}, u32[]{:S(2)}) collective-permute-start(bf16[144,768]{1,0:T(8,128)(2,1)S(1)} %get-tuple-element.83), channel_id=1, source_target_pairs={{0,2},{2,4},{4,6},{6,0},{1,3},{3,5},{5,7},{7,1},{8,10},{10,12},{12... | collective-permute-start | bytes 663560 | tf_op jit(solution)/shard_map/ppermute | solution.py:338
  60.3 12.5 %collective-permute-start.17 = (bf16[144,768]{1,0:T(8,128)(2,1)S(1)}, bf16[144,768]{1,0:T(8,128)(2,1)S(1)}, u32[]{:S(2)}, u32[]{:S(2)}) collective-permute-start(bf16[144,768]{1,0:T(8,128)(2,1)S(1)} %get-tuple-element.84), channel_id=1, source_target_pairs={{0,4},{2,6},{4,0},{6,2},{1,5},{3,7},{5,1},{7,3},{8,12},{10,14},{12... | collective-permute-start | bytes 663560 | tf_op jit(solution)/shard_map/ppermute | solution.py:338
  63.7 9.1 %collective-permute-start.18 = (bf16[144,768]{1,0:T(8,128)(2,1)S(1)}, bf16[144,768]{1,0:T(8,128)(2,1)S(1)}, u32[]{:S(2)}, u32[]{:S(2)}) collective-permute-start(bf16[144,768]{1,0:T(8,128)(2,1)S(1)} %get-tuple-element.85), channel_id=1, source_target_pairs={{0,6},{2,0},{4,2},{6,4},{1,7},{3,1},{5,3},{7,5},{8,14},{10,8},{12,... | collective-permute-start | bytes 663560 | tf_op jit(solution)/shard_map/ppermute | solution.py:338
  66.1 14.9 %all-to-all-start = ((f32[64,2,128]{2,1,0:T(2,128)}), f32[64,2,128]{2,1,0:T(2,128)S(1)}, u32[]{:S(2)}, u32[]{:S(2)}) async-start(f32[64,2,128]{2,1,0:T(2,128)} %get-tuple-element.89), calls=%async_computation | async-start | bytes 131072 | tf_op jit(solution)/shard_map/all_to_all | solution.py:415
  (2 other events, 2.0 us)

commit v3 on v2

--- a/solution.py
+++ b/solution.py
@@ -74,15 +74,30 @@
     return lambda *operands: run(*operands, *after)
 
 
-def pack_grad(idx, g, send, keep, scr):
-    scr[...] = jnp.swapaxes(g[...], 0, 1)
-    c = idx[3]
+def pack_first(idx, grad, query, decay, *refs):
+    outs, send, keep = refs[0:4], refs[4], refs[5]
+    g, q, a, heads, scr, sems = refs[6:12]
+    copies = [
+        pltpu.make_async_copy(source, target, sems.at[i])
+        for i, (source, target) in enumerate(((grad, g), (query, q), (decay, a)))
+    ]
+    for copy in copies:
+        copy.start()
+    x, c = idx[0], idx[3]
+    copies[0].wait()
+    heads[...] = jnp.swapaxes(g[...], 0, 1)
     for i in range(NH):
-        send[i] = scr[NH * (1 - c) + i]
-        keep[i] = scr[NH * c + i]
-
-
-def pack_rows(idx, a, b, out):
+        send[i] = heads[NH * (1 - c) + i]
+        keep[i] = heads[NH * c + i]
+    copies[1].wait()
+    scr[:, :, :DK] = jnp.swapaxes(q[...], 0, 1)
+    copies[2].wait()
+    scr[:, :, DK:] = jnp.swapaxes(a[...], 0, 1)
+    for s in range(4):
+        outs[s][...] = scr[(x + s) % 4]
+
+
+def pack_rows(a, b, out):
     width = a.shape[-1]
     out[:, :, :width] = jnp.swapaxes(a[...], 0, 1)
     out[:, :, width:] = jnp.swapaxes(b[...], 0, 1)
@@ -90,37 +105,36 @@
 
 def pack_pair(idx, a, b, *rest):
     outs, scr = rest[:4], rest[4]
-    pack_rows(idx, a, b, scr)
+    pack_rows(a, b, scr)
     for s in range(4):
         outs[s][...] = scr[(idx[0] + s) % 4]
 
 
-def join_all(idx, qa, keep, recv, *outs):
+def join_grad(idx, keep, recv, *outs):
     c = idx[3]
     half = TOK // 2
     mine = pl.ds(pl.multiple_of(half * c, half), half)
     theirs = pl.ds(pl.multiple_of(half * (1 - c), half), half)
     for s in range(4):
         h = (idx[0] + s) % 4
-        outs[s][:, : 2 * DK] = qa[h]
-        outs[s][mine, 2 * DK :] = keep[h]
-        outs[s][theirs, 2 * DK :] = recv[h]
+        outs[s][mine, :] = keep[h]
+        outs[s][theirs, :] = recv[h]
 
 
 def query_part(idx, *refs):
-    qag, kv = refs[0:4], refs[4:8]
-    check = refs[8]
-    dq_out, qdq_out = refs[9:11]
-    kv_out = refs[11:15]
-    scr = refs[15]
+    qa, gr, kv = refs[0:4], refs[4:8], refs[8:12]
+    check = refs[12]
+    dq_out, qdq_out = refs[13:15]
+    kv_out = refs[15:19]
+    scr = refs[19]
     low = triangle(False)
     tri = low.astype(B16)
     for s in range(4):
         h = (idx[0] + s) % 4
-        q = qag[s][:, :DK].astype(F32)
-        cum = dot(tri, qag[s][:, DK : 2 * DK], NN)
+        q = qa[s][:, :DK].astype(F32)
+        cum = dot(tri, qa[s][:, DK:], NN)
         k = kv[s][:, :DK].astype(F32)
-        g = qag[s][:, 2 * DK :]
+        g = gr[s][...]
         scores = jnp.where(low, dot(g, kv[s][:, DK:], NT), 0.0)
         reached = dot(g, check[0, h], NT) + dot3(scores, k * jnp.exp(-cum), NN)
         dq = SCALE * jnp.exp(cum) * reached
@@ -146,16 +160,16 @@
 
 
 def line_state(idx, *refs):
-    qag = refs[0:4]
-    chunks = refs[4:8]
-    qa_out, g_out = refs[8:10]
-    acc, cum_scr = refs[10:12]
+    qa, gr = refs[0:4], refs[4:8]
+    chunks = refs[8:12]
+    qa_out, g_out = refs[12:14]
+    acc, cum_scr = refs[14:16]
     x, z = idx[0], idx[1]
     for s in range(4):
         j = (x - s + 4) % 4
         rows = pl.ds(pl.multiple_of(TOK * j, TOK), TOK)
-        qa_out[rows, :] = qag[s][:, : 2 * DK]
-        g_out[rows, :] = qag[s][:, 2 * DK :]
+        qa_out[rows, :] = qa[s][...]
+        g_out[rows, :] = gr[s][...]
     base = line_cum(qa_out, cum_scr)
     rise = qa_out[:, :DK].astype(F32) * jnp.exp(cum_scr[...])
     high, lo = split(SCALE * rise)
@@ -351,31 +365,44 @@
     vm = pltpu.VMEM
 
     half = TOK // 2
-    send, keep = call(
-        pack_grad, [sds((NH, half, DV))] * 2, 1, [vm((2 * NH, half, DV), B16)]
-    )(idx, out_grad)
+    hbm = pl.BlockSpec(memory_space=pltpu.HBM)
+    *qa, send, keep = pl.pallas_call(
+        pack_first,
+        out_shape=[sds((TOK, 2 * DK))] * 4 + [sds((NH, half, DV))] * 2,
+        in_specs=[pl.BlockSpec(memory_space=pltpu.SMEM), hbm, hbm, hbm],
+        scratch_shapes=[
+            vm((half, 2 * NH, DV), B16),
+            vm((TOK, NH, DK), B16),
+            vm((TOK, NH, DK), B16),
+            vm((2 * NH, half, DV), B16),
+            vm((NH, TOK, 2 * DK), B16),
+            pltpu.SemaphoreType.DMA((3,)),
+        ],
+        name="pack_first",
+        compiler_params=pltpu.CompilerParams(vmem_limit_bytes=16 * 1024 * 1024),
+    )(idx, *(pltpu.with_memory_space_constraint(a, pltpu.HBM) for a in (out_grad, query, log_decay)))
     recv = lax.ppermute(send, H, [(0, 1), (1, 0)])
-    qa = call(pack_rows, sds((NH, TOK, 2 * DK)), 2, ())(idx, query, log_decay)
-    qag = call(join_all, [sds((TOK, 2 * DK + DV))] * 4, 3, ())(idx, qa, keep, recv)
-    qag_line = spread(qag, X)
+    qa_line = spread(qa, X)
+    g = call(join_grad, [sds((TOK, DV))] * 4, 2, ())(idx, keep, recv)
+    g_line = spread(g, X)
     kv = call(
         pack_pair, [sds((TOK, DK + DV))] * 4, 2, [vm((NH, TOK, DK + DV), B16)]
     )(idx, key, value)
     res = call(
         query_part,
         [sds((TOK, NH, DK)), sds((NH, TOK, DK), F32)] + [sds((TOK + 16, DK + DV))] * 4,
-        9,
+        13,
         [vm((NH, TOK, DK), F32)],
-    )(idx, *qag, *kv, checkpoints)
+    )(idx, *qa, *g, *kv, checkpoints)
     dq, qdq, kv = res[0], res[1], res[2:]
     res = call(
         line_state,
         [sds((TOK + 8, DK), F32)] * 4
         + [sds((4 * TOK, 2 * DK)), sds((4 * TOK, DV))],
-        4,
+        8,
         [vm((DV, DK), F32), vm((4 * TOK, DK), F32)],
         (qdq,),
-    )(idx, *qag_line)
+    )(idx, *qa_line, *g_line)
     chunks, qa_rows, g_rows = res[:4], res[4], res[5]
     z_in = spread(chunks, Z)
     kv_line = spread(kv, X)

time: 82.6 us -> 79.9 us (0.967)
  waiting for transfers between devices: 22.4 us -> 17.6 us
  starting transfers between devices: 40.5 us -> 42.3 us
    ppermute x18 -> x21, waiting for transfers between devices: 15.9 us -> 12.3 us  [shifted(): return lax.ppermute(value, axis, [(i, (i + s) % 4) for i in range(4)])]
    ppermute x18 -> x21, starting transfers between devices: 35.1 us -> 37.4 us  [shifted(): return lax.ppermute(value, axis, [(i, (i + s) % 4) for i in range(4)])]
    pallas_call x0 -> x1, Pallas kernels: none -> 1.97 us  [whole(): pl.pallas_call(pack_first, out_shape=[sds((TOK, 2 * DK))] * 4 + [sds((NH,...]
    pallas_call x12 -> x10, Pallas kernels: 17.3 us -> 15.9 us  [call(): return lambda *operands: run(*operands, *after)]
  transfers between devices with their start and end apart: 20 -> 23, of which waited for: 9 -> 9; matrix products, arithmetic and copies ran while one was open for 0% -> 0% of each run, Pallas kernels for 13% -> 13%
where the time goes in v3:
time: 79.9 us; the launch traced here: 79.7 us
  starting transfers between devices  42.3 us (53%)
  Pallas kernels  17.9 us (22%)
  waiting for transfers between devices  17.6 us (22%)
  local copies, waits for them, and re-layouts  1.05 us (1%)
    ppermute x21, starting transfers between devices, shifted(): return lax.ppermute(value, axis, [(i, (i + s) % 4) for i in range(4)])  37.4 us
    pallas_call x10, Pallas kernels, call(): return lambda *operands: run(*operands, *after)  15.9 us
    ppermute x21, waiting for transfers between devices, shifted(): return lax.ppermute(value, axis, [(i, (i + s) % 4) for i in range(4)])  12.3 us
    all_to_all x1, waiting for transfers between devices, whole(): sums = lax.all_to_all(sums, SEQ, split_axis=0, concat_axis=0, tiled=True)  5.28 us
    all_to_all x1, starting transfers between devices, whole(): sums = lax.all_to_all(sums, SEQ, split_axis=0, concat_axis=0, tiled=True)  4.83 us
    pallas_call x1, Pallas kernels, whole(): pl.pallas_call(pack_first, out_shape=[sds((TOK, 2 * DK))] * 4 + [sds((NH,...  1.97 us
  transfers between devices with their start and end apart: 23, of which 9 were waited for; matrix products, arithmetic and copies ran while one was open for 0% of the time, Pallas kernels for 13%

profile of v3, /device:TPU:0, one launch (start us, length us, event | category | flops | bytes accessed | tf_op | source)
XLA Modules:
  0.0 79.7 jit_solution(3591913990746201818)
XLA Ops:
  0.7 2.0 %pack_first.1 = (bf16[128,512]{1,0:T(8,128)(2,1)S(1)}, bf16[128,512]{1,0:T(8,128)(2,1)S(1)}, bf16[128,512]{1,0:T(8,128)(2,1)S(1)}, bf16[128,512]{1,0:T(8,128)(2,...) custom-call(s32[4]{0:T(128)S(1)} %pad_add_fusion.idx.refs_0_, bf16[64,8,512]{2,1,0:T(8,128)(2,1)} %grad.1, ...), custom_call_target="tpu_custom_call" | custom-call | tf_op jit(solution)/shard_map/pack_first/pallas_call | solution.py:369
  2.8 1.7 %collective-permute-start.1 = (bf16[128,512]{1,0:T(8,128)(2,1)S(1)}, bf16[128,512]{1,0:T(8,128)(2,1)S(1)}, u32[]{:S(2)}, u32[]{:S(2)}) collective-permute-start(bf16[128,512]{1,0:T(8,128)(2,1)S(1)} %get-tuple-element.52.refs_2_), channel_id=1, source_target_pairs={{0,2},{2,4},{4,6},{6,0},{1,3},{3,5},{5,7},{7,1},{8,10},{10,12},{12... | collective-permute-start | bytes 393224 | tf_op jit(solution)/shard_map/ppermute | solution.py:352
  4.5 2.7 %collective-permute-start.2 = (bf16[128,512]{1,0:T(8,128)(2,1)S(1)}, bf16[128,512]{1,0:T(8,128)(2,1)S(1)}, u32[]{:S(2)}, u32[]{:S(2)}) collective-permute-start(bf16[128,512]{1,0:T(8,128)(2,1)S(1)} %get-tuple-element.53.refs_3_), channel_id=1, source_target_pairs={{0,4},{2,6},{4,0},{6,2},{1,5},{3,7},{5,1},{7,3},{8,12},{10,14},{12... | collective-permute-start | bytes 393224 | tf_op jit(solution)/shard_map/ppermute | solution.py:352
  7.2 1.4 %collective-permute-start.3 = (bf16[128,512]{1,0:T(8,128)(2,1)S(1)}, bf16[128,512]{1,0:T(8,128)(2,1)S(1)}, u32[]{:S(2)}, u32[]{:S(2)}) collective-permute-start(bf16[128,512]{1,0:T(8,128)(2,1)S(1)} %get-tuple-element.54.refs_4_), channel_id=1, source_target_pairs={{0,6},{2,0},{4,2},{6,4},{1,7},{3,1},{5,3},{7,5},{8,14},{10,8},{12,... | collective-permute-start | bytes 393224 | tf_op jit(solution)/shard_map/ppermute | solution.py:352
  10.8 1.9 %collective-permute-start.6 = (bf16[128,512]{1,0:T(8,128)(2,1)S(1)}, bf16[128,512]{1,0:T(8,128)(2,1)S(1)}, u32[]{:S(2)}, u32[]{:S(2)}) collective-permute-start(bf16[128,512]{1,0:T(8,128)(2,1)S(1)} %get-tuple-element.60.refs_8_), channel_id=1, source_target_pairs={{0,6},{2,0},{4,2},{6,4},{1,7},{3,1},{5,3},{7,5},{8,14},{10,8},{12,... | collective-permute-start | bytes 393224 | tf_op jit(solution)/shard_map/ppermute | solution.py:352
  14.5 2.8 %shard_map.95 = (bf16[128,4,256]{2,1,0:T(4,128)(2,1)}, f32[4,128,256]{2,1,0:T(8,128)S(1)}, bf16[144,768]{1,0:T(8,128)(2,1)S(1)}, bf16[144,768]{1,0:T(8,128)(2,1)...) custom-call(s32[4]{0:T(128)S(1)} %pad_add_fusion.idx.refs_0_, ...), custom_call_target="tpu_custom_call" | custom-call | tf_op jit(solution)/shard_map/pallas_call | solution.py:74
  17.4 2.1 %collective-permute-done.5.refs_7_ = bf16[128,512]{1,0:T(8,128)(2,1)S(1)} collective-permute-done((bf16[128,512]{1,0:T(8,128)(2,1)S(1)}, bf16[128,512]{1,0:T(8,128)(2,1)S(1)}, u32[]{:S(2)}, u32[]{:S(2)}) %collective-permute-start.5) | collective-permute-done | bytes 131104 | tf_op jit(solution)/shard_map/ppermute | solution.py:352
  20.7 2.0 %collective-permute-start.7 = (f32[136,256]{1,0:T(8,128)S(1)}, f32[136,256]{1,0:T(8,128)S(1)}, u32[]{:S(2)}, u32[]{:S(2)}) collective-permute-start(f32[136,256]{1,0:T(8,128)S(1)} %get-tuple-element.68), channel_id=1, source_target_pairs={{0,8},{8,16},{16,24},{24,0},{1,9},{9,17},{17,25},{25,1},{2,10},{10... | collective-permute-start | bytes 417800 | tf_op jit(solution)/shard_map/ppermute | solution.py:352
  22.7 3.6 %collective-permute-start.8 = (f32[136,256]{1,0:T(8,128)S(1)}, f32[136,256]{1,0:T(8,128)S(1)}, u32[]{:S(2)}, u32[]{:S(2)}) collective-permute-start(f32[136,256]{1,0:T(8,128)S(1)} %get-tuple-element.69), channel_id=1, source_target_pairs={{0,16},{8,24},{16,0},{24,8},{1,17},{9,25},{17,1},{25,9},{2,18},{10... | collective-permute-start | bytes 417800 | tf_op jit(solution)/shard_map/ppermute | solution.py:352
  28.4 3.9 %collective-permute-done.8.refs_3_ = f32[136,256]{1,0:T(8,128)S(1)} collective-permute-done((f32[136,256]{1,0:T(8,128)S(1)}, f32[136,256]{1,0:T(8,128)S(1)}, u32[]{:S(2)}, u32[]{:S(2)}) %collective-permute-start.8) | collective-permute-done | bytes 139296 | tf_op jit(solution)/shard_map/ppermute | solution.py:352
  33.0 3.1 %collective-permute-start.12 = (f32[136,256]{1,0:T(8,128)S(1)}, f32[136,256]{1,0:T(8,128)S(1)}, u32[]{:S(2)}, u32[]{:S(2)}) collective-permute-start(f32[136,256]{1,0:T(8,128)S(1)} %get-tuple-element.71.refs_1_), channel_id=1, source_target_pairs={{0,96},{32,0},{64,32},{96,64},{1,97},{33,1},{65,33},{97,65},{2,98}... | collective-permute-start | bytes 417800 | tf_op jit(solution)/shard_map/ppermute | solution.py:352
  38.8 2.9 %collective-permute-start.17 = (bf16[144,768]{1,0:T(8,128)(2,1)S(1)}, bf16[144,768]{1,0:T(8,128)(2,1)S(1)}, u32[]{:S(2)}, u32[]{:S(2)}) collective-permute-start(bf16[144,768]{1,0:T(8,128)(2,1)S(1)} %get-tuple-element.79), channel_id=1, source_target_pairs={{0,4},{2,6},{4,0},{6,2},{1,5},{3,7},{5,1},{7,3},{8,12},{10,14},{12... | collective-permute-start | bytes 663560 | tf_op jit(solution)/shard_map/ppermute | solution.py:352
  41.7 2.0 %collective-permute-start.18 = (bf16[144,768]{1,0:T(8,128)(2,1)S(1)}, bf16[144,768]{1,0:T(8,128)(2,1)S(1)}, u32[]{:S(2)}, u32[]{:S(2)}) collective-permute-start(bf16[144,768]{1,0:T(8,128)(2,1)S(1)} %get-tuple-element.80), channel_id=1, source_target_pairs={{0,6},{2,0},{4,2},{6,4},{1,7},{3,1},{5,3},{7,5},{8,14},{10,8},{12,... | collective-permute-start | bytes 663560 | tf_op jit(solution)/shard_map/ppermute | solution.py:352
  46.0 2.4 %collective-permute-start.13 = (f32[128,256]{1,0:T(8,128)S(1)}, f32[128,256]{1,0:T(8,128)S(1)}, u32[]{:S(2)}, u32[]{:S(2)}) collective-permute-start(f32[128,256]{1,0:T(8,128)S(1)} %get-tuple-element.74), channel_id=1, source_target_pairs={{0,8},{8,16},{16,24},{24,0},{1,9},{9,17},{17,25},{25,1},{2,10},{10... | collective-permute-start | bytes 393224 | tf_op jit(solution)/shard_map/ppermute | solution.py:352
  48.4 1.8 %collective-permute-start.14 = (f32[128,256]{1,0:T(8,128)S(1)}, f32[128,256]{1,0:T(8,128)S(1)}, u32[]{:S(2)}, u32[]{:S(2)}) collective-permute-start(f32[128,256]{1,0:T(8,128)S(1)} %get-tuple-element.75), channel_id=1, source_target_pairs={{0,16},{8,24},{16,0},{24,8},{1,17},{9,25},{17,1},{25,9},{2,18},{10... | collective-permute-start | bytes 393224 | tf_op jit(solution)/shard_map/ppermute | solution.py:352
  51.1 3.2 %shard_map.99 = (f32[512,256]{1,0:T(8,128)S(1)}, f32[512,512]{1,0:T(8,128)S(1)}, bf16[512,512]{1,0:T(8,128)(2,1)S(1)}, f32[512,256]{1,0:T(8,128)S(1)}, bf16[512,...) custom-call(s32[4]{0:T(128)S(1)} %pad_add_fusion.idx.refs_0_, bf16[512,512]{1,0:T(8,128)(2,1)S(1)} %get-tuple-element.81.refs_1_, ...), custom_call_target="tpu_custom_call" | custom-call | tf_op jit(solution)/shard_map/pallas_call | solution.py:74
  54.4 1.5 %collective-permute-done.14.refs_3_ = f32[128,256]{1,0:T(8,128)S(1)} collective-permute-done((f32[128,256]{1,0:T(8,128)S(1)}, f32[128,256]{1,0:T(8,128)S(1)}, u32[]{:S(2)}, u32[]{:S(2)}) %collective-permute-start.14) | collective-permute-done | bytes 131104 | tf_op jit(solution)/shard_map/ppermute | solution.py:352
  56.0 2.2 %shard_map.100 = (bf16[144,768]{1,0:T(8,128)(2,1)S(1)}, bf16[144,768]{1,0:T(8,128)(2,1)S(1)}, bf16[144,768]{1,0:T(8,128)(2,1)S(1)}, bf16[144,768]{1,0:T(8,128)(2,1)S(1)}, f32[64,2,128]{2,1,0:T(2,128)}) custom-call(s32[4]{0:T(128)S(1)} %pad_add_fusion.idx.refs_0_, f32[128,256]{1,0:T(8,128)S(1)} %get-tuple-element.73.refs_1_, ...), custom_call_target="tpu_custom_call" | custom-call | tf_op jit(solution)/shard_map/pallas_call | solution.py:74
  59.5 2.3 %collective-permute-start.20 = (bf16[144,768]{1,0:T(8,128)(2,1)S(1)}, bf16[144,768]{1,0:T(8,128)(2,1)S(1)}, u32[]{:S(2)}, u32[]{:S(2)}) collective-permute-start(bf16[144,768]{1,0:T(8,128)(2,1)S(1)} %get-tuple-element.92), channel_id=1, source_target_pairs={{0,4},{2,6},{4,0},{6,2},{1,5},{3,7},{5,1},{7,3},{8,12},{10,14},{12... | collective-permute-start | bytes 663560 | tf_op jit(solution)/shard_map/ppermute | solution.py:352
  61.8 2.1 %collective-permute-start.21 = (bf16[144,768]{1,0:T(8,128)(2,1)S(1)}, bf16[144,768]{1,0:T(8,128)(2,1)S(1)}, u32[]{:S(2)}, u32[]{:S(2)}) collective-permute-start(bf16[144,768]{1,0:T(8,128)(2,1)S(1)} %get-tuple-element.93), channel_id=1, source_target_pairs={{0,6},{2,0},{4,2},{6,4},{1,7},{3,1},{5,3},{7,5},{8,14},{10,8},{12,... | collective-permute-start | bytes 663560 | tf_op jit(solution)/shard_map/ppermute | solution.py:352
  63.9 4.8 %all-to-all-start = ((f32[64,2,128]{2,1,0:T(2,128)}), f32[64,2,128]{2,1,0:T(2,128)S(1)}, u32[]{:S(2)}, u32[]{:S(2)}) async-start(f32[64,2,128]{2,1,0:T(2,128)} %get-tuple-element.97), calls=%async_computation | async-start | bytes 131072 | tf_op jit(solution)/shard_map/all_to_all | solution.py:442
  68.8 1.7 %collective-permute-done.20.refs_3_ = bf16[144,768]{1,0:T(8,128)(2,1)S(1)} collective-permute-done((bf16[144,768]{1,0:T(8,128)(2,1)S(1)}, bf16[144,768]{1,0:T(8,128)(2,1)S(1)}, u32[]{:S(2)}, u32[]{:S(2)}) %collective-permute-start.20) | collective-permute-done | bytes 221216 | tf_op jit(solution)/shard_map/ppermute | solution.py:352
  70.8 2.3 %shard_map.101 = (bf16[128,4,256]{2,1,0:T(4,128)(2,1)}, bf16[128,4,512]{2,1,0:T(4,128)(2,1)}, f32[128,4,256]{2,1,0:T(4,128)S(1)}) custom-call(s32[4]{0:T(128)S(1)} %pad_add_fusion.idx.refs_0_, bf16[144,768]{1,0:T(8,128)(2,1)S(1)} %get-tuple-element.90.refs_1_, bf16[144,768]{1,0:T(8,128)(2,1)S(1)} %collective-permute-done.19.refs_2_, ...), custom_call_target="tpu_custom_call" | custom-call | tf_op jit(solution)/shard_map/pallas_call | solution.py:74
  73.1 5.3 %all-to-all-done.refs_2_ = f32[64,2,128]{2,1,0:T(2,128)S(1)} async-done(((f32[64,2,128]{2,1,0:T(2,128)}), f32[64,2,128]{2,1,0:T(2,128)S(1)}, u32[]{:S(2)}, u32[]{:S(2)}) %all-to-all-start) | async-done | bytes 65568 | tf_op jit(solution)/shard_map/all_to_all | solution.py:442
  (40 shorter events, 17.1 us)
Async XLA Ops:
  0.7 13.8 %copy-start = (bf16[1,4,256,512]{3,2,1,0:T(8,128)(2,1)S(1)}, bf16[1,4,256,512]{3,2,1,0:T(8,128)(2,1)}, u32[]{:S(2)}) copy-start(bf16[1,4,256,512]{3,2,1,0:T(8,128)(2,1)} %refs_13_.1) | copy-start | bytes 3145732
  2.7 5.9 %collective-permute-start = (bf16[4,64,512]{2,1,0:T(8,128)(2,1)S(1)}, bf16[4,64,512]{2,1,0:T(8,128)(2,1)S(1)}, u32[]{:S(2)}, u32[]{:S(2)}) collective-permute-start(bf16[4,64,512]{2,1,0:T(8,128)(2,1)S(1)} %get-tuple-element.56), channel_id=1, source_target_pairs={{0,1},{1,0},{2,3},{3,2},{4,5},{5,4},{6,7},{7,6},{8,9},{9,8},{10,11... | collective-permute-start | bytes 786440 | tf_op jit(solution)/shard_map/ppermute | solution.py:384
  2.8 8.0 %collective-permute-start.1 = (bf16[128,512]{1,0:T(8,128)(2,1)S(1)}, bf16[128,512]{1,0:T(8,128)(2,1)S(1)}, u32[]{:S(2)}, u32[]{:S(2)}) collective-permute-start(bf16[128,512]{1,0:T(8,128)(2,1)S(1)} %get-tuple-element.52.refs_2_), channel_id=1, source_target_pairs={{0,2},{2,4},{4,6},{6,0},{1,3},{3,5},{5,7},{7,1},{8,10},{10,12},{12... | collective-permute-start | bytes 393224 | tf_op jit(solution)/shard_map/ppermute | solution.py:352
  4.5 12.9 %collective-permute-start.2 = (bf16[128,512]{1,0:T(8,128)(2,1)S(1)}, bf16[128,512]{1,0:T(8,128)(2,1)S(1)}, u32[]{:S(2)}, u32[]{:S(2)}) collective-permute-start(bf16[128,512]{1,0:T(8,128)(2,1)S(1)} %get-tuple-element.53.refs_3_), channel_id=1, source_target_pairs={{0,4},{2,6},{4,0},{6,2},{1,5},{3,7},{5,1},{7,3},{8,12},{10,14},{12... | collective-permute-start | bytes 393224 | tf_op jit(solution)/shard_map/ppermute | solution.py:352
  7.2 10.2 %collective-permute-start.3 = (bf16[128,512]{1,0:T(8,128)(2,1)S(1)}, bf16[128,512]{1,0:T(8,128)(2,1)S(1)}, u32[]{:S(2)}, u32[]{:S(2)}) collective-permute-start(bf16[128,512]{1,0:T(8,128)(2,1)S(1)} %get-tuple-element.54.refs_4_), channel_id=1, source_target_pairs={{0,6},{2,0},{4,2},{6,4},{1,7},{3,1},{5,3},{7,5},{8,14},{10,8},{12,... | collective-permute-start | bytes 393224 | tf_op jit(solution)/shard_map/ppermute | solution.py:352
  9.2 8.1 %collective-permute-start.4 = (bf16[128,512]{1,0:T(8,128)(2,1)S(1)}, bf16[128,512]{1,0:T(8,128)(2,1)S(1)}, u32[]{:S(2)}, u32[]{:S(2)}) collective-permute-start(bf16[128,512]{1,0:T(8,128)(2,1)S(1)} %get-tuple-element.58.refs_6_), channel_id=1, source_target_pairs={{0,2},{2,4},{4,6},{6,0},{1,3},{3,5},{5,7},{7,1},{8,10},{10,12},{12... | collective-permute-start | bytes 393224 | tf_op jit(solution)/shard_map/ppermute | solution.py:352
  9.9 9.5 %collective-permute-start.5 = (bf16[128,512]{1,0:T(8,128)(2,1)S(1)}, bf16[128,512]{1,0:T(8,128)(2,1)S(1)}, u32[]{:S(2)}, u32[]{:S(2)}) collective-permute-start(bf16[128,512]{1,0:T(8,128)(2,1)S(1)} %get-tuple-element.59.refs_7_), channel_id=1, source_target_pairs={{0,4},{2,6},{4,0},{6,2},{1,5},{3,7},{5,1},{7,3},{8,12},{10,14},{12... | collective-permute-start | bytes 393224 | tf_op jit(solution)/shard_map/ppermute | solution.py:352
  10.8 8.7 %collective-permute-start.6 = (bf16[128,512]{1,0:T(8,128)(2,1)S(1)}, bf16[128,512]{1,0:T(8,128)(2,1)S(1)}, u32[]{:S(2)}, u32[]{:S(2)}) collective-permute-start(bf16[128,512]{1,0:T(8,128)(2,1)S(1)} %get-tuple-element.60.refs_8_), channel_id=1, source_target_pairs={{0,6},{2,0},{4,2},{6,4},{1,7},{3,1},{5,3},{7,5},{8,14},{10,8},{12,... | collective-permute-start | bytes 393224 | tf_op jit(solution)/shard_map/ppermute | solution.py:352
  20.7 7.7 %collective-permute-start.7 = (f32[136,256]{1,0:T(8,128)S(1)}, f32[136,256]{1,0:T(8,128)S(1)}, u32[]{:S(2)}, u32[]{:S(2)}) collective-permute-start(f32[136,256]{1,0:T(8,128)S(1)} %get-tuple-element.68), channel_id=1, source_target_pairs={{0,8},{8,16},{16,24},{24,0},{1,9},{9,17},{17,25},{25,1},{2,10},{10... | collective-permute-start | bytes 417800 | tf_op jit(solution)/shard_map/ppermute | solution.py:352
  22.7 9.7 %collective-permute-start.8 = (f32[136,256]{1,0:T(8,128)S(1)}, f32[136,256]{1,0:T(8,128)S(1)}, u32[]{:S(2)}, u32[]{:S(2)}) collective-permute-start(f32[136,256]{1,0:T(8,128)S(1)} %get-tuple-element.69), channel_id=1, source_target_pairs={{0,16},{8,24},{16,0},{24,8},{1,17},{9,25},{17,1},{25,9},{2,18},{10... | collective-permute-start | bytes 417800 | tf_op jit(solution)/shard_map/ppermute | solution.py:352
  26.3 6.1 %collective-permute-start.9 = (f32[136,256]{1,0:T(8,128)S(1)}, f32[136,256]{1,0:T(8,128)S(1)}, u32[]{:S(2)}, u32[]{:S(2)}) collective-permute-start(f32[136,256]{1,0:T(8,128)S(1)} %get-tuple-element.70), channel_id=1, source_target_pairs={{0,24},{8,0},{16,8},{24,16},{1,25},{9,1},{17,9},{25,17},{2,26},{10... | collective-permute-start | bytes 417800 | tf_op jit(solution)/shard_map/ppermute | solution.py:352
  33.0 8.6 %collective-permute-start.12 = (f32[136,256]{1,0:T(8,128)S(1)}, f32[136,256]{1,0:T(8,128)S(1)}, u32[]{:S(2)}, u32[]{:S(2)}) collective-permute-start(f32[136,256]{1,0:T(8,128)S(1)} %get-tuple-element.71.refs_1_), channel_id=1, source_target_pairs={{0,96},{32,0},{64,32},{96,64},{1,97},{33,1},{65,33},{97,65},{2,98}... | collective-permute-start | bytes 417800 | tf_op jit(solution)/shard_map/ppermute | solution.py:352
  36.1 14.1 %collective-permute-start.16 = (bf16[144,768]{1,0:T(8,128)(2,1)S(1)}, bf16[144,768]{1,0:T(8,128)(2,1)S(1)}, u32[]{:S(2)}, u32[]{:S(2)}) collective-permute-start(bf16[144,768]{1,0:T(8,128)(2,1)S(1)} %get-tuple-element.78), channel_id=1, source_target_pairs={{0,2},{2,4},{4,6},{6,0},{1,3},{3,5},{5,7},{7,1},{8,10},{10,12},{12... | collective-permute-start | bytes 663560 | tf_op jit(solution)/shard_map/ppermute | solution.py:352
  37.2 6.7 %collective-permute-start.11 = (f32[136,256]{1,0:T(8,128)S(1)}, f32[136,256]{1,0:T(8,128)S(1)}, u32[]{:S(2)}, u32[]{:S(2)}) collective-permute-start(f32[136,256]{1,0:T(8,128)S(1)} %get-tuple-element.71.refs_1_), channel_id=1, source_target_pairs={{0,64},{32,96},{64,0},{96,32},{1,65},{33,97},{65,1},{97,33},{2,66}... | collective-permute-start | bytes 417800 | tf_op jit(solution)/shard_map/ppermute | solution.py:352
  37.8 7.5 %collective-permute-start.10 = (f32[136,256]{1,0:T(8,128)S(1)}, f32[136,256]{1,0:T(8,128)S(1)}, u32[]{:S(2)}, u32[]{:S(2)}) collective-permute-start(f32[136,256]{1,0:T(8,128)S(1)} %get-tuple-element.71.refs_1_), channel_id=1, source_target_pairs={{0,32},{32,64},{64,96},{96,0},{1,33},{33,65},{65,97},{97,1},{2,34}... | collective-permute-start | bytes 417800 | tf_op jit(solution)/shard_map/ppermute | solution.py:352
  38.8 12.3 %collective-permute-start.17 = (bf16[144,768]{1,0:T(8,128)(2,1)S(1)}, bf16[144,768]{1,0:T(8,128)(2,1)S(1)}, u32[]{:S(2)}, u32[]{:S(2)}) collective-permute-start(bf16[144,768]{1,0:T(8,128)(2,1)S(1)} %get-tuple-element.79), channel_id=1, source_target_pairs={{0,4},{2,6},{4,0},{6,2},{1,5},{3,7},{5,1},{7,3},{8,12},{10,14},{12... | collective-permute-start | bytes 663560 | tf_op jit(solution)/shard_map/ppermute | solution.py:352
  41.7 9.4 %collective-permute-start.18 = (bf16[144,768]{1,0:T(8,128)(2,1)S(1)}, bf16[144,768]{1,0:T(8,128)(2,1)S(1)}, u32[]{:S(2)}, u32[]{:S(2)}) collective-permute-start(bf16[144,768]{1,0:T(8,128)(2,1)S(1)} %get-tuple-element.80), channel_id=1, source_target_pairs={{0,6},{2,0},{4,2},{6,4},{1,7},{3,1},{5,3},{7,5},{8,14},{10,8},{12,... | collective-permute-start | bytes 663560 | tf_op jit(solution)/shard_map/ppermute | solution.py:352
  46.0 8.4 %collective-permute-start.13 = (f32[128,256]{1,0:T(8,128)S(1)}, f32[128,256]{1,0:T(8,128)S(1)}, u32[]{:S(2)}, u32[]{:S(2)}) collective-permute-start(f32[128,256]{1,0:T(8,128)S(1)} %get-tuple-element.74), channel_id=1, source_target_pairs={{0,8},{8,16},{16,24},{24,0},{1,9},{9,17},{17,25},{25,1},{2,10},{10... | collective-permute-start | bytes 393224 | tf_op jit(solution)/shard_map/ppermute | solution.py:352
  48.4 7.6 %collective-permute-start.14 = (f32[128,256]{1,0:T(8,128)S(1)}, f32[128,256]{1,0:T(8,128)S(1)}, u32[]{:S(2)}, u32[]{:S(2)}) collective-permute-start(f32[128,256]{1,0:T(8,128)S(1)} %get-tuple-element.75), channel_id=1, source_target_pairs={{0,16},{8,24},{16,0},{24,8},{1,17},{9,25},{17,1},{25,9},{2,18},{10... | collective-permute-start | bytes 393224 | tf_op jit(solution)/shard_map/ppermute | solution.py:352
  50.2 5.7 %collective-permute-start.15 = (f32[128,256]{1,0:T(8,128)S(1)}, f32[128,256]{1,0:T(8,128)S(1)}, u32[]{:S(2)}, u32[]{:S(2)}) collective-permute-start(f32[128,256]{1,0:T(8,128)S(1)} %get-tuple-element.76), channel_id=1, source_target_pairs={{0,24},{8,0},{16,8},{24,16},{1,25},{9,1},{17,9},{25,17},{2,26},{10... | collective-permute-start | bytes 393224 | tf_op jit(solution)/shard_map/ppermute | solution.py:352
  58.1 10.6 %collective-permute-start.19 = (bf16[144,768]{1,0:T(8,128)(2,1)S(1)}, bf16[144,768]{1,0:T(8,128)(2,1)S(1)}, u32[]{:S(2)}, u32[]{:S(2)}) collective-permute-start(bf16[144,768]{1,0:T(8,128)(2,1)S(1)} %get-tuple-element.91), channel_id=1, source_target_pairs={{0,2},{2,4},{4,6},{6,0},{1,3},{3,5},{5,7},{7,1},{8,10},{10,12},{12... | collective-permute-start | bytes 663560 | tf_op jit(solution)/shard_map/ppermute | solution.py:352
  59.5 11.0 %collective-permute-start.20 = (bf16[144,768]{1,0:T(8,128)(2,1)S(1)}, bf16[144,768]{1,0:T(8,128)(2,1)S(1)}, u32[]{:S(2)}, u32[]{:S(2)}) collective-permute-start(bf16[144,768]{1,0:T(8,128)(2,1)S(1)} %get-tuple-element.92), channel_id=1, source_target_pairs={{0,4},{2,6},{4,0},{6,2},{1,5},{3,7},{5,1},{7,3},{8,12},{10,14},{12... | collective-permute-start | bytes 663560 | tf_op jit(solution)/shard_map/ppermute | solution.py:352
  61.8 9.0 %collective-permute-start.21 = (bf16[144,768]{1,0:T(8,128)(2,1)S(1)}, bf16[144,768]{1,0:T(8,128)(2,1)S(1)}, u32[]{:S(2)}, u32[]{:S(2)}) collective-permute-start(bf16[144,768]{1,0:T(8,128)(2,1)S(1)} %get-tuple-element.93), channel_id=1, source_target_pairs={{0,6},{2,0},{4,2},{6,4},{1,7},{3,1},{5,3},{7,5},{8,14},{10,8},{12,... | collective-permute-start | bytes 663560 | tf_op jit(solution)/shard_map/ppermute | solution.py:352
  63.9 14.4 %all-to-all-start = ((f32[64,2,128]{2,1,0:T(2,128)}), f32[64,2,128]{2,1,0:T(2,128)S(1)}, u32[]{:S(2)}, u32[]{:S(2)}) async-start(f32[64,2,128]{2,1,0:T(2,128)} %get-tuple-element.97), calls=%async_computation | async-start | bytes 131072 | tf_op jit(solution)/shard_map/all_to_all | solution.py:442
  (2 other events, 5.1 us)

commit v4 on v3

--- a/solution.py
+++ b/solution.py
@@ -77,21 +77,23 @@
 def pack_first(idx, grad, query, decay, *refs):
     outs, send, keep = refs[0:4], refs[4], refs[5]
     g, q, a, heads, scr, sems = refs[6:12]
-    copies = [
-        pltpu.make_async_copy(source, target, sems.at[i])
-        for i, (source, target) in enumerate(((grad, g), (query, q), (decay, a)))
-    ]
+    quarter = TOK // 4
+    pieces = [pl.ds(quarter * i, quarter) for i in range(2)]
+    copies = [pltpu.make_async_copy(grad.at[p], g.at[p], sems.at[i]) for i, p in enumerate(pieces)]
+    copies.append(pltpu.make_async_copy(query, q, sems.at[2]))
+    copies.append(pltpu.make_async_copy(decay, a, sems.at[3]))
     for copy in copies:
         copy.start()
     x, c = idx[0], idx[3]
-    copies[0].wait()
-    heads[...] = jnp.swapaxes(g[...], 0, 1)
+    for i, p in enumerate(pieces):
+        copies[i].wait()
+        heads[:, p, :] = jnp.swapaxes(g[p], 0, 1)
     for i in range(NH):
         send[i] = heads[NH * (1 - c) + i]
         keep[i] = heads[NH * c + i]
-    copies[1].wait()
+    copies[2].wait()
     scr[:, :, :DK] = jnp.swapaxes(q[...], 0, 1)
-    copies[2].wait()
+    copies[3].wait()
     scr[:, :, DK:] = jnp.swapaxes(a[...], 0, 1)
     for s in range(4):
         outs[s][...] = scr[(x + s) % 4]
@@ -148,37 +150,40 @@
     dq_out[...] = jnp.swapaxes(scr[...].astype(B16), 0, 1)
 
 
-def line_cum(qa, cum_scr):
+def line_prep(idx, *refs):
+    qa = refs[0:4]
+    rise, cum, logs = refs[4:7]
+    rows_qa = refs[7]
+    x = idx[0]
+    for s in range(4):
+        j = (x - s + 4) % 4
+        rows_qa[pl.ds(pl.multiple_of(TOK * j, TOK), TOK), :] = qa[s][...]
     tri = triangle(False).astype(B16)
     base = jnp.zeros((1, DK), F32)
     for j in range(4):
         rows = slice(TOK * j, TOK * (j + 1))
-        cum = dot(tri, qa[rows, DK:], NN) + base
-        base = cum[TOK - 1 :, :]
-        cum_scr[rows, :] = cum
-    return base
+        inside = dot(tri, rows_qa[rows, DK:], NN) + base
+        base = inside[TOK - 1 :, :]
+        cum[rows, :] = inside
+        q = rows_qa[rows, :DK].astype(F32)
+        rise[rows, :DK], rise[rows, DK:] = split(SCALE * q * jnp.exp(inside))
+    logs[...] = jnp.broadcast_to(base, (8, DK))
 
 
 def line_state(idx, *refs):
-    qa, gr = refs[0:4], refs[4:8]
-    chunks = refs[8:12]
-    qa_out, g_out = refs[12:14]
-    acc, cum_scr = refs[14:16]
+    gr, rise, logs = refs[0:4], refs[4], refs[5]
+    chunks, g_out = refs[6:10], refs[10]
+    acc = refs[11]
     x, z = idx[0], idx[1]
     for s in range(4):
         j = (x - s + 4) % 4
-        rows = pl.ds(pl.multiple_of(TOK * j, TOK), TOK)
-        qa_out[rows, :] = qa[s][...]
-        g_out[rows, :] = gr[s][...]
-    base = line_cum(qa_out, cum_scr)
-    rise = qa_out[:, :DK].astype(F32) * jnp.exp(cum_scr[...])
-    high, lo = split(SCALE * rise)
-    g = g_out[...]
-    acc[...] = dot(g, high, TN) + dot(g, lo, TN)
+        g_out[pl.ds(pl.multiple_of(TOK * j, TOK), TOK), :] = gr[s][...]
+    both = dot(g_out[...], rise[...], TN)
+    acc[...] = both[:, :DK] + both[:, DK:]
     for s in range(4):
         at = pl.multiple_of(TOK * ((z + s) % 4), TOK)
         chunks[s][:TOK, :] = acc[pl.ds(at, TOK), :]
-        chunks[s][TOK:, :] = jnp.broadcast_to(base, (8, DK))
+        chunks[s][TOK:, :] = logs[...]
 
 
 def scan_z(idx, *refs):
@@ -218,22 +223,21 @@
 
 
 def near_part(idx, *refs):
-    qa, g = refs[0:2]
-    kv = refs[2:6]
-    dk_near, dv_near, k_end, ends, v_out, k_out = refs[6:12]
-    rise, cum = refs[12:14]
-    last = line_cum(qa, cum)
+    g, rise, cum = refs[0:3]
+    kv = refs[3:7]
+    dk_near, dv_near, k_end, ends, v_out, k_out = refs[7:13]
     x = idx[0]
     for s in range(4):
         j = (x - s + 4) % 4
         rows = pl.ds(pl.multiple_of(TOK * j, TOK), TOK)
         k_out[rows, :] = kv[s][:TOK, :DK]
         v_out[rows, :] = kv[s][:TOK, DK:]
-    rise[...] = SCALE * qa[:, :DK].astype(F32) * jnp.exp(cum[...])
-    end = jnp.exp(last - cum[...])
+    end = jnp.exp(cum[4 * TOK - 1 :, :] - cum[...])
     ends[...] = end
-    k_end[:, :DK], k_end[:, DK:] = split(k_out[...].astype(F32) * end)
-    upper = triangle(True)
+    k_high, k_low = split(k_out[...].astype(F32) * end)
+    k_end[:, :DK] = k_high
+    k_end[:, DK : 2 * DK] = k_low
+    k_end[:, 2 * DK :] = k_high
     for j in range(4):
         rows = slice(TOK * j, TOK * (j + 1))
         width = 4 * TOK - TOK * j
@@ -242,11 +246,15 @@
         keep = lax.broadcasted_iota(jnp.int32, (TOK, width), 1) >= lax.broadcasted_iota(
             jnp.int32, (TOK, width), 0
         )
+        high, lo = rise[later, :DK], rise[later, DK:]
         scores = jnp.where(keep, dot(v_out[rows, :], g[later, :], NT), 0.0)
-        dk_near[rows, :] = fall * dot3(scores, rise[later, :], NN)
-        k_fall = k_out[rows, :].astype(F32) * fall
-        affinity = jnp.where(keep, dot3(k_fall, rise[later, :], NT), 0.0)
-        dv_near[rows, :] = dot2(affinity, g[later, :], NN)
+        s_high, s_low = split(scores)
+        dk_near[rows, :] = fall * (
+            dot(s_high, high, NN) + (dot(s_low, high, NN) + dot(s_high, lo, NN))
+        )
+        f_high, f_low = split(k_out[rows, :].astype(F32) * fall)
+        affinity = dot(f_high, high, NT) + (dot(f_low, high, NT) + dot(f_high, lo, NT))
+        dv_near[rows, :] = dot2(jnp.where(keep, affinity, 0.0), g[later, :], NN)
 
 
 def far_part(idx, *refs):
@@ -255,49 +263,48 @@
     dk_near, dv_near, k_end, ends, v, k = refs[8:14]
     outs = refs[14:18]
     sums = refs[18]
-    state, scr, total = refs[19:22]
+    state, dk_all, dv_all, ahead, total = refs[19:24]
     x, z = idx[0], idx[1]
     for s in range(4):
         j = (z - s + 4) % 4
-        state[pl.ds(pl.multiple_of(TOK * j, TOK), TOK), :] = parts[s][...]
-    high, lo = split(state[...])
-    reached = dot(v[...], high, NN) + dot(v[...], lo, NN)
+        rows = pl.ds(pl.multiple_of(TOK * j, TOK), TOK)
+        high, lo = split(parts[s][...])
+        state[rows, :DK] = high
+        state[rows, DK : 2 * DK] = high
+        state[rows, 2 * DK :] = lo
+    reached = dot(v[...], state[:, :DK], NN) + dot(v[...], state[:, 2 * DK :], NN)
     dk = dk_near[...] + ends[...] * reached
-    e_high, e_low = k_end[:, :DK], k_end[:, DK:]
-    dv = dv_near[...] + (
-        dot(e_high, high, NT) + (dot(e_low, high, NT) + dot(e_high, lo, NT))
-    )
-    kdk = k[...].astype(F32) * dk
-    group = lax.broadcasted_iota(jnp.int32, (GROUPS, TOK), 0)
-    token = lax.broadcasted_iota(jnp.int32, (GROUPS, TOK), 1)
-    after = (token >= (group + 1) * (TOK // GROUPS)).astype(B16)
-    for j in range(4):
-        total[j : j + 1, :] = -jnp.sum(
-            kdk[TOK * j : TOK * (j + 1), :], axis=0, keepdims=True
-        )
+    dk_all[...] = dk
+    dv_all[...] = dv_near[...] + dot(k_end[...], state[...], NT)
+    kdk_high, kdk_low = split(k[...].astype(F32) * dk)
+    group = lax.broadcasted_iota(jnp.int32, (4 * GROUPS + 8, 4 * TOK), 0)
+    token = lax.broadcasted_iota(jnp.int32, (4 * GROUPS + 8, 4 * TOK), 1)
+    first = jnp.where(group < 4 * GROUPS, (group + 1) * (TOK // GROUPS), 0)
+    after = (token >= first).astype(B16)
+    behind = dot(after, kdk_high, NN) + dot(after, kdk_low, NN)
     for s in range(4):
         j = (x - s + 4) % 4
-        tot = (
+        total[pl.ds(j, 1), :] = (
             kv[s][TOK : TOK + 1, :DK].astype(F32)
             + kv[s][TOK : TOK + 1, DK : 2 * DK].astype(F32)
             + kv[s][TOK : TOK + 1, 2 * DK :].astype(F32)
         )
-        total[pl.ds(j, 1), :] = total[pl.ds(j, 1), :] + tot
     running = jnp.zeros((1, DK), F32)
     for j in reversed(range(4)):
-        rows = slice(TOK * j, TOK * (j + 1))
-        part_high, part_low = split(kdk[rows, :])
-        ahead = three(running - (dot(after, part_high, NN) + dot(after, part_low, NN)))
+        rows = slice(GROUPS * j, GROUPS * (j + 1))
+        for i, word in enumerate(three(running - behind[rows, :])):
+            ahead[j, :, DK * i : DK * (i + 1)] = word
         running = running + total[j : j + 1, :]
-        scr[j, :TOK, :DK] = dk[rows, :].astype(B16)
-        scr[j, :TOK, DK:] = dv[rows, :].astype(B16)
-        for i in range(3):
-            scr[j, TOK:, DK * i : DK * (i + 1)] = ahead[i]
+    running = running - behind[4 * GROUPS : 4 * GROUPS + 1, :]
     block = jnp.concatenate([running[:, :128], running[:, 128:]], axis=0)
     for d in range(64):
         sums[d] = block
     for s in range(4):
-        outs[s][...] = scr[(x + s) % 4]
+        j = (x + s) % 4
+        rows = pl.ds(pl.multiple_of(TOK * j, TOK), TOK)
+        outs[s][:TOK, :DK] = dk_all[rows, :].astype(B16)
+        outs[s][:TOK, DK:] = dv_all[rows, :].astype(B16)
+        outs[s][TOK:, :] = ahead[j]
 
 
 def final_part(idx, *refs):
@@ -337,7 +344,7 @@
     da_part[...] = jnp.swapaxes(s_da[...], 0, 1)
 
 
-def decay_part(idx, da_part, sums, da_out):
+def decay_part(idx, da_part, sums, da_out, rounded, sems):
     line = idx[2] * 4 + idx[1]
     later = []
     for h in range(NH):
@@ -345,7 +352,15 @@
         for l in range(1, 16):
             acc = acc + jnp.where(l > line, sums[4 * l + h], 0.0)
         later.append(jnp.concatenate([acc[0:1], acc[1:2]], axis=1))
-    da_out[...] = (da_part[...] + jnp.concatenate(later, axis=0)[None]).astype(B16)
+    later = jnp.concatenate(later, axis=0)[None]
+    copies = []
+    for i in range(2):
+        rows = pl.ds(TOK // 2 * i, TOK // 2)
+        rounded[rows] = (da_part[rows] + later).astype(B16)
+        copies.append(pltpu.make_async_copy(rounded.at[rows], da_out.at[rows], sems.at[i]))
+        copies[i].start()
+    for copy in copies:
+        copy.wait()
 
 
 def shifted(value, axis, s):
@@ -376,7 +391,7 @@
             vm((TOK, NH, DK), B16),
             vm((2 * NH, half, DV), B16),
             vm((NH, TOK, 2 * DK), B16),
-            pltpu.SemaphoreType.DMA((3,)),
+            pltpu.SemaphoreType.DMA((4,)),
         ],
         name="pack_first",
         compiler_params=pltpu.CompilerParams(vmem_limit_bytes=16 * 1024 * 1024),
@@ -395,15 +410,19 @@
         [vm((NH, TOK, DK), F32)],
     )(idx, *qa, *g, *kv, checkpoints)
     dq, qdq, kv = res[0], res[1], res[2:]
-    res = call(
+    rise, cum, logs = call(
+        line_prep,
+        [sds((4 * TOK, 2 * DK)), sds((4 * TOK, DK), F32), sds((8, DK), F32)],
+        4,
+        [vm((4 * TOK, 2 * DK), B16)],
+    )(idx, *qa_line)
+    *chunks, g_rows = call(
         line_state,
-        [sds((TOK + 8, DK), F32)] * 4
-        + [sds((4 * TOK, 2 * DK)), sds((4 * TOK, DV))],
-        8,
-        [vm((DV, DK), F32), vm((4 * TOK, DK), F32)],
+        [sds((TOK + 8, DK), F32)] * 4 + [sds((4 * TOK, DV))],
+        6,
+        [vm((DV, DK), F32)],
         (qdq,),
-    )(idx, *qa_line, *g_line)
-    chunks, qa_rows, g_rows = res[:4], res[4], res[5]
+    )(idx, *g_line, rise, logs)
     z_in = spread(chunks, Z)
     kv_line = spread(kv, X)
     total, suffix = call(
@@ -422,20 +441,26 @@
         [
             sds((4 * TOK, DK), F32),
             sds((4 * TOK, DV), F32),
-            sds((4 * TOK, 2 * DK)),
+            sds((4 * TOK, 3 * DK)),
             sds((4 * TOK, DK), F32),
             sds((4 * TOK, DV)),
             sds((4 * TOK, DK)),
         ],
-        6,
-        [vm((4 * TOK, DK), F32)] * 2,
+        7,
+        (),
         (token,),
-    )(idx, qa_rows, g_rows, *kv_line)
+    )(idx, g_rows, rise, cum, *kv_line)
     res = call(
         far_part,
         [sds((TOK + GROUPS, DK + DV))] * 4 + [sds((64, 2, 128), F32)],
         14,
-        [vm((DV, DK), F32), vm((4, TOK + GROUPS, DK + DV), B16), vm((4, DK), F32)],
+        [
+            vm((DV, 3 * DK), B16),
+            vm((4 * TOK, DK), F32),
+            vm((4 * TOK, DV), F32),
+            vm((4, GROUPS, DK + DV), B16),
+            vm((4, DK), F32),
+        ],
     )(idx, *carry_in, *kv_line, *near)
     back, sums = res[:4], res[4]
     back_in = spread(back, X)
@@ -451,7 +476,16 @@
             vm((NH, TOK, DK), F32),
         ],
     )(idx, *back_in, qdq, key)
-    da = call(decay_part, sds((TOK, NH, DK)), 2, ())(idx, da_part, sums)
+    vmem = pl.BlockSpec(memory_space=pltpu.VMEM)
+    da = pl.pallas_call(
+        decay_part,
+        out_shape=sds((TOK, NH, DK)),
+        in_specs=[pl.BlockSpec(memory_space=pltpu.SMEM), vmem, vmem],
+        out_specs=hbm,
+        scratch_shapes=[vm((TOK, NH, DK), B16), pltpu.SemaphoreType.DMA((2,))],
+        name="decay_part",
+        compiler_params=pltpu.CompilerParams(vmem_limit_bytes=16 * 1024 * 1024),
+    )(idx, da_part, sums)
     return dq, dk, dv, da
 
 

time: 79.9 us -> 79.9 us (level)
  local copies, waits for them, and re-layouts: 1.05 us -> 0.01 us
    pallas_call x0 -> x1, Pallas kernels: none -> 1.33 us  [whole(): pl.pallas_call(decay_part, out_shape=sds((TOK, NH, DK)), in_specs=[pl.Blo...]
    unnamed x6, local copies, waits for them, and re-layouts: 1.05 us -> 0.01 us
  transfers between devices with their start and end apart: 23 -> 23, of which waited for: 9 -> 10; matrix products, arithmetic and copies ran while one was open for 0% -> 0% of each run, Pallas kernels for 13% -> 14%
where the time goes in v4:
time: 79.9 us; the launch traced here: 79.7 us
  starting transfers between devices  42.3 us (53%)
  Pallas kernels  18.5 us (23%)
  waiting for transfers between devices  17.8 us (22%)
  between operations  0.92 us (1%)
    ppermute x21, starting transfers between devices, shifted(): return lax.ppermute(value, axis, [(i, (i + s) % 4) for i in range(4)])  37.4 us
    pallas_call x10, Pallas kernels, call(): return lambda *operands: run(*operands, *after)  15.3 us
    ppermute x21, waiting for transfers between devices, shifted(): return lax.ppermute(value, axis, [(i, (i + s) % 4) for i in range(4)])  12.5 us
    all_to_all x1, waiting for transfers between devices, whole(): sums = lax.all_to_all(sums, SEQ, split_axis=0, concat_axis=0, tiled=True)  5.29 us
    all_to_all x1, starting transfers between devices, whole(): sums = lax.all_to_all(sums, SEQ, split_axis=0, concat_axis=0, tiled=True)  4.86 us
    pallas_call x1, Pallas kernels, whole(): pl.pallas_call(pack_first, out_shape=[sds((TOK, 2 * DK))] * 4 + [sds((NH,...  1.9 us
  transfers between devices with their start and end apart: 23, of which 10 were waited for; matrix products, arithmetic and copies ran while one was open for 0% of the time, Pallas kernels for 14%

profile of v4, /device:TPU:0, one launch (start us, length us, event | category | flops | bytes accessed | tf_op | source)
XLA Modules:
  0.0 79.7 jit_solution(7563008311485697507)
XLA Ops:
  0.7 1.9 %pack_first.1 = (bf16[128,512]{1,0:T(8,128)(2,1)S(1)}, bf16[128,512]{1,0:T(8,128)(2,1)S(1)}, bf16[128,512]{1,0:T(8,128)(2,1)S(1)}, bf16[128,512]{1,0:T(8,128)(2,...) custom-call(s32[4]{0:T(128)S(1)} %pad_add_fusion.idx.refs_0_, bf16[64,8,512]{2,1,0:T(8,128)(2,1)} %grad.1, ...), custom_call_target="tpu_custom_call" | custom-call | tf_op jit(solution)/shard_map/pack_first/pallas_call | solution.py:384
  2.7 1.7 %collective-permute-start.4 = (bf16[128,512]{1,0:T(8,128)(2,1)S(1)}, bf16[128,512]{1,0:T(8,128)(2,1)S(1)}, u32[]{:S(2)}, u32[]{:S(2)}) collective-permute-start(bf16[128,512]{1,0:T(8,128)(2,1)S(1)} %get-tuple-element.54.refs_2_), channel_id=1, source_target_pairs={{0,2},{2,4},{4,6},{6,0},{1,3},{3,5},{5,7},{7,1},{8,10},{10,12},{12... | collective-permute-start | bytes 393224 | tf_op jit(solution)/shard_map/ppermute | solution.py:367
  4.4 2.7 %collective-permute-start.5 = (bf16[128,512]{1,0:T(8,128)(2,1)S(1)}, bf16[128,512]{1,0:T(8,128)(2,1)S(1)}, u32[]{:S(2)}, u32[]{:S(2)}) collective-permute-start(bf16[128,512]{1,0:T(8,128)(2,1)S(1)} %get-tuple-element.55.refs_3_), channel_id=1, source_target_pairs={{0,4},{2,6},{4,0},{6,2},{1,5},{3,7},{5,1},{7,3},{8,12},{10,14},{12... | collective-permute-start | bytes 393224 | tf_op jit(solution)/shard_map/ppermute | solution.py:367
  7.1 1.4 %collective-permute-start.6 = (bf16[128,512]{1,0:T(8,128)(2,1)S(1)}, bf16[128,512]{1,0:T(8,128)(2,1)S(1)}, u32[]{:S(2)}, u32[]{:S(2)}) collective-permute-start(bf16[128,512]{1,0:T(8,128)(2,1)S(1)} %get-tuple-element.56.refs_4_), channel_id=1, source_target_pairs={{0,6},{2,0},{4,2},{6,4},{1,7},{3,1},{5,3},{7,5},{8,14},{10,8},{12,... | collective-permute-start | bytes 393224 | tf_op jit(solution)/shard_map/ppermute | solution.py:367
  10.7 1.9 %collective-permute-start.3 = (bf16[128,512]{1,0:T(8,128)(2,1)S(1)}, bf16[128,512]{1,0:T(8,128)(2,1)S(1)}, u32[]{:S(2)}, u32[]{:S(2)}) collective-permute-start(bf16[128,512]{1,0:T(8,128)(2,1)S(1)} %get-tuple-element.62.refs_8_), channel_id=1, source_target_pairs={{0,6},{2,0},{4,2},{6,4},{1,7},{3,1},{5,3},{7,5},{8,14},{10,8},{12,... | collective-permute-start | bytes 393224 | tf_op jit(solution)/shard_map/ppermute | solution.py:367
  15.2 2.8 %shard_map.95 = (bf16[128,4,256]{2,1,0:T(4,128)(2,1)}, f32[4,128,256]{2,1,0:T(8,128)S(1)}, bf16[144,768]{1,0:T(8,128)(2,1)S(1)}, bf16[144,768]{1,0:T(8,128)(2,1)...) custom-call(s32[4]{0:T(128)S(1)} %pad_add_fusion.idx.refs_0_, ...), custom_call_target="tpu_custom_call" | custom-call | tf_op jit(solution)/shard_map/pallas_call | solution.py:74
  20.5 2.0 %collective-permute-start.7 = (f32[136,256]{1,0:T(8,128)S(1)}, f32[136,256]{1,0:T(8,128)S(1)}, u32[]{:S(2)}, u32[]{:S(2)}) collective-permute-start(f32[136,256]{1,0:T(8,128)S(1)} %get-tuple-element.72), channel_id=1, source_target_pairs={{0,8},{8,16},{16,24},{24,0},{1,9},{9,17},{17,25},{25,1},{2,10},{10... | collective-permute-start | bytes 417800 | tf_op jit(solution)/shard_map/ppermute | solution.py:367
  22.5 3.6 %collective-permute-start.8 = (f32[136,256]{1,0:T(8,128)S(1)}, f32[136,256]{1,0:T(8,128)S(1)}, u32[]{:S(2)}, u32[]{:S(2)}) collective-permute-start(f32[136,256]{1,0:T(8,128)S(1)} %get-tuple-element.73), channel_id=1, source_target_pairs={{0,16},{8,24},{16,0},{24,8},{1,17},{9,25},{17,1},{25,9},{2,18},{10... | collective-permute-start | bytes 417800 | tf_op jit(solution)/shard_map/ppermute | solution.py:367
  28.2 3.9 %collective-permute-done.8.refs_3_ = f32[136,256]{1,0:T(8,128)S(1)} collective-permute-done((f32[136,256]{1,0:T(8,128)S(1)}, f32[136,256]{1,0:T(8,128)S(1)}, u32[]{:S(2)}, u32[]{:S(2)}) %collective-permute-start.8) | collective-permute-done | bytes 139296 | tf_op jit(solution)/shard_map/ppermute | solution.py:367
  32.8 3.1 %collective-permute-start.12 = (f32[136,256]{1,0:T(8,128)S(1)}, f32[136,256]{1,0:T(8,128)S(1)}, u32[]{:S(2)}, u32[]{:S(2)}) collective-permute-start(f32[136,256]{1,0:T(8,128)S(1)} %get-tuple-element.75.refs_1_), channel_id=1, source_target_pairs={{0,96},{32,0},{64,32},{96,64},{1,97},{33,1},{65,33},{97,65},{2,98}... | collective-permute-start | bytes 417800 | tf_op jit(solution)/shard_map/ppermute | solution.py:367
  38.5 2.9 %collective-permute-start.17 = (bf16[144,768]{1,0:T(8,128)(2,1)S(1)}, bf16[144,768]{1,0:T(8,128)(2,1)S(1)}, u32[]{:S(2)}, u32[]{:S(2)}) collective-permute-start(bf16[144,768]{1,0:T(8,128)(2,1)S(1)} %get-tuple-element.83), channel_id=1, source_target_pairs={{0,4},{2,6},{4,0},{6,2},{1,5},{3,7},{5,1},{7,3},{8,12},{10,14},{12... | collective-permute-start | bytes 663560 | tf_op jit(solution)/shard_map/ppermute | solution.py:367
  41.5 2.0 %collective-permute-start.18 = (bf16[144,768]{1,0:T(8,128)(2,1)S(1)}, bf16[144,768]{1,0:T(8,128)(2,1)S(1)}, u32[]{:S(2)}, u32[]{:S(2)}) collective-permute-start(bf16[144,768]{1,0:T(8,128)(2,1)S(1)} %get-tuple-element.84), channel_id=1, source_target_pairs={{0,6},{2,0},{4,2},{6,4},{1,7},{3,1},{5,3},{7,5},{8,14},{10,8},{12,... | collective-permute-start | bytes 663560 | tf_op jit(solution)/shard_map/ppermute | solution.py:367
  43.6 1.4 %collective-permute-done.10.refs_2_ = f32[136,256]{1,0:T(8,128)S(1)} collective-permute-done((f32[136,256]{1,0:T(8,128)S(1)}, f32[136,256]{1,0:T(8,128)S(1)}, u32[]{:S(2)}, u32[]{:S(2)}) %collective-permute-start.10) | collective-permute-done | bytes 139296 | tf_op jit(solution)/shard_map/ppermute | solution.py:367
  45.8 2.4 %collective-permute-start.13 = (f32[128,256]{1,0:T(8,128)S(1)}, f32[128,256]{1,0:T(8,128)S(1)}, u32[]{:S(2)}, u32[]{:S(2)}) collective-permute-start(f32[128,256]{1,0:T(8,128)S(1)} %get-tuple-element.78), channel_id=1, source_target_pairs={{0,8},{8,16},{16,24},{24,0},{1,9},{9,17},{17,25},{25,1},{2,10},{10... | collective-permute-start | bytes 393224 | tf_op jit(solution)/shard_map/ppermute | solution.py:367
  48.1 1.8 %collective-permute-start.14 = (f32[128,256]{1,0:T(8,128)S(1)}, f32[128,256]{1,0:T(8,128)S(1)}, u32[]{:S(2)}, u32[]{:S(2)}) collective-permute-start(f32[128,256]{1,0:T(8,128)S(1)} %get-tuple-element.79), channel_id=1, source_target_pairs={{0,16},{8,24},{16,0},{24,8},{1,17},{9,25},{17,1},{25,9},{2,18},{10... | collective-permute-start | bytes 393224 | tf_op jit(solution)/shard_map/ppermute | solution.py:367
  50.9 3.2 %shard_map.100 = (f32[512,256]{1,0:T(8,128)S(1)}, f32[512,512]{1,0:T(8,128)S(1)}, bf16[512,768]{1,0:T(8,128)(2,1)S(1)}, f32[512,256]{1,0:T(8,128)S(1)}, bf16[512...) custom-call(s32[4]{0:T(128)S(1)} %pad_add_fusion.idx.refs_0_, bf16[512,512]{1,0:T(8,128)(2,1)S(1)} %get-tuple-element.85.refs_1_, ...), custom_call_target="tpu_custom_call" | custom-call | tf_op jit(solution)/shard_map/pallas_call | solution.py:74
  54.1 1.6 %collective-permute-done.14.refs_3_ = f32[128,256]{1,0:T(8,128)S(1)} collective-permute-done((f32[128,256]{1,0:T(8,128)S(1)}, f32[128,256]{1,0:T(8,128)S(1)}, u32[]{:S(2)}, u32[]{:S(2)}) %collective-permute-start.14) | collective-permute-done | bytes 131104 | tf_op jit(solution)/shard_map/ppermute | solution.py:367
  55.7 2.3 %shard_map.101 = (bf16[144,768]{1,0:T(8,128)(2,1)S(1)}, bf16[144,768]{1,0:T(8,128)(2,1)S(1)}, bf16[144,768]{1,0:T(8,128)(2,1)S(1)}, bf16[144,768]{1,0:T(8,128)(2,1)S(1)}, f32[64,2,128]{2,1,0:T(2,128)}) custom-call(s32[4]{0:T(128)S(1)} %pad_add_fusion.idx.refs_0_, f32[128,256]{1,0:T(8,128)S(1)} %get-tuple-element.77.refs_1_, ...), custom_call_target="tpu_custom_call" | custom-call | tf_op jit(solution)/shard_map/pallas_call | solution.py:74
  59.3 2.4 %collective-permute-start.20 = (bf16[144,768]{1,0:T(8,128)(2,1)S(1)}, bf16[144,768]{1,0:T(8,128)(2,1)S(1)}, u32[]{:S(2)}, u32[]{:S(2)}) collective-permute-start(bf16[144,768]{1,0:T(8,128)(2,1)S(1)} %get-tuple-element.96), channel_id=1, source_target_pairs={{0,4},{2,6},{4,0},{6,2},{1,5},{3,7},{5,1},{7,3},{8,12},{10,14},{12... | collective-permute-start | bytes 663560 | tf_op jit(solution)/shard_map/ppermute | solution.py:367
  61.6 2.1 %collective-permute-start.21 = (bf16[144,768]{1,0:T(8,128)(2,1)S(1)}, bf16[144,768]{1,0:T(8,128)(2,1)S(1)}, u32[]{:S(2)}, u32[]{:S(2)}) collective-permute-start(bf16[144,768]{1,0:T(8,128)(2,1)S(1)} %get-tuple-element.97), channel_id=1, source_target_pairs={{0,6},{2,0},{4,2},{6,4},{1,7},{3,1},{5,3},{7,5},{8,14},{10,8},{12,... | collective-permute-start | bytes 663560 | tf_op jit(solution)/shard_map/ppermute | solution.py:367
  63.8 4.9 %all-to-all-start = ((f32[64,2,128]{2,1,0:T(2,128)}), f32[64,2,128]{2,1,0:T(2,128)S(1)}, u32[]{:S(2)}, u32[]{:S(2)}) async-start(f32[64,2,128]{2,1,0:T(2,128)} %get-tuple-element.101), calls=%async_computation | async-start | bytes 131072 | tf_op jit(solution)/shard_map/all_to_all | solution.py:467
  68.6 1.6 %collective-permute-done.20.refs_3_ = bf16[144,768]{1,0:T(8,128)(2,1)S(1)} collective-permute-done((bf16[144,768]{1,0:T(8,128)(2,1)S(1)}, bf16[144,768]{1,0:T(8,128)(2,1)S(1)}, u32[]{:S(2)}, u32[]{:S(2)}) %collective-permute-start.20) | collective-permute-done | bytes 221216 | tf_op jit(solution)/shard_map/ppermute | solution.py:367
  70.6 2.3 %shard_map.102 = (bf16[128,4,256]{2,1,0:T(4,128)(2,1)}, bf16[128,4,512]{2,1,0:T(4,128)(2,1)}, f32[128,4,256]{2,1,0:T(4,128)S(1)}) custom-call(s32[4]{0:T(128)S(1)} %pad_add_fusion.idx.refs_0_, bf16[144,768]{1,0:T(8,128)(2,1)S(1)} %get-tuple-element.94.refs_1_, bf16[144,768]{1,0:T(8,128)(2,1)S(1)} %collective-permute-done.19.refs_2_, ...), custom_call_target="tpu_custom_call" | custom-call | tf_op jit(solution)/shard_map/pallas_call | solution.py:74
  72.9 5.3 %all-to-all-done.sums = f32[64,2,128]{2,1,0:T(2,128)S(1)} async-done(((f32[64,2,128]{2,1,0:T(2,128)}), f32[64,2,128]{2,1,0:T(2,128)S(1)}, u32[]{:S(2)}, u32[]{:S(2)}) %all-to-all-start) | async-done | bytes 65568 | tf_op jit(solution)/shard_map/all_to_all | solution.py:467
  (41 shorter events, 17.6 us)
Async XLA Ops:
  2.6 12.6 %copy-start = (bf16[1,4,256,512]{3,2,1,0:T(8,128)(2,1)S(1)}, bf16[1,4,256,512]{3,2,1,0:T(8,128)(2,1)}, u32[]{:S(2)}) copy-start(bf16[1,4,256,512]{3,2,1,0:T(8,128)(2,1)} %refs_13_.1) | copy-start | bytes 3145732
  2.6 5.9 %collective-permute-start = (bf16[4,64,512]{2,1,0:T(8,128)(2,1)S(1)}, bf16[4,64,512]{2,1,0:T(8,128)(2,1)S(1)}, u32[]{:S(2)}, u32[]{:S(2)}) collective-permute-start(bf16[4,64,512]{2,1,0:T(8,128)(2,1)S(1)} %get-tuple-element.58), channel_id=1, source_target_pairs={{0,1},{1,0},{2,3},{3,2},{4,5},{5,4},{6,7},{7,6},{8,9},{9,8},{10,11... | collective-permute-start | bytes 786440 | tf_op jit(solution)/shard_map/ppermute | solution.py:399
  2.7 8.0 %collective-permute-start.4 = (bf16[128,512]{1,0:T(8,128)(2,1)S(1)}, bf16[128,512]{1,0:T(8,128)(2,1)S(1)}, u32[]{:S(2)}, u32[]{:S(2)}) collective-permute-start(bf16[128,512]{1,0:T(8,128)(2,1)S(1)} %get-tuple-element.54.refs_2_), channel_id=1, source_target_pairs={{0,2},{2,4},{4,6},{6,0},{1,3},{3,5},{5,7},{7,1},{8,10},{10,12},{12... | collective-permute-start | bytes 393224 | tf_op jit(solution)/shard_map/ppermute | solution.py:367
  4.4 9.9 %collective-permute-start.5 = (bf16[128,512]{1,0:T(8,128)(2,1)S(1)}, bf16[128,512]{1,0:T(8,128)(2,1)S(1)}, u32[]{:S(2)}, u32[]{:S(2)}) collective-permute-start(bf16[128,512]{1,0:T(8,128)(2,1)S(1)} %get-tuple-element.55.refs_3_), channel_id=1, source_target_pairs={{0,4},{2,6},{4,0},{6,2},{1,5},{3,7},{5,1},{7,3},{8,12},{10,14},{12... | collective-permute-start | bytes 393224 | tf_op jit(solution)/shard_map/ppermute | solution.py:367
  7.1 7.2 %collective-permute-start.6 = (bf16[128,512]{1,0:T(8,128)(2,1)S(1)}, bf16[128,512]{1,0:T(8,128)(2,1)S(1)}, u32[]{:S(2)}, u32[]{:S(2)}) collective-permute-start(bf16[128,512]{1,0:T(8,128)(2,1)S(1)} %get-tuple-element.56.refs_4_), channel_id=1, source_target_pairs={{0,6},{2,0},{4,2},{6,4},{1,7},{3,1},{5,3},{7,5},{8,14},{10,8},{12,... | collective-permute-start | bytes 393224 | tf_op jit(solution)/shard_map/ppermute | solution.py:367
  9.2 8.9 %collective-permute-start.1 = (bf16[128,512]{1,0:T(8,128)(2,1)S(1)}, bf16[128,512]{1,0:T(8,128)(2,1)S(1)}, u32[]{:S(2)}, u32[]{:S(2)}) collective-permute-start(bf16[128,512]{1,0:T(8,128)(2,1)S(1)} %get-tuple-element.60.refs_6_), channel_id=1, source_target_pairs={{0,2},{2,4},{4,6},{6,0},{1,3},{3,5},{5,7},{7,1},{8,10},{10,12},{12... | collective-permute-start | bytes 393224 | tf_op jit(solution)/shard_map/ppermute | solution.py:367
  9.8 9.5 %collective-permute-start.2 = (bf16[128,512]{1,0:T(8,128)(2,1)S(1)}, bf16[128,512]{1,0:T(8,128)(2,1)S(1)}, u32[]{:S(2)}, u32[]{:S(2)}) collective-permute-start(bf16[128,512]{1,0:T(8,128)(2,1)S(1)} %get-tuple-element.61.refs_7_), channel_id=1, source_target_pairs={{0,4},{2,6},{4,0},{6,2},{1,5},{3,7},{5,1},{7,3},{8,12},{10,14},{12... | collective-permute-start | bytes 393224 | tf_op jit(solution)/shard_map/ppermute | solution.py:367
  10.7 8.7 %collective-permute-start.3 = (bf16[128,512]{1,0:T(8,128)(2,1)S(1)}, bf16[128,512]{1,0:T(8,128)(2,1)S(1)}, u32[]{:S(2)}, u32[]{:S(2)}) collective-permute-start(bf16[128,512]{1,0:T(8,128)(2,1)S(1)} %get-tuple-element.62.refs_8_), channel_id=1, source_target_pairs={{0,6},{2,0},{4,2},{6,4},{1,7},{3,1},{5,3},{7,5},{8,14},{10,8},{12,... | collective-permute-start | bytes 393224 | tf_op jit(solution)/shard_map/ppermute | solution.py:367
  20.5 7.7 %collective-permute-start.7 = (f32[136,256]{1,0:T(8,128)S(1)}, f32[136,256]{1,0:T(8,128)S(1)}, u32[]{:S(2)}, u32[]{:S(2)}) collective-permute-start(f32[136,256]{1,0:T(8,128)S(1)} %get-tuple-element.72), channel_id=1, source_target_pairs={{0,8},{8,16},{16,24},{24,0},{1,9},{9,17},{17,25},{25,1},{2,10},{10... | collective-permute-start | bytes 417800 | tf_op jit(solution)/shard_map/ppermute | solution.py:367
  22.5 9.7 %collective-permute-start.8 = (f32[136,256]{1,0:T(8,128)S(1)}, f32[136,256]{1,0:T(8,128)S(1)}, u32[]{:S(2)}, u32[]{:S(2)}) collective-permute-start(f32[136,256]{1,0:T(8,128)S(1)} %get-tuple-element.73), channel_id=1, source_target_pairs={{0,16},{8,24},{16,0},{24,8},{1,17},{9,25},{17,1},{25,9},{2,18},{10... | collective-permute-start | bytes 417800 | tf_op jit(solution)/shard_map/ppermute | solution.py:367
  26.0 6.1 %collective-permute-start.9 = (f32[136,256]{1,0:T(8,128)S(1)}, f32[136,256]{1,0:T(8,128)S(1)}, u32[]{:S(2)}, u32[]{:S(2)}) collective-permute-start(f32[136,256]{1,0:T(8,128)S(1)} %get-tuple-element.74), channel_id=1, source_target_pairs={{0,24},{8,0},{16,8},{24,16},{1,25},{9,1},{17,9},{25,17},{2,26},{10... | collective-permute-start | bytes 417800 | tf_op jit(solution)/shard_map/ppermute | solution.py:367
  32.8 8.6 %collective-permute-start.12 = (f32[136,256]{1,0:T(8,128)S(1)}, f32[136,256]{1,0:T(8,128)S(1)}, u32[]{:S(2)}, u32[]{:S(2)}) collective-permute-start(f32[136,256]{1,0:T(8,128)S(1)} %get-tuple-element.75.refs_1_), channel_id=1, source_target_pairs={{0,96},{32,0},{64,32},{96,64},{1,97},{33,1},{65,33},{97,65},{2,98}... | collective-permute-start | bytes 417800 | tf_op jit(solution)/shard_map/ppermute | solution.py:367
  35.9 14.1 %collective-permute-start.16 = (bf16[144,768]{1,0:T(8,128)(2,1)S(1)}, bf16[144,768]{1,0:T(8,128)(2,1)S(1)}, u32[]{:S(2)}, u32[]{:S(2)}) collective-permute-start(bf16[144,768]{1,0:T(8,128)(2,1)S(1)} %get-tuple-element.82), channel_id=1, source_target_pairs={{0,2},{2,4},{4,6},{6,0},{1,3},{3,5},{5,7},{7,1},{8,10},{10,12},{12... | collective-permute-start | bytes 663560 | tf_op jit(solution)/shard_map/ppermute | solution.py:367
  36.9 6.7 %collective-permute-start.11 = (f32[136,256]{1,0:T(8,128)S(1)}, f32[136,256]{1,0:T(8,128)S(1)}, u32[]{:S(2)}, u32[]{:S(2)}) collective-permute-start(f32[136,256]{1,0:T(8,128)S(1)} %get-tuple-element.75.refs_1_), channel_id=1, source_target_pairs={{0,64},{32,96},{64,0},{96,32},{1,65},{33,97},{65,1},{97,33},{2,66}... | collective-permute-start | bytes 417800 | tf_op jit(solution)/shard_map/ppermute | solution.py:367
  37.6 7.5 %collective-permute-start.10 = (f32[136,256]{1,0:T(8,128)S(1)}, f32[136,256]{1,0:T(8,128)S(1)}, u32[]{:S(2)}, u32[]{:S(2)}) collective-permute-start(f32[136,256]{1,0:T(8,128)S(1)} %get-tuple-element.75.refs_1_), channel_id=1, source_target_pairs={{0,32},{32,64},{64,96},{96,0},{1,33},{33,65},{65,97},{97,1},{2,34}... | collective-permute-start | bytes 417800 | tf_op jit(solution)/shard_map/ppermute | solution.py:367
  38.5 12.4 %collective-permute-start.17 = (bf16[144,768]{1,0:T(8,128)(2,1)S(1)}, bf16[144,768]{1,0:T(8,128)(2,1)S(1)}, u32[]{:S(2)}, u32[]{:S(2)}) collective-permute-start(bf16[144,768]{1,0:T(8,128)(2,1)S(1)} %get-tuple-element.83), channel_id=1, source_target_pairs={{0,4},{2,6},{4,0},{6,2},{1,5},{3,7},{5,1},{7,3},{8,12},{10,14},{12... | collective-permute-start | bytes 663560 | tf_op jit(solution)/shard_map/ppermute | solution.py:367
  41.5 9.4 %collective-permute-start.18 = (bf16[144,768]{1,0:T(8,128)(2,1)S(1)}, bf16[144,768]{1,0:T(8,128)(2,1)S(1)}, u32[]{:S(2)}, u32[]{:S(2)}) collective-permute-start(bf16[144,768]{1,0:T(8,128)(2,1)S(1)} %get-tuple-element.84), channel_id=1, source_target_pairs={{0,6},{2,0},{4,2},{6,4},{1,7},{3,1},{5,3},{7,5},{8,14},{10,8},{12,... | collective-permute-start | bytes 663560 | tf_op jit(solution)/shard_map/ppermute | solution.py:367
  45.8 8.3 %collective-permute-start.13 = (f32[128,256]{1,0:T(8,128)S(1)}, f32[128,256]{1,0:T(8,128)S(1)}, u32[]{:S(2)}, u32[]{:S(2)}) collective-permute-start(f32[128,256]{1,0:T(8,128)S(1)} %get-tuple-element.78), channel_id=1, source_target_pairs={{0,8},{8,16},{16,24},{24,0},{1,9},{9,17},{17,25},{25,1},{2,10},{10... | collective-permute-start | bytes 393224 | tf_op jit(solution)/shard_map/ppermute | solution.py:367
  48.1 7.6 %collective-permute-start.14 = (f32[128,256]{1,0:T(8,128)S(1)}, f32[128,256]{1,0:T(8,128)S(1)}, u32[]{:S(2)}, u32[]{:S(2)}) collective-permute-start(f32[128,256]{1,0:T(8,128)S(1)} %get-tuple-element.79), channel_id=1, source_target_pairs={{0,16},{8,24},{16,0},{24,8},{1,17},{9,25},{17,1},{25,9},{2,18},{10... | collective-permute-start | bytes 393224 | tf_op jit(solution)/shard_map/ppermute | solution.py:367
  50.0 5.7 %collective-permute-start.15 = (f32[128,256]{1,0:T(8,128)S(1)}, f32[128,256]{1,0:T(8,128)S(1)}, u32[]{:S(2)}, u32[]{:S(2)}) collective-permute-start(f32[128,256]{1,0:T(8,128)S(1)} %get-tuple-element.80), channel_id=1, source_target_pairs={{0,24},{8,0},{16,8},{24,16},{1,25},{9,1},{17,9},{25,17},{2,26},{10... | collective-permute-start | bytes 393224 | tf_op jit(solution)/shard_map/ppermute | solution.py:367
  58.0 10.6 %collective-permute-start.19 = (bf16[144,768]{1,0:T(8,128)(2,1)S(1)}, bf16[144,768]{1,0:T(8,128)(2,1)S(1)}, u32[]{:S(2)}, u32[]{:S(2)}) collective-permute-start(bf16[144,768]{1,0:T(8,128)(2,1)S(1)} %get-tuple-element.95), channel_id=1, source_target_pairs={{0,2},{2,4},{4,6},{6,0},{1,3},{3,5},{5,7},{7,1},{8,10},{10,12},{12... | collective-permute-start | bytes 663560 | tf_op jit(solution)/shard_map/ppermute | solution.py:367
  59.3 11.0 %collective-permute-start.20 = (bf16[144,768]{1,0:T(8,128)(2,1)S(1)}, bf16[144,768]{1,0:T(8,128)(2,1)S(1)}, u32[]{:S(2)}, u32[]{:S(2)}) collective-permute-start(bf16[144,768]{1,0:T(8,128)(2,1)S(1)} %get-tuple-element.96), channel_id=1, source_target_pairs={{0,4},{2,6},{4,0},{6,2},{1,5},{3,7},{5,1},{7,3},{8,12},{10,14},{12... | collective-permute-start | bytes 663560 | tf_op jit(solution)/shard_map/ppermute | solution.py:367
  61.6 9.0 %collective-permute-start.21 = (bf16[144,768]{1,0:T(8,128)(2,1)S(1)}, bf16[144,768]{1,0:T(8,128)(2,1)S(1)}, u32[]{:S(2)}, u32[]{:S(2)}) collective-permute-start(bf16[144,768]{1,0:T(8,128)(2,1)S(1)} %get-tuple-element.97), channel_id=1, source_target_pairs={{0,6},{2,0},{4,2},{6,4},{1,7},{3,1},{5,3},{7,5},{8,14},{10,8},{12,... | collective-permute-start | bytes 663560 | tf_op jit(solution)/shard_map/ppermute | solution.py:367
  63.8 14.5 %all-to-all-start = ((f32[64,2,128]{2,1,0:T(2,128)}), f32[64,2,128]{2,1,0:T(2,128)S(1)}, u32[]{:S(2)}, u32[]{:S(2)}) async-start(f32[64,2,128]{2,1,0:T(2,128)} %get-tuple-element.101), calls=%async_computation | async-start | bytes 131072 | tf_op jit(solution)/shard_map/all_to_all | solution.py:467
  (2 other events, 23.8 us)

commit v5 on v4

--- a/solution.py
+++ b/solution.py
@@ -56,16 +56,22 @@
     return jax.ShapeDtypeStruct(shape, dtype)
 
 
+def placed_kernel(body):
+    def run(*refs):
+        return body(tuple(lax.axis_index(axis) for axis in (X, Z, Y, H)), *refs)
+
+    return run
+
+
 def call(body, outs, n_in, scratch=(), after=()):
-    specs = [pl.BlockSpec(memory_space=pltpu.SMEM)]
-    specs += [pl.BlockSpec(memory_space=pltpu.VMEM)] * n_in
+    specs = [pl.BlockSpec(memory_space=pltpu.VMEM)] * n_in
     specs += [pl.BlockSpec(memory_space=pl.ANY)] * len(after)
 
-    def ordered(*refs):
-        return body(*refs[: 1 + n_in], *refs[1 + n_in + len(after) :])
+    def ordered(idx, *refs):
+        return body(idx, *refs[:n_in], *refs[n_in + len(after) :])
 
     run = pl.pallas_call(
-        ordered,
+        placed_kernel(ordered),
         out_shape=outs,
         in_specs=specs,
         scratch_shapes=list(scratch),
@@ -375,16 +381,14 @@
 
 
 def whole(query, key, value, out_grad, log_decay, checkpoints):
-    x, z, y, c = (lax.axis_index(axis) for axis in (X, Z, Y, H))
-    idx = jnp.stack([x, z, y, c]).astype(jnp.int32)
     vm = pltpu.VMEM
 
     half = TOK // 2
     hbm = pl.BlockSpec(memory_space=pltpu.HBM)
     *qa, send, keep = pl.pallas_call(
-        pack_first,
+        placed_kernel(pack_first),
         out_shape=[sds((TOK, 2 * DK))] * 4 + [sds((NH, half, DV))] * 2,
-        in_specs=[pl.BlockSpec(memory_space=pltpu.SMEM), hbm, hbm, hbm],
+        in_specs=[hbm, hbm, hbm],
         scratch_shapes=[
             vm((half, 2 * NH, DV), B16),
             vm((TOK, NH, DK), B16),
@@ -395,34 +399,32 @@
         ],
         name="pack_first",
         compiler_params=pltpu.CompilerParams(vmem_limit_bytes=16 * 1024 * 1024),
-    )(idx, *(pltpu.with_memory_space_constraint(a, pltpu.HBM) for a in (out_grad, query, log_decay)))
+    )(*(pltpu.with_memory_space_constraint(a, pltpu.HBM) for a in (out_grad, query, log_decay)))
     recv = lax.ppermute(send, H, [(0, 1), (1, 0)])
     qa_line = spread(qa, X)
-    g = call(join_grad, [sds((TOK, DV))] * 4, 2, ())(idx, keep, recv)
+    g = call(join_grad, [sds((TOK, DV))] * 4, 2, ())(keep, recv)
     g_line = spread(g, X)
-    kv = call(
-        pack_pair, [sds((TOK, DK + DV))] * 4, 2, [vm((NH, TOK, DK + DV), B16)]
-    )(idx, key, value)
+    kv = call(pack_pair, [sds((TOK, DK + DV))] * 4, 2, [vm((NH, TOK, DK + DV), B16)])(key, value)
     res = call(
         query_part,
         [sds((TOK, NH, DK)), sds((NH, TOK, DK), F32)] + [sds((TOK + 16, DK + DV))] * 4,
         13,
         [vm((NH, TOK, DK), F32)],
-    )(idx, *qa, *g, *kv, checkpoints)
+    )(*qa, *g, *kv, checkpoints)
     dq, qdq, kv = res[0], res[1], res[2:]
     rise, cum, logs = call(
         line_prep,
         [sds((4 * TOK, 2 * DK)), sds((4 * TOK, DK), F32), sds((8, DK), F32)],
         4,
         [vm((4 * TOK, 2 * DK), B16)],
-    )(idx, *qa_line)
+    )(*qa_line)
     *chunks, g_rows = call(
         line_state,
         [sds((TOK + 8, DK), F32)] * 4 + [sds((4 * TOK, DV))],
         6,
         [vm((DV, DK), F32)],
         (qdq,),
-    )(idx, *g_line, rise, logs)
+    )(*g_line, rise, logs)
     z_in = spread(chunks, Z)
     kv_line = spread(kv, X)
     total, suffix = call(
@@ -430,11 +432,11 @@
         [sds((TOK + 8, DK), F32), sds((4, TOK + 8, DK), F32)],
         4,
         [vm((4, TOK + 8, DK), F32)],
-    )(idx, *z_in)
+    )(*z_in)
     y_in = spread([total] * 4, Y)
     *carry, token = call(
         scan_y, [sds((TOK, DK), F32)] * 4 + [sds((8, 128), F32)], 5, [vm((4, TOK + 8, DK), F32)]
-    )(idx, *y_in, suffix)
+    )(*y_in, suffix)
     carry_in = spread(carry, Z)
     near = call(
         near_part,
@@ -449,7 +451,7 @@
         7,
         (),
         (token,),
-    )(idx, g_rows, rise, cum, *kv_line)
+    )(g_rows, rise, cum, *kv_line)
     res = call(
         far_part,
         [sds((TOK + GROUPS, DK + DV))] * 4 + [sds((64, 2, 128), F32)],
@@ -461,7 +463,7 @@
             vm((4, GROUPS, DK + DV), B16),
             vm((4, DK), F32),
         ],
-    )(idx, *carry_in, *kv_line, *near)
+    )(*carry_in, *kv_line, *near)
     back, sums = res[:4], res[4]
     back_in = spread(back, X)
     sums = lax.all_to_all(sums, SEQ, split_axis=0, concat_axis=0, tiled=True)
@@ -475,17 +477,17 @@
             vm((NH, TOK, DK), B16),
             vm((NH, TOK, DK), F32),
         ],
-    )(idx, *back_in, qdq, key)
+    )(*back_in, qdq, key)
     vmem = pl.BlockSpec(memory_space=pltpu.VMEM)
     da = pl.pallas_call(
-        decay_part,
+        placed_kernel(decay_part),
         out_shape=sds((TOK, NH, DK)),
-        in_specs=[pl.BlockSpec(memory_space=pltpu.SMEM), vmem, vmem],
+        in_specs=[vmem, vmem],
         out_specs=hbm,
         scratch_shapes=[vm((TOK, NH, DK), B16), pltpu.SemaphoreType.DMA((2,))],
         name="decay_part",
         compiler_params=pltpu.CompilerParams(vmem_limit_bytes=16 * 1024 * 1024),
-    )(idx, da_part, sums)
+    )(da_part, sums)
     return dq, dk, dv, da
 
 

time: 79.9 us -> 76.6 us (0.959)
  Pallas kernels: 18.5 us -> 12.2 us
  waiting for transfers between devices: 17.8 us -> 20.2 us
  local copies, waits for them, and re-layouts: 0.01 us -> 1.05 us
    pallas_call x10, Pallas kernels: 15.3 us -> 9.98 us  [call(): return lambda *operands: run(*operands, *after)]
    ppermute x21, waiting for transfers between devices: 12.5 us -> 14.4 us  [shifted(): return lax.ppermute(value, axis, [(i, (i + s) % 4) for i in range(4)])]
    unnamed x6, local copies, waits for them, and re-layouts: 0.01 us -> 1.05 us
    pallas_call x2, Pallas kernels: 3.23 us -> 2.25 us  [the longest x1 1.47 us: whole(): pl.pallas_call(placed_kernel(pack_first), out_shape=[sds((TOK, 2 * DK))]...]
  transfers between devices with their start and end apart: 23 -> 23, of which waited for: 10 -> 11; matrix products, arithmetic and copies ran while one was open for 0% -> 0% of each run, Pallas kernels for 14% -> 10%
where the time goes in v5:
time: 76.6 us; the launch traced here: 76.4 us
  starting transfers between devices  42 us (55%)
  waiting for transfers between devices  20.2 us (26%)
  Pallas kernels  12.2 us (16%)
  local copies, waits for them, and re-layouts  1.05 us (1%)
  between operations  0.91 us (1%)
    ppermute x21, starting transfers between devices, shifted(): return lax.ppermute(value, axis, [(i, (i + s) % 4) for i in range(4)])  36.8 us
    ppermute x21, waiting for transfers between devices, shifted(): return lax.ppermute(value, axis, [(i, (i + s) % 4) for i in range(4)])  14.4 us
    pallas_call x10, Pallas kernels, call(): return lambda *operands: run(*operands, *after)  9.98 us
    all_to_all x1, waiting for transfers between devices, whole(): sums = lax.all_to_all(sums, SEQ, split_axis=0, concat_axis=0, tiled=True)  5.76 us
    all_to_all x1, starting transfers between devices, whole(): sums = lax.all_to_all(sums, SEQ, split_axis=0, concat_axis=0, tiled=True)  5.1 us
  transfers between devices with their start and end apart: 23, of which 11 were waited for; matrix products, arithmetic and copies ran while one was open for 0% of the time, Pallas kernels for 10%

profile of v5, /device:TPU:0, one launch (start us, length us, event | category | flops | bytes accessed | tf_op | source)
XLA Modules:
  0.0 76.4 jit_solution(16852973294075525780)
XLA Ops:
  0.6 1.5 %pack_first.1 = (bf16[128,512]{1,0:T(8,128)(2,1)S(1)}, bf16[128,512]{1,0:T(8,128)(2,1)S(1)}, bf16[128,512]{1,0:T(8,128)(2,1)S(1)}, bf16[128,512]{1,0:T(8,128)(2,...) custom-call(bf16[64,8,512]{2,1,0:T(8,128)(2,1)} %refs_0_.2, bf16[128,4,256]{2,1,0:T(4,128)(2,1)} %refs_1_.2, ...), custom_call_target="tpu_custom_call" | custom-call | tf_op jit(solution)/shard_map/pack_first/pallas_call | solution.py:388
  2.2 1.7 %collective-permute-start.4 = (bf16[128,512]{1,0:T(8,128)(2,1)S(1)}, bf16[128,512]{1,0:T(8,128)(2,1)S(1)}, u32[]{:S(2)}, u32[]{:S(2)}) collective-permute-start(bf16[128,512]{1,0:T(8,128)(2,1)S(1)} %get-tuple-element.54.refs_1_), channel_id=1, source_target_pairs={{0,2},{2,4},{4,6},{6,0},{1,3},{3,5},{5,7},{7,1},{8,10},{10,12},{12... | collective-permute-start | bytes 393224 | tf_op jit(solution)/shard_map/ppermute | solution.py:373
  3.9 2.7 %collective-permute-start.5 = (bf16[128,512]{1,0:T(8,128)(2,1)S(1)}, bf16[128,512]{1,0:T(8,128)(2,1)S(1)}, u32[]{:S(2)}, u32[]{:S(2)}) collective-permute-start(bf16[128,512]{1,0:T(8,128)(2,1)S(1)} %get-tuple-element.55.refs_2_), channel_id=1, source_target_pairs={{0,4},{2,6},{4,0},{6,2},{1,5},{3,7},{5,1},{7,3},{8,12},{10,14},{12... | collective-permute-start | bytes 393224 | tf_op jit(solution)/shard_map/ppermute | solution.py:373
  6.6 1.4 %collective-permute-start.6 = (bf16[128,512]{1,0:T(8,128)(2,1)S(1)}, bf16[128,512]{1,0:T(8,128)(2,1)S(1)}, u32[]{:S(2)}, u32[]{:S(2)}) collective-permute-start(bf16[128,512]{1,0:T(8,128)(2,1)S(1)} %get-tuple-element.56.refs_3_), channel_id=1, source_target_pairs={{0,6},{2,0},{4,2},{6,4},{1,7},{3,1},{5,3},{7,5},{8,14},{10,8},{12,... | collective-permute-start | bytes 393224 | tf_op jit(solution)/shard_map/ppermute | solution.py:373
  9.7 1.9 %collective-permute-start.3 = (bf16[128,512]{1,0:T(8,128)(2,1)S(1)}, bf16[128,512]{1,0:T(8,128)(2,1)S(1)}, u32[]{:S(2)}, u32[]{:S(2)}) collective-permute-start(bf16[128,512]{1,0:T(8,128)(2,1)S(1)} %get-tuple-element.62.refs_7_), channel_id=1, source_target_pairs={{0,6},{2,0},{4,2},{6,4},{1,7},{3,1},{5,3},{7,5},{8,14},{10,8},{12,... | collective-permute-start | bytes 393224 | tf_op jit(solution)/shard_map/ppermute | solution.py:373
  14.3 2.3 %shard_map.95 = (bf16[128,4,256]{2,1,0:T(4,128)(2,1)}, f32[4,128,256]{2,1,0:T(8,128)S(1)}, bf16[144,768]{1,0:T(8,128)(2,1)S(1)}, bf16[144,768]{1,0:T(8,128)(2,1)...) custom-call(bf16[128,512]{1,0:T(8,128)(2,1)S(1)} %get-tuple-element.53.refs_0_, ...), custom_call_target="tpu_custom_call" | custom-call | tf_op jit(solution)/shard_map/pallas_call | solution.py:80
  16.6 2.2 %collective-permute-done.2.refs_2_ = bf16[128,512]{1,0:T(8,128)(2,1)S(1)} collective-permute-done((bf16[128,512]{1,0:T(8,128)(2,1)S(1)}, bf16[128,512]{1,0:T(8,128)(2,1)S(1)}, u32[]{:S(2)}, u32[]{:S(2)}) %collective-permute-start.2) | collective-permute-done | bytes 131104 | tf_op jit(solution)/shard_map/ppermute | solution.py:373
  19.4 2.0 %collective-permute-start.7 = (f32[136,256]{1,0:T(8,128)S(1)}, f32[136,256]{1,0:T(8,128)S(1)}, u32[]{:S(2)}, u32[]{:S(2)}) collective-permute-start(f32[136,256]{1,0:T(8,128)S(1)} %get-tuple-element.72), channel_id=1, source_target_pairs={{0,8},{8,16},{16,24},{24,0},{1,9},{9,17},{17,25},{25,1},{2,10},{10... | collective-permute-start | bytes 417800 | tf_op jit(solution)/shard_map/ppermute | solution.py:373
  21.4 3.6 %collective-permute-start.8 = (f32[136,256]{1,0:T(8,128)S(1)}, f32[136,256]{1,0:T(8,128)S(1)}, u32[]{:S(2)}, u32[]{:S(2)}) collective-permute-start(f32[136,256]{1,0:T(8,128)S(1)} %get-tuple-element.73), channel_id=1, source_target_pairs={{0,16},{8,24},{16,0},{24,8},{1,17},{9,25},{17,1},{25,9},{2,18},{10... | collective-permute-start | bytes 417800 | tf_op jit(solution)/shard_map/ppermute | solution.py:373
  27.1 3.9 %collective-permute-done.8.refs_2_ = f32[136,256]{1,0:T(8,128)S(1)} collective-permute-done((f32[136,256]{1,0:T(8,128)S(1)}, f32[136,256]{1,0:T(8,128)S(1)}, u32[]{:S(2)}, u32[]{:S(2)}) %collective-permute-start.8) | collective-permute-done | bytes 139296 | tf_op jit(solution)/shard_map/ppermute | solution.py:373
  31.2 3.1 %collective-permute-start.12 = (f32[136,256]{1,0:T(8,128)S(1)}, f32[136,256]{1,0:T(8,128)S(1)}, u32[]{:S(2)}, u32[]{:S(2)}) collective-permute-start(f32[136,256]{1,0:T(8,128)S(1)} %get-tuple-element.75.refs_0_), channel_id=1, source_target_pairs={{0,96},{32,0},{64,32},{96,64},{1,97},{33,1},{65,33},{97,65},{2,98}... | collective-permute-start | bytes 417800 | tf_op jit(solution)/shard_map/ppermute | solution.py:373
  37.1 2.6 %collective-permute-start.17 = (bf16[144,768]{1,0:T(8,128)(2,1)S(1)}, bf16[144,768]{1,0:T(8,128)(2,1)S(1)}, u32[]{:S(2)}, u32[]{:S(2)}) collective-permute-start(bf16[144,768]{1,0:T(8,128)(2,1)S(1)} %get-tuple-element.83), channel_id=1, source_target_pairs={{0,4},{2,6},{4,0},{6,2},{1,5},{3,7},{5,1},{7,3},{8,12},{10,14},{12... | collective-permute-start | bytes 663560 | tf_op jit(solution)/shard_map/ppermute | solution.py:373
  39.7 2.1 %collective-permute-start.18 = (bf16[144,768]{1,0:T(8,128)(2,1)S(1)}, bf16[144,768]{1,0:T(8,128)(2,1)S(1)}, u32[]{:S(2)}, u32[]{:S(2)}) collective-permute-start(bf16[144,768]{1,0:T(8,128)(2,1)S(1)} %get-tuple-element.84), channel_id=1, source_target_pairs={{0,6},{2,0},{4,2},{6,4},{1,7},{3,1},{5,3},{7,5},{8,14},{10,8},{12,... | collective-permute-start | bytes 663560 | tf_op jit(solution)/shard_map/ppermute | solution.py:373
  43.8 2.4 %collective-permute-start.13 = (f32[128,256]{1,0:T(8,128)S(1)}, f32[128,256]{1,0:T(8,128)S(1)}, u32[]{:S(2)}, u32[]{:S(2)}) collective-permute-start(f32[128,256]{1,0:T(8,128)S(1)} %get-tuple-element.78), channel_id=1, source_target_pairs={{0,8},{8,16},{16,24},{24,0},{1,9},{9,17},{17,25},{25,1},{2,10},{10... | collective-permute-start | bytes 393224 | tf_op jit(solution)/shard_map/ppermute | solution.py:373
  46.1 2.0 %collective-permute-start.14 = (f32[128,256]{1,0:T(8,128)S(1)}, f32[128,256]{1,0:T(8,128)S(1)}, u32[]{:S(2)}, u32[]{:S(2)}) collective-permute-start(f32[128,256]{1,0:T(8,128)S(1)} %get-tuple-element.79), channel_id=1, source_target_pairs={{0,16},{8,24},{16,0},{24,8},{1,17},{9,25},{17,1},{25,9},{2,18},{10... | collective-permute-start | bytes 393224 | tf_op jit(solution)/shard_map/ppermute | solution.py:373
  48.9 2.7 %shard_map.100 = (f32[512,256]{1,0:T(8,128)S(1)}, f32[512,512]{1,0:T(8,128)S(1)}, bf16[512,768]{1,0:T(8,128)(2,1)S(1)}, f32[512,256]{1,0:T(8,128)S(1)}, bf16[512...) custom-call(bf16[512,512]{1,0:T(8,128)(2,1)S(1)} %get-tuple-element.85.refs_0_, ...), custom_call_target="tpu_custom_call" | custom-call | tf_op jit(solution)/shard_map/pallas_call | solution.py:80
  51.6 2.1 %collective-permute-done.14.refs_2_ = f32[128,256]{1,0:T(8,128)S(1)} collective-permute-done((f32[128,256]{1,0:T(8,128)S(1)}, f32[128,256]{1,0:T(8,128)S(1)}, u32[]{:S(2)}, u32[]{:S(2)}) %collective-permute-start.14) | collective-permute-done | bytes 131104 | tf_op jit(solution)/shard_map/ppermute | solution.py:373
  53.7 1.7 %shard_map.101 = (bf16[144,768]{1,0:T(8,128)(2,1)S(1)}, bf16[144,768]{1,0:T(8,128)(2,1)S(1)}, bf16[144,768]{1,0:T(8,128)(2,1)S(1)}, bf16[144,768]{1,0:T(8,128)(2,1)S(1)}, f32[64,2,128]{2,1,0:T(2,128)}) custom-call(f32[128,256]{1,0:T(8,128)S(1)} %get-tuple-element.77.refs_0_, f32[128,256]{1,0:T(8,128)S(1)} %collective-permute-done.13.refs_1_, ...), custom_call_target="tpu_custom_call" | custom-call | tf_op jit(solution)/shard_map/pallas_call | solution.py:80
  56.6 2.4 %collective-permute-start.20 = (bf16[144,768]{1,0:T(8,128)(2,1)S(1)}, bf16[144,768]{1,0:T(8,128)(2,1)S(1)}, u32[]{:S(2)}, u32[]{:S(2)}) collective-permute-start(bf16[144,768]{1,0:T(8,128)(2,1)S(1)} %get-tuple-element.96), channel_id=1, source_target_pairs={{0,4},{2,6},{4,0},{6,2},{1,5},{3,7},{5,1},{7,3},{8,12},{10,14},{12... | collective-permute-start | bytes 663560 | tf_op jit(solution)/shard_map/ppermute | solution.py:373
  59.0 1.8 %collective-permute-start.21 = (bf16[144,768]{1,0:T(8,128)(2,1)S(1)}, bf16[144,768]{1,0:T(8,128)(2,1)S(1)}, u32[]{:S(2)}, u32[]{:S(2)}) collective-permute-start(bf16[144,768]{1,0:T(8,128)(2,1)S(1)} %get-tuple-element.97), channel_id=1, source_target_pairs={{0,6},{2,0},{4,2},{6,4},{1,7},{3,1},{5,3},{7,5},{8,14},{10,8},{12,... | collective-permute-start | bytes 663560 | tf_op jit(solution)/shard_map/ppermute | solution.py:373
  60.8 5.1 %all-to-all-start = ((f32[64,2,128]{2,1,0:T(2,128)}), f32[64,2,128]{2,1,0:T(2,128)S(1)}, u32[]{:S(2)}, u32[]{:S(2)}) async-start(f32[64,2,128]{2,1,0:T(2,128)} %get-tuple-element.101), calls=%async_computation | async-start | bytes 131072 | tf_op jit(solution)/shard_map/all_to_all | solution.py:469
  65.9 1.5 %collective-permute-done.20.refs_2_ = bf16[144,768]{1,0:T(8,128)(2,1)S(1)} collective-permute-done((bf16[144,768]{1,0:T(8,128)(2,1)S(1)}, bf16[144,768]{1,0:T(8,128)(2,1)S(1)}, u32[]{:S(2)}, u32[]{:S(2)}) %collective-permute-start.20) | collective-permute-done | bytes 221216 | tf_op jit(solution)/shard_map/ppermute | solution.py:373
  67.9 1.8 %shard_map.102 = (bf16[128,4,256]{2,1,0:T(4,128)(2,1)}, bf16[128,4,512]{2,1,0:T(4,128)(2,1)}, f32[128,4,256]{2,1,0:T(4,128)S(1)}) custom-call(bf16[144,768]{1,0:T(8,128)(2,1)S(1)} %get-tuple-element.94.refs_0_, bf16[144,768]{1,0:T(8,128)(2,1)S(1)} %collective-permute-done.19.refs_1_, bf16[144,768]{1,0:T(8,128)(2,1)S(1)} %collective-permute-done.20.refs_2_, ...), custom_call_target="tpu_custom_call" | custom-call | tf_op jit(solution)/shard_map/pallas_call | solution.py:80
  69.7 5.8 %all-to-all-done.refs_1_ = f32[64,2,128]{2,1,0:T(2,128)S(1)} async-done(((f32[64,2,128]{2,1,0:T(2,128)}), f32[64,2,128]{2,1,0:T(2,128)S(1)}, u32[]{:S(2)}, u32[]{:S(2)}) %all-to-all-start) | async-done | bytes 65568 | tf_op jit(solution)/shard_map/all_to_all | solution.py:469
  (40 shorter events, 15.3 us)
Async XLA Ops:
  0.6 13.7 %copy-start.1 = (bf16[1,4,256,512]{3,2,1,0:T(8,128)(2,1)S(1)}, bf16[1,4,256,512]{3,2,1,0:T(8,128)(2,1)}, u32[]{:S(2)}) copy-start(bf16[1,4,256,512]{3,2,1,0:T(8,128)(2,1)} %refs_12_.1) | copy-start | bytes 3145732
  2.1 5.9 %collective-permute-start = (bf16[4,64,512]{2,1,0:T(8,128)(2,1)S(1)}, bf16[4,64,512]{2,1,0:T(8,128)(2,1)S(1)}, u32[]{:S(2)}, u32[]{:S(2)}) collective-permute-start(bf16[4,64,512]{2,1,0:T(8,128)(2,1)S(1)} %get-tuple-element.58), channel_id=1, source_target_pairs={{0,1},{1,0},{2,3},{3,2},{4,5},{5,4},{6,7},{7,6},{8,9},{9,8},{10,11... | collective-permute-start | bytes 786440 | tf_op jit(solution)/shard_map/ppermute | solution.py:403
  2.2 7.4 %collective-permute-start.4 = (bf16[128,512]{1,0:T(8,128)(2,1)S(1)}, bf16[128,512]{1,0:T(8,128)(2,1)S(1)}, u32[]{:S(2)}, u32[]{:S(2)}) collective-permute-start(bf16[128,512]{1,0:T(8,128)(2,1)S(1)} %get-tuple-element.54.refs_1_), channel_id=1, source_target_pairs={{0,2},{2,4},{4,6},{6,0},{1,3},{3,5},{5,7},{7,1},{8,10},{10,12},{12... | collective-permute-start | bytes 393224 | tf_op jit(solution)/shard_map/ppermute | solution.py:373
  3.9 9.9 %collective-permute-start.5 = (bf16[128,512]{1,0:T(8,128)(2,1)S(1)}, bf16[128,512]{1,0:T(8,128)(2,1)S(1)}, u32[]{:S(2)}, u32[]{:S(2)}) collective-permute-start(bf16[128,512]{1,0:T(8,128)(2,1)S(1)} %get-tuple-element.55.refs_2_), channel_id=1, source_target_pairs={{0,4},{2,6},{4,0},{6,2},{1,5},{3,7},{5,1},{7,3},{8,12},{10,14},{12... | collective-permute-start | bytes 393224 | tf_op jit(solution)/shard_map/ppermute | solution.py:373
  6.6 7.3 %collective-permute-start.6 = (bf16[128,512]{1,0:T(8,128)(2,1)S(1)}, bf16[128,512]{1,0:T(8,128)(2,1)S(1)}, u32[]{:S(2)}, u32[]{:S(2)}) collective-permute-start(bf16[128,512]{1,0:T(8,128)(2,1)S(1)} %get-tuple-element.56.refs_3_), channel_id=1, source_target_pairs={{0,6},{2,0},{4,2},{6,4},{1,7},{3,1},{5,3},{7,5},{8,14},{10,8},{12,... | collective-permute-start | bytes 393224 | tf_op jit(solution)/shard_map/ppermute | solution.py:373
  8.1 8.5 %collective-permute-start.1 = (bf16[128,512]{1,0:T(8,128)(2,1)S(1)}, bf16[128,512]{1,0:T(8,128)(2,1)S(1)}, u32[]{:S(2)}, u32[]{:S(2)}) collective-permute-start(bf16[128,512]{1,0:T(8,128)(2,1)S(1)} %get-tuple-element.60.refs_5_), channel_id=1, source_target_pairs={{0,2},{2,4},{4,6},{6,0},{1,3},{3,5},{5,7},{7,1},{8,10},{10,12},{12... | collective-permute-start | bytes 393224 | tf_op jit(solution)/shard_map/ppermute | solution.py:373
  8.8 10.1 %collective-permute-start.2 = (bf16[128,512]{1,0:T(8,128)(2,1)S(1)}, bf16[128,512]{1,0:T(8,128)(2,1)S(1)}, u32[]{:S(2)}, u32[]{:S(2)}) collective-permute-start(bf16[128,512]{1,0:T(8,128)(2,1)S(1)} %get-tuple-element.61.refs_6_), channel_id=1, source_target_pairs={{0,4},{2,6},{4,0},{6,2},{1,5},{3,7},{5,1},{7,3},{8,12},{10,14},{12... | collective-permute-start | bytes 393224 | tf_op jit(solution)/shard_map/ppermute | solution.py:373
  9.7 9.2 %collective-permute-start.3 = (bf16[128,512]{1,0:T(8,128)(2,1)S(1)}, bf16[128,512]{1,0:T(8,128)(2,1)S(1)}, u32[]{:S(2)}, u32[]{:S(2)}) collective-permute-start(bf16[128,512]{1,0:T(8,128)(2,1)S(1)} %get-tuple-element.62.refs_7_), channel_id=1, source_target_pairs={{0,6},{2,0},{4,2},{6,4},{1,7},{3,1},{5,3},{7,5},{8,14},{10,8},{12,... | collective-permute-start | bytes 393224 | tf_op jit(solution)/shard_map/ppermute | solution.py:373
  19.4 7.7 %collective-permute-start.7 = (f32[136,256]{1,0:T(8,128)S(1)}, f32[136,256]{1,0:T(8,128)S(1)}, u32[]{:S(2)}, u32[]{:S(2)}) collective-permute-start(f32[136,256]{1,0:T(8,128)S(1)} %get-tuple-element.72), channel_id=1, source_target_pairs={{0,8},{8,16},{16,24},{24,0},{1,9},{9,17},{17,25},{25,1},{2,10},{10... | collective-permute-start | bytes 417800 | tf_op jit(solution)/shard_map/ppermute | solution.py:373
  21.4 9.7 %collective-permute-start.8 = (f32[136,256]{1,0:T(8,128)S(1)}, f32[136,256]{1,0:T(8,128)S(1)}, u32[]{:S(2)}, u32[]{:S(2)}) collective-permute-start(f32[136,256]{1,0:T(8,128)S(1)} %get-tuple-element.73), channel_id=1, source_target_pairs={{0,16},{8,24},{16,0},{24,8},{1,17},{9,25},{17,1},{25,9},{2,18},{10... | collective-permute-start | bytes 417800 | tf_op jit(solution)/shard_map/ppermute | solution.py:373
  25.0 6.1 %collective-permute-start.9 = (f32[136,256]{1,0:T(8,128)S(1)}, f32[136,256]{1,0:T(8,128)S(1)}, u32[]{:S(2)}, u32[]{:S(2)}) collective-permute-start(f32[136,256]{1,0:T(8,128)S(1)} %get-tuple-element.74), channel_id=1, source_target_pairs={{0,24},{8,0},{16,8},{24,16},{1,25},{9,1},{17,9},{25,17},{2,26},{10... | collective-permute-start | bytes 417800 | tf_op jit(solution)/shard_map/ppermute | solution.py:373
  31.2 8.5 %collective-permute-start.12 = (f32[136,256]{1,0:T(8,128)S(1)}, f32[136,256]{1,0:T(8,128)S(1)}, u32[]{:S(2)}, u32[]{:S(2)}) collective-permute-start(f32[136,256]{1,0:T(8,128)S(1)} %get-tuple-element.75.refs_0_), channel_id=1, source_target_pairs={{0,96},{32,0},{64,32},{96,64},{1,97},{33,1},{65,33},{97,65},{2,98}... | collective-permute-start | bytes 417800 | tf_op jit(solution)/shard_map/ppermute | solution.py:373
  34.3 13.9 %collective-permute-start.16 = (bf16[144,768]{1,0:T(8,128)(2,1)S(1)}, bf16[144,768]{1,0:T(8,128)(2,1)S(1)}, u32[]{:S(2)}, u32[]{:S(2)}) collective-permute-start(bf16[144,768]{1,0:T(8,128)(2,1)S(1)} %get-tuple-element.82), channel_id=1, source_target_pairs={{0,2},{2,4},{4,6},{6,0},{1,3},{3,5},{5,7},{7,1},{8,10},{10,12},{12... | collective-permute-start | bytes 663560 | tf_op jit(solution)/shard_map/ppermute | solution.py:373
  35.5 6.7 %collective-permute-start.11 = (f32[136,256]{1,0:T(8,128)S(1)}, f32[136,256]{1,0:T(8,128)S(1)}, u32[]{:S(2)}, u32[]{:S(2)}) collective-permute-start(f32[136,256]{1,0:T(8,128)S(1)} %get-tuple-element.75.refs_0_), channel_id=1, source_target_pairs={{0,64},{32,96},{64,0},{96,32},{1,65},{33,97},{65,1},{97,33},{2,66}... | collective-permute-start | bytes 417800 | tf_op jit(solution)/shard_map/ppermute | solution.py:373
  36.1 7.5 %collective-permute-start.10 = (f32[136,256]{1,0:T(8,128)S(1)}, f32[136,256]{1,0:T(8,128)S(1)}, u32[]{:S(2)}, u32[]{:S(2)}) collective-permute-start(f32[136,256]{1,0:T(8,128)S(1)} %get-tuple-element.75.refs_0_), channel_id=1, source_target_pairs={{0,32},{32,64},{64,96},{96,0},{1,33},{33,65},{65,97},{97,1},{2,34}... | collective-permute-start | bytes 417800 | tf_op jit(solution)/shard_map/ppermute | solution.py:373
  37.1 11.8 %collective-permute-start.17 = (bf16[144,768]{1,0:T(8,128)(2,1)S(1)}, bf16[144,768]{1,0:T(8,128)(2,1)S(1)}, u32[]{:S(2)}, u32[]{:S(2)}) collective-permute-start(bf16[144,768]{1,0:T(8,128)(2,1)S(1)} %get-tuple-element.83), channel_id=1, source_target_pairs={{0,4},{2,6},{4,0},{6,2},{1,5},{3,7},{5,1},{7,3},{8,12},{10,14},{12... | collective-permute-start | bytes 663560 | tf_op jit(solution)/shard_map/ppermute | solution.py:373
  39.7 9.2 %collective-permute-start.18 = (bf16[144,768]{1,0:T(8,128)(2,1)S(1)}, bf16[144,768]{1,0:T(8,128)(2,1)S(1)}, u32[]{:S(2)}, u32[]{:S(2)}) collective-permute-start(bf16[144,768]{1,0:T(8,128)(2,1)S(1)} %get-tuple-element.84), channel_id=1, source_target_pairs={{0,6},{2,0},{4,2},{6,4},{1,7},{3,1},{5,3},{7,5},{8,14},{10,8},{12,... | collective-permute-start | bytes 663560 | tf_op jit(solution)/shard_map/ppermute | solution.py:373
  43.8 7.8 %collective-permute-start.13 = (f32[128,256]{1,0:T(8,128)S(1)}, f32[128,256]{1,0:T(8,128)S(1)}, u32[]{:S(2)}, u32[]{:S(2)}) collective-permute-start(f32[128,256]{1,0:T(8,128)S(1)} %get-tuple-element.78), channel_id=1, source_target_pairs={{0,8},{8,16},{16,24},{24,0},{1,9},{9,17},{17,25},{25,1},{2,10},{10... | collective-permute-start | bytes 393224 | tf_op jit(solution)/shard_map/ppermute | solution.py:373
  46.1 7.6 %collective-permute-start.14 = (f32[128,256]{1,0:T(8,128)S(1)}, f32[128,256]{1,0:T(8,128)S(1)}, u32[]{:S(2)}, u32[]{:S(2)}) collective-permute-start(f32[128,256]{1,0:T(8,128)S(1)} %get-tuple-element.79), channel_id=1, source_target_pairs={{0,16},{8,24},{16,0},{24,8},{1,17},{9,25},{17,1},{25,9},{2,18},{10... | collective-permute-start | bytes 393224 | tf_op jit(solution)/shard_map/ppermute | solution.py:373
  48.2 5.6 %collective-permute-start.15 = (f32[128,256]{1,0:T(8,128)S(1)}, f32[128,256]{1,0:T(8,128)S(1)}, u32[]{:S(2)}, u32[]{:S(2)}) collective-permute-start(f32[128,256]{1,0:T(8,128)S(1)} %get-tuple-element.80), channel_id=1, source_target_pairs={{0,24},{8,0},{16,8},{24,16},{1,25},{9,1},{17,9},{25,17},{2,26},{10... | collective-permute-start | bytes 393224 | tf_op jit(solution)/shard_map/ppermute | solution.py:373
  55.5 10.4 %collective-permute-start.19 = (bf16[144,768]{1,0:T(8,128)(2,1)S(1)}, bf16[144,768]{1,0:T(8,128)(2,1)S(1)}, u32[]{:S(2)}, u32[]{:S(2)}) collective-permute-start(bf16[144,768]{1,0:T(8,128)(2,1)S(1)} %get-tuple-element.95), channel_id=1, source_target_pairs={{0,2},{2,4},{4,6},{6,0},{1,3},{3,5},{5,7},{7,1},{8,10},{10,12},{12... | collective-permute-start | bytes 663560 | tf_op jit(solution)/shard_map/ppermute | solution.py:373
  56.6 10.7 %collective-permute-start.20 = (bf16[144,768]{1,0:T(8,128)(2,1)S(1)}, bf16[144,768]{1,0:T(8,128)(2,1)S(1)}, u32[]{:S(2)}, u32[]{:S(2)}) collective-permute-start(bf16[144,768]{1,0:T(8,128)(2,1)S(1)} %get-tuple-element.96), channel_id=1, source_target_pairs={{0,4},{2,6},{4,0},{6,2},{1,5},{3,7},{5,1},{7,3},{8,12},{10,14},{12... | collective-permute-start | bytes 663560 | tf_op jit(solution)/shard_map/ppermute | solution.py:373
  59.0 8.9 %collective-permute-start.21 = (bf16[144,768]{1,0:T(8,128)(2,1)S(1)}, bf16[144,768]{1,0:T(8,128)(2,1)S(1)}, u32[]{:S(2)}, u32[]{:S(2)}) collective-permute-start(bf16[144,768]{1,0:T(8,128)(2,1)S(1)} %get-tuple-element.97), channel_id=1, source_target_pairs={{0,6},{2,0},{4,2},{6,4},{1,7},{3,1},{5,3},{7,5},{8,14},{10,8},{12,... | collective-permute-start | bytes 663560 | tf_op jit(solution)/shard_map/ppermute | solution.py:373
  60.8 14.7 %all-to-all-start = ((f32[64,2,128]{2,1,0:T(2,128)}), f32[64,2,128]{2,1,0:T(2,128)S(1)}, u32[]{:S(2)}, u32[]{:S(2)}) async-start(f32[64,2,128]{2,1,0:T(2,128)} %get-tuple-element.101), calls=%async_computation | async-start | bytes 131072 | tf_op jit(solution)/shard_map/all_to_all | solution.py:469
  (2 other events, 4.5 us)
